TPU v7x, 32 devices: a whole 2x2x4 slice. The times are simulated.
32 devices in a mesh: dp: 4 (over z), row: 4 (over y, x), col: 2 (over core).
Axes of the slice: x: 2, y: 2, z: 4, core: 2. Of those that a mesh axis runs over, the one named last changes fastest.
Arguments:
- layer_input: bfloat16 [8192, 1536], P(('dp', 'row'), 'col'), may hold values from -6 to 6
- gain_attn: float32 [1536], P('col'), may hold values from 0.25 to 1.75
- gain_ffn: float32 [1536], P('col'), may hold values from 0.25 to 1.75
- w_query: bfloat16 [1536, 1536], P('col', 'row'), may hold values from -0.15625 to 0.15625
- w_key: bfloat16 [1536, 768], P('col', 'row'), may hold values from -0.15625 to 0.15625
- w_value: bfloat16 [1536, 768], P('col', 'row'), may hold values from -0.15625 to 0.15625
- w_out: bfloat16 [1536, 1536], P('row', 'col'), may hold values from -1.25 to 1.25
- w_gate: bfloat16 [1536, 4096], P('col', 'row'), may hold values from -0.15625 to 0.15625
- w_up: bfloat16 [1536, 4096], P('col', 'row'), may hold values from -0.15625 to 0.15625
- w_down: bfloat16 [4096, 1536], P('row', 'col'), may hold values from -0.09375 to 0.09375
- cotangent: bfloat16 [8192, 1536], P(('dp', 'row'), 'col'), may hold values from -6 to 6
Outputs:
- layer_output: float32 [8192, 1536], P(('dp', 'row'), 'col')
- grad_input: float32 [8192, 1536], P(('dp', 'row'), 'col')
- grad_gain_attn: float32 [1536], P('col')
- grad_gain_ffn: float32 [1536], P('col')
- grad_query: float32 [1536, 1536], P('col', 'row')
- grad_key: float32 [1536, 768], P('col', 'row')
- grad_value: float32 [1536, 768], P('col', 'row')
- grad_out: float32 [1536, 1536], P('row', 'col')
- grad_gate: float32 [1536, 4096], P('col', 'row')
- grad_up: float32 [1536, 4096], P('col', 'row')
- grad_down: float32 [4096, 1536], P('row', 'col')
All inputs are finite; a program needn't handle non-finite values.
Results may differ from a plain program's by a relative error of at most 0.014.
Values may be sent and summed in bfloat16 or wider, within the bound.
A program may use at most 192 MiB of HBM per device.

v0:
```python
import jax
import jax.numpy as jnp
from jax import lax
from jax.sharding import PartitionSpec as P

D = 1536
HD = 96
LENGTH = 1024


EPS = 1e-05
THETA = 100000.0


def rotate(values, heads, inverse):
    count = values.shape[0]
    half = HD // 2
    pos = (jnp.arange(count) % LENGTH).astype(jnp.float32)
    freq = THETA ** (-jnp.arange(half).astype(jnp.float32) * 2.0 / HD)
    angle = pos[:, None] * freq[None, :]
    cosine = jnp.cos(angle)[:, None, :]
    sine = jnp.sin(angle)[:, None, :]
    shaped = values.reshape(count, heads, HD)
    first = shaped[..., :half]
    second = shaped[..., half:]
    if inverse:
        joined = jnp.concatenate(
            [first * cosine + second * sine, second * cosine - first * sine], -1
        )
    else:
        joined = jnp.concatenate(
            [first * cosine - second * sine, second * cosine + first * sine], -1
        )
    return joined.reshape(count, heads * HD)


def masked_scores(query_block, keys_seq, block_index):
    rows = query_block.shape[0]
    span = keys_seq.shape[0]
    scores = jnp.einsum(
        "qkgd,skd->kgqs", query_block, keys_seq, preferred_element_type=jnp.float32
    ) * HD ** (-0.5)
    qpos = block_index * rows + jnp.arange(rows)
    allowed = jnp.arange(span)[None, :] <= qpos[:, None]
    return jnp.where(allowed[None, None], scores, -1e30)


def attend_forward(queries, keys, values, kv_heads):
    total = queries.shape[0]
    group = queries.shape[1] // (kv_heads * HD)
    block = min(512, LENGTH)
    count = LENGTH // block
    outputs = []
    sums = []
    for seq in range(total // LENGTH):
        start = seq * LENGTH
        keys_seq = keys[start : start + LENGTH].reshape(LENGTH, kv_heads, HD)
        vals_seq = values[start : start + LENGTH].reshape(LENGTH, kv_heads, HD)
        query_seq = queries[start : start + LENGTH].reshape(count, block, kv_heads, group, HD)

        def one_block(pair):
            query_block, index = pair
            scores = masked_scores(query_block, keys_seq, index)
            top = jnp.max(scores, -1, keepdims=True)
            expo = jnp.exp(scores - top)
            total_weight = jnp.sum(expo, -1, keepdims=True)
            probs = (expo / total_weight).astype(jnp.bfloat16)
            mixed = jnp.einsum(
                "kgqs,skd->qkgd", probs, vals_seq, preferred_element_type=jnp.float32
            )
            return (mixed.reshape(block, -1), (top + jnp.log(total_weight))[..., 0])

        mixed, logsum = lax.map(one_block, (query_seq, jnp.arange(count)))
        outputs.append(mixed.reshape(LENGTH, -1))
        sums.append(logsum)
    return (jnp.concatenate(outputs, 0), sums)


def attend_backward(queries, keys, values, grad_mixed, sums, kv_heads):
    total = queries.shape[0]
    group = queries.shape[1] // (kv_heads * HD)
    block = min(512, LENGTH)
    count = LENGTH // block
    scale = HD ** (-0.5)
    grad_q = []
    grad_k = []
    grad_v = []
    for seq in range(total // LENGTH):
        start = seq * LENGTH
        keys_seq = keys[start : start + LENGTH].reshape(LENGTH, kv_heads, HD)
        vals_seq = values[start : start + LENGTH].reshape(LENGTH, kv_heads, HD)
        query_seq = queries[start : start + LENGTH].reshape(count, block, kv_heads, group, HD)
        grad_seq = grad_mixed[start : start + LENGTH].reshape(count, block, kv_heads, group, HD)

        def one_block(carry, quad):
            key_acc, val_acc = carry
            query_block, grad_block, logsum, index = quad
            scores = masked_scores(query_block, keys_seq, index)
            probs = jnp.exp(scores - logsum[..., None])
            grad_probs = jnp.einsum(
                "qkgd,skd->kgqs", grad_block, vals_seq, preferred_element_type=jnp.float32
            )
            inner = jnp.sum(probs * grad_probs, -1, keepdims=True)
            grad_scores = (probs * (grad_probs - inner)).astype(jnp.bfloat16)
            dq_block = (
                jnp.einsum(
                    "kgqs,skd->qkgd", grad_scores, keys_seq, preferred_element_type=jnp.float32
                )
                * scale
            )
            key_acc = (
                key_acc
                + jnp.einsum(
                    "kgqs,qkgd->skd", grad_scores, query_block, preferred_element_type=jnp.float32
                )
                * scale
            )
            val_acc = val_acc + jnp.einsum(
                "kgqs,qkgd->skd",
                probs.astype(jnp.bfloat16),
                grad_block,
                preferred_element_type=jnp.float32,
            )
            return ((key_acc, val_acc), dq_block.reshape(block, -1))

        zero = jnp.zeros((LENGTH, kv_heads, HD), jnp.float32)
        (key_acc, val_acc), dq_seq = lax.scan(
            one_block, (zero, zero), (query_seq, grad_seq, sums[seq], jnp.arange(count))
        )
        grad_q.append(dq_seq.reshape(LENGTH, -1))
        grad_k.append(key_acc.reshape(LENGTH, -1))
        grad_v.append(val_acc.reshape(LENGTH, -1))
    return (jnp.concatenate(grad_q, 0), jnp.concatenate(grad_k, 0), jnp.concatenate(grad_v, 0))


def width_total(values):
    return lax.psum(values, "col")


def gather_tokens(values):
    return lax.all_gather(values, "row", axis=0, tiled=True)


def width_sum(values):
    return lax.psum(values, "col")


def token_sum(source, weight):
    return lax.psum_scatter(
        jnp.einsum("tj,jc->tc", source, weight, preferred_element_type=jnp.float32),
        "row",
        scatter_dimension=0,
        tiled=True,
    )


def on_device(
    layer_input,
    gain_attn,
    gain_ffn,
    w_query,
    w_key,
    w_value,
    w_out,
    w_gate,
    w_up,
    w_down,
    cotangent,
):
    input_f32 = layer_input.astype(jnp.float32)
    q_cols = w_query.shape[1]
    k_cols = w_key.shape[1]
    f_cols = w_gate.shape[1]
    w_in = jnp.concatenate([w_query, w_key, w_value], 1)
    w_gateup = jnp.concatenate([w_gate, w_up], 1)
    rstd1 = lax.rsqrt(width_total(jnp.sum(input_f32 * input_f32, 1)) / D + EPS)[:, None]
    normed_a = (input_f32 * rstd1 * gain_attn).astype(jnp.bfloat16)
    all_a = gather_tokens(normed_a)
    projected = width_sum(jnp.dot(all_a, w_in, preferred_element_type=jnp.float32))
    q_sum = projected[:, :q_cols]
    k_sum = projected[:, q_cols : q_cols + k_cols]
    v_sum = projected[:, q_cols + k_cols :]
    heads_q = q_sum.shape[1] // HD
    heads_k = k_sum.shape[1] // HD
    queries = rotate(q_sum, heads_q, False).astype(jnp.bfloat16)
    keys = rotate(k_sum, heads_k, False).astype(jnp.bfloat16)
    values = v_sum.astype(jnp.bfloat16)
    mixed, sums = attend_forward(queries, keys, values, heads_k)
    own_attn = mixed.astype(jnp.bfloat16)
    hidden = input_f32 + token_sum(own_attn, w_out)
    rstd2 = lax.rsqrt(width_total(jnp.sum(hidden * hidden, 1)) / D + EPS)[:, None]
    normed_f = (hidden * rstd2 * gain_ffn).astype(jnp.bfloat16)
    all_f = gather_tokens(normed_f)
    gateup_part = jnp.dot(all_f, w_gateup, preferred_element_type=jnp.float32)
    gateup = width_sum(gateup_part)
    gate = gateup[:, :f_cols]
    upper = gateup[:, f_cols:]
    sig = 1.0 / (1.0 + jnp.exp(-gate))
    own_middle = (gate * sig * upper).astype(jnp.bfloat16)
    layer_output = hidden + token_sum(own_middle, w_down)
    all_dy = gather_tokens(cotangent)
    gw_down = jnp.einsum("tf,tc->fc", own_middle, all_dy, preferred_element_type=jnp.float32)
    mid_part = jnp.einsum("tc,fc->tf", all_dy, w_down, preferred_element_type=jnp.float32)
    d_mid = width_sum(mid_part)
    d_gate = (d_mid * upper * sig * (1.0 + gate * (1.0 - sig))).astype(jnp.bfloat16)
    d_up = (d_mid * gate * sig).astype(jnp.bfloat16)
    d_gateup = jnp.concatenate([d_gate, d_up], 1)
    gw_gateup = jnp.einsum("tc,tf->cf", all_f, d_gateup, preferred_element_type=jnp.float32)
    d_nf = token_sum(d_gateup, w_gateup.T)
    part_gain_ffn = jnp.sum(d_nf * hidden * rstd2, 0)
    scaled2 = d_nf * gain_ffn
    inner2 = width_total(jnp.sum(scaled2 * hidden, 1))[:, None]
    d_hidden = cotangent.astype(jnp.float32) + rstd2 * scaled2 - hidden * rstd2**3 * inner2 / D
    all_dya = gather_tokens(d_hidden.astype(jnp.bfloat16))
    gw_out = jnp.einsum("tq,tc->qc", own_attn, all_dya, preferred_element_type=jnp.float32)
    attn_part = jnp.einsum("tc,qc->tq", all_dya, w_out, preferred_element_type=jnp.float32)
    d_attn = width_sum(attn_part).astype(jnp.bfloat16)
    dq_rot, dk_rot, dv = attend_backward(queries, keys, values, d_attn, sums, heads_k)
    d_q = rotate(dq_rot, heads_q, True).astype(jnp.bfloat16)
    d_k = rotate(dk_rot, heads_k, True).astype(jnp.bfloat16)
    d_v = dv.astype(jnp.bfloat16)
    d_proj = jnp.concatenate([d_q, d_k, d_v], 1)
    gw_in = jnp.einsum("tc,tj->cj", all_a, d_proj, preferred_element_type=jnp.float32)
    sum_down, sum_gateup, sum_in, sum_out = lax.psum((gw_down, gw_gateup, gw_in, gw_out), "dp")
    d_na = token_sum(d_proj, w_in.T)
    part_gain_attn = jnp.sum(d_na * input_f32 * rstd1, 0)
    scaled1 = d_na * gain_attn
    inner1 = width_total(jnp.sum(scaled1 * input_f32, 1))[:, None]
    grad_input = d_hidden + rstd1 * scaled1 - input_f32 * rstd1**3 * inner1 / D
    gain_a, gain_f = lax.psum((part_gain_attn, part_gain_ffn), ("dp", "row"))
    return (
        layer_output,
        grad_input,
        gain_a,
        gain_f,
        sum_in[:, :q_cols],
        sum_in[:, q_cols : q_cols + k_cols],
        sum_in[:, q_cols + k_cols :],
        sum_out,
        sum_gateup[:, :f_cols],
        sum_gateup[:, f_cols:],
        sum_down,
    )


def solution(mesh):
    return jax.shard_map(
        on_device,
        mesh=mesh,
        in_specs=(
            P(("dp", "row"), "col"),
            P("col"),
            P("col"),
            P("col", "row"),
            P("col", "row"),
            P("col", "row"),
            P("row", "col"),
            P("col", "row"),
            P("col", "row"),
            P("row", "col"),
            P(("dp", "row"), "col"),
        ),
        out_specs=(
            P(("dp", "row"), "col"),
            P(("dp", "row"), "col"),
            P("col"),
            P("col"),
            P("col", "row"),
            P("col", "row"),
            P("col", "row"),
            P("row", "col"),
            P("col", "row"),
            P("col", "row"),
            P("row", "col"),
        ),
        check_vma=False,
    )
```

profile of v0, /device:TPU:0, one launch (start us, length us, event | category | flops | bytes accessed | tf_op | source)
XLA Modules:
  0.0 1411.9 jit_solution(6619210359016683264)
XLA Ops:
  14.7 46.1 %all-gather.5.cloned.1.call-done = bf16[2048,768]{1,0:T(8,128)(2,1)} async-done(((bf16[512,768]{1,0:T(8,128)(2,1)}), bf16[2048,768]{1,0:T(8,128)(2,1)}) %all-gather.5.cloned.1.call-update) | async-done | bytes 3145744 | tf_op jit(solution)/shard_map/all_gather | solution.py:141
  60.9 7.2 fusion.111
  69.6 30.8 %all-reduce.8.cloned.1.call-done = f32[2048,768]{1,0:T(8,128)} async-done(((f32[2048,768]{1,0:T(8,128)}), f32[2048,768]{1,0:T(8,128)}) %all-reduce.8.cloned.1.call-update) | async-done | bytes 6291472 | tf_op jit(solution)/shard_map/psum | solution.py:145
  106.4 3.8 slice.114
  126.4 25.8 %while.54 = (s32[]{:T(128)}, bf16[2,512,384]{2,1,0:T(8,128)(2,1)}, f32[2,2,2,512]{3,2,1,0:T(2,128)S(1)}, s32[2]{0:T(128)}, bf16[2,512,2,2,96]{1,4,3,2,0:T(8,128)...) while((s32[]{:T(128)}, bf16[2,512,384]{2,1,0:T(8,128)(2,1)}, ...), condition=%wide.region_6.7_spmd, body=%wide.region_3.6_spmd.sunk | while | flops 830994944 | bytes 30478976 | solution.py:73
  132.8 4.4 fusion.187
  145.7 4.4 fusion.187
  160.8 24.7 %while.55 = (s32[]{:T(128)}, bf16[2,512,384]{2,1,0:T(8,128)(2,1)}, f32[2,2,2,512]{3,2,1,0:T(2,128)}, s32[2]{0:T(128)}, bf16[2,512,2,2,96]{1,4,3,2,0:T(8,128)(2,1...) while((s32[]{:T(128)}, bf16[2,512,384]{2,1,0:T(8,128)(2,1)}, ...), condition=%wide.region_10.11_spmd, body=%wide.region_7.10_spmd.sunk | while | flops 830994944 | bytes 30610104 | solution.py:73
  185.5 6.6 fusion.106
  192.8 70.7 %reduce-scatter.5.cloned.1.call-done = f32[512,768]{1,0:T(8,128)} async-done(((f32[2048,768]{1,0:T(8,128)}), f32[512,768]{1,0:T(8,128)}) %reduce-scatter.5.cloned.1.call-update) | async-done | bytes 1572880 | tf_op jit(solution)/shard_map/reduce_scatter | solution.py:149
  273.1 36.0 %all-gather.9.cloned.1.call-done = bf16[2048,768]{1,0:T(8,128)(2,1)} async-done(((bf16[512,768]{1,0:T(8,128)(2,1)}), bf16[2048,768]{1,0:T(8,128)(2,1)}) %all-gather.9.cloned.1.call-update) | async-done | bytes 3145744 | tf_op jit(solution)/shard_map/all_gather | solution.py:141
  309.1 7.6 fusion.130
  316.7 38.5 %all-gather.7.cloned.1.call-done = bf16[2048,768]{1,0:T(8,128)(2,1)} async-done(((bf16[512,768]{1,0:T(8,128)(2,1)}), bf16[2048,768]{1,0:T(8,128)(2,1)}) %all-gather.7.cloned.1.call-update) | async-done | bytes 3145744 | tf_op jit(solution)/shard_map/all_gather | solution.py:141
  355.2 12.5 fusion.128
  367.8 82.7 %all-reduce.12.cloned.1.call-done = (f32[2048,2048]{1,0:T(8,128)}, f32[2048,1024]{1,0:T(8,128)}) async-done(((f32[2048,2048]{1,0:T(8,128)}, f32[2048,1024]{1,0:T(8,128)}), (f32[2048,2048]{1,0:T(8,128)}, f32[2048,1024]{1,0:T(8,128)})) %all-reduce.12.cloned.1.call-update) | async-done | bytes 25165840 | tf_op jit(solution)/shard_map/psum | solution.py:145
  450.5 12.9 multiply_convert_fusion.1
  466.6 10.5 fusion.95
  477.1 8.5 fusion.129
  485.7 62.8 %reduce-scatter.9.cloned.1.call-done = f32[512,768]{1,0:T(8,128)} async-done(((f32[2048,768]{1,0:T(8,128)}), f32[512,768]{1,0:T(8,128)}) %reduce-scatter.9.cloned.1.call-update) | async-done | bytes 1572880 | tf_op jit(solution)/shard_map/reduce_scatter | solution.py:149
  553.5 68.1 %reduce-scatter.7.cloned.1.call-done = f32[512,768]{1,0:T(8,128)} async-done(((f32[2048,768]{1,0:T(8,128)}), f32[512,768]{1,0:T(8,128)}) %reduce-scatter.7.cloned.1.call-update) | async-done | bytes 1572880 | tf_op jit(solution)/shard_map/reduce_scatter | solution.py:149
  621.6 4.1 fusion.123
  625.8 43.9 %all-gather.11.cloned.1.call-done = bf16[2048,768]{1,0:T(8,128)(2,1)} async-done(((bf16[512,768]{1,0:T(8,128)(2,1)}), bf16[2048,768]{1,0:T(8,128)(2,1)}) %all-gather.11.cloned.1.call-update) | async-done | bytes 3145744 | tf_op jit(solution)/shard_map/all_gather | solution.py:141
  669.8 5.5 fusion.131
  675.3 12.2 all-reduce.13
  688.8 4.8 reshape.360
  697.6 74.2 %while.56 = (s32[]{:T(128)}, f32[1024,2,96]{0,2,1:T(8,128)}, f32[1024,2,96]{0,2,1:T(8,128)}, f32[2,512,384]{1,0,2:T(2,128)}, bf16[2,512,2,2,96]{1,4,3,2,0:T(8,12...) while((s32[]{:T(128)}, f32[1024,2,96]{0,2,1:T(8,128)}, ...), condition=%wide.region_23.24_spmd.clone, body=%wide.region_21.23_spmd.clone.sunk | while | flops 2046425600 | bytes 131526960 | solution.py:127
  700.6 4.5 fusion.200
  709.8 14.9 %dynamic_update_slice.36 = f32[2,512,384]{1,0,2:T(2,128)} dynamic-update-slice(f32[2,512,384]{1,0,2:T(2,128)} %get-tuple-element.816, f32[1,512,384]{1,0,2:T(1,128)S(1)} %copy.94, s32[]{:T(128)} %get-tuple-element.813, s32[]{:T(128)} %constant.122.clone.1..sunk, s32[]{:T(128)} %constant.122.clone.1..sunk) | dynamic-update-slice | bytes 1572868 | tf_op jit(solution)/shard_map/while/body/jit(dynamic_update_index_in_dim)/dynamic_update_slice | solution.py:73
  724.8 4.0 fusion.202
  728.8 5.7 fusion.203
  737.5 4.5 fusion.200
  746.7 14.9 %dynamic_update_slice.36 = f32[2,512,384]{1,0,2:T(2,128)} dynamic-update-slice(f32[2,512,384]{1,0,2:T(2,128)} %get-tuple-element.816, f32[1,512,384]{1,0,2:T(1,128)S(1)} %copy.94, s32[]{:T(128)} %get-tuple-element.813, s32[]{:T(128)} %constant.122.clone.1..sunk, s32[]{:T(128)} %constant.122.clone.1..sunk) | dynamic-update-slice | bytes 1572868 | tf_op jit(solution)/shard_map/while/body/jit(dynamic_update_index_in_dim)/dynamic_update_slice | solution.py:73
  761.6 4.2 fusion.202
  765.8 5.9 fusion.203
  775.7 4.7 reshape.361
  785.5 70.2 %while.57 = (s32[]{:T(128)}, f32[1024,2,96]{0,2,1:T(8,128)S(1)}, f32[1024,2,96]{0,2,1:T(8,128)}, f32[2,512,384]{1,0,2:T(2,128)}, bf16[2,512,2,2,96]{1,4,3,2,0:T(...) while((s32[]{:T(128)}, f32[1024,2,96]{0,2,1:T(8,128)S(1)}, ...), condition=%wide.region_26.27_spmd.clone, body=%wide.region_24.26_spmd.clone.sunk | while | flops 2046425600 | bytes 133099856 | solution.py:127
  796.6 14.9 %dynamic_update_slice.37 = f32[2,512,384]{1,0,2:T(2,128)} dynamic-update-slice(f32[2,512,384]{1,0,2:T(2,128)} %get-tuple-element.777, f32[1,512,384]{1,0,2:T(1,128)S(1)} %copy.95, s32[]{:T(128)} %get-tuple-element.774, s32[]{:T(128)} %constant.122.clone.1..sunk.1, s32[]{:T(128)} %constant.122.clone.1..sunk.1) | dynamic-update-slice | bytes 1572868 | tf_op jit(solution)/shard_map/while/body/jit(dynamic_update_index_in_dim)/dynamic_update_slice | solution.py:73
  814.7 5.8 fusion.216
  831.6 14.9 %dynamic_update_slice.37 = f32[2,512,384]{1,0,2:T(2,128)} dynamic-update-slice(f32[2,512,384]{1,0,2:T(2,128)} %get-tuple-element.777, f32[1,512,384]{1,0,2:T(1,128)S(1)} %copy.95, s32[]{:T(128)} %get-tuple-element.774, s32[]{:T(128)} %constant.122.clone.1..sunk.1, s32[]{:T(128)} %constant.122.clone.1..sunk.1) | dynamic-update-slice | bytes 1572868 | tf_op jit(solution)/shard_map/while/body/jit(dynamic_update_index_in_dim)/dynamic_update_slice | solution.py:73
  849.7 6.0 fusion.216
  868.3 5.5 fusion.109
  873.9 8.5 fusion.132
  882.4 9.1 fusion.94
  894.5 4.1 fusion.108
  898.7 45.4 %reduce-scatter.11.cloned.1.call-done = f32[512,768]{1,0:T(8,128)} async-done(((f32[2048,768]{1,0:T(8,128)}), f32[512,768]{1,0:T(8,128)}) %reduce-scatter.11.cloned.1.call-update) | async-done | bytes 1572880 | tf_op jit(solution)/shard_map/reduce_scatter | solution.py:149
  948.6 44.6 %all-reduce = (f32[768]{0:T(1024)}, f32[768]{0:T(1024)}) all-reduce(f32[768]{0:T(1024)S(1)} %get-tuple-element.363, f32[768]{0:T(1024)S(1)} %copy-done.59), channel_id=1, replica_groups=mesh['dp'=4,'row'=4,'col'=2] {'dp','row'}, use_global_device_ids=true, to_apply=%region_31.32 | all-reduce | flops 1536 | bytes 12288 | tf_op jit(solution)/shard_map/psum | solution.py:230
  996.3 391.9 %all-reduce.10.cloned.1.call-done = (f32[768,768]{1,0:T(8,128)}, f32[384,768]{1,0:T(8,128)}, f32[768,2048]{1,0:T(8,128)}, f32[1024,768]{1,0:T(8,128)}) async-done(((f32[768,768]{1,0:T(8,128)}, f32[384,768]{1,0:T(8,128)}, f32[768,2048]{1,0:T(8,128)}, f32[1024,768]{1,0:T(8,128)}), (f32[768,768]{1,0:T(8,128)}, f32[384,768]{1,0:T(8,128)}, f32[768,2048]{1,0:T(8,128)}, ...) | async-done | bytes 12976144 | tf_op jit(solution)/shard_map/psum | solution.py:224
  1391.4 6.7 fusion.124
  (317 shorter events, 185.5 us)
Async XLA Ops:
  7.2 301.9 %copy-start = (bf16[1024,768]{1,0:T(8,128)(2,1)S(1)}, bf16[1024,768]{1,0:T(8,128)(2,1)}, u32[]{:S(2)}) copy-start(bf16[1024,768]{1,0:T(8,128)(2,1)} %param.28) | copy-start | bytes 4718596
  7.2 7.2 copy-start.48
  7.2 7.3 copy-start.49
  7.2 53.6 %copy-start.64 = (bf16[768,384]{1,0:T(8,128)(2,1)S(1)}, bf16[768,384]{1,0:T(8,128)(2,1)}, u32[]{:S(2)}) copy-start(bf16[768,384]{1,0:T(8,128)(2,1)} %param.22) | copy-start | bytes 1769476
  7.2 53.6 %all-gather.5.cloned.1.call-start = ((), (), s32[]{:S(2)}) async-start(), calls=%async_computation.4 | async-start | bytes 3932160 | tf_op jit(solution)/shard_map/all_gather | solution.py:141
  14.3 86.1 %all-reduce.8.cloned.1.call-start = ((), (), s32[]{:S(2)}) async-start(), calls=%async_computation.5 | async-start | bytes 12582912 | tf_op jit(solution)/shard_map/psum | solution.py:145
  14.5 53.5 %copy-start.42 = (bf16[768,192]{1,0:T(8,128)(2,1)}, bf16[768,192]{1,0:T(8,128)(2,1)S(1)}, u32[]{:S(2)}) copy-start(bf16[768,192]{1,0:T(8,128)(2,1)S(1)} %copy.38) | copy-start | bytes 884740
  14.7 53.4 %copy-start.44 = (bf16[768,192]{1,0:T(8,128)(2,1)}, bf16[768,192]{1,0:T(8,128)(2,1)S(1)}, u32[]{:S(2)}) copy-start(bf16[768,192]{1,0:T(8,128)(2,1)S(1)} %copy.39) | copy-start | bytes 884740
  68.1 195.4 %reduce-scatter.5.cloned.1.call-start = ((), (), s32[]{:S(2)}) async-start(), calls=%async_computation.6 | async-start | bytes 7864320 | tf_op jit(solution)/shard_map/reduce_scatter | solution.py:149
  69.6 46.7 %copy-start.20 = (f32[2048,48]{0,1:T(8,128)}, f32[2048,48]{0,1:T(8,128)S(1)}, u32[]{:S(2)}) copy-start(f32[2048,48]{0,1:T(8,128)S(1)} %get-tuple-element.477) | copy-start | bytes 1179652
  69.6 46.7 %copy-start.22 = (f32[2048,48]{0,1:T(8,128)}, f32[2048,48]{0,1:T(8,128)S(1)}, u32[]{:S(2)}) copy-start(f32[2048,48]{0,1:T(8,128)S(1)} %get-tuple-element.478) | copy-start | bytes 1179652
  152.1 8.7 copy-start.8
  152.1 8.7 copy-start.50
  185.5 6.6 copy-start.6
  185.5 6.6 copy-start.10
  185.5 6.6 copy-start.16
  192.1 75.7 %copy-start.55 = (f32[768]{0:T(1024)S(1)}, f32[768]{0:T(1024)}, u32[]{:S(2)}) copy-start(f32[768]{0:T(1024)} %param.21) | copy-start | bytes 9220
  192.1 116.9 %all-gather.9.cloned.1.call-start = ((), (), s32[]{:S(2)}) async-start(), calls=%async_computation.9 | async-start | bytes 3932160 | tf_op jit(solution)/shard_map/all_gather | solution.py:141
  192.7 162.5 %all-gather.7.cloned.1.call-start = ((), (), s32[]{:S(2)}) async-start(), calls=%async_computation.7 | async-start | bytes 3932160 | tf_op jit(solution)/shard_map/all_gather | solution.py:141
  269.0 181.5 %all-reduce.12.cloned.1.call-start = ((), (), s32[]{:S(2)}) async-start(), calls=%async_computation.14 | async-start | bytes 50331648 | tf_op jit(solution)/shard_map/psum | solution.py:145
  367.7 180.8 %reduce-scatter.9.cloned.1.call-start = ((), (), s32[]{:S(2)}) async-start(), calls=%async_computation.10 | async-start | bytes 7864320 | tf_op jit(solution)/shard_map/reduce_scatter | solution.py:149
  477.1 144.5 %reduce-scatter.7.cloned.1.call-start = ((), (), s32[]{:S(2)}) async-start(), calls=%async_computation.8 | async-start | bytes 7864320 | tf_op jit(solution)/shard_map/reduce_scatter | solution.py:149
  485.6 184.1 %all-gather.11.cloned.1.call-start = ((), (), s32[]{:S(2)}) async-start(), calls=%async_computation.11 | async-start | bytes 3932160 | tf_op jit(solution)/shard_map/all_gather | solution.py:141
  548.5 73.1 %copy-start.29 = (f32[512,768]{1,0:T(8,128)S(1)}, f32[512,768]{1,0:T(8,128)}, u32[]{:S(2)}) copy-start(f32[512,768]{1,0:T(8,128)} %reduce-scatter.9.cloned.1.call-done) | copy-start | bytes 4718596
  625.8 318.3 %reduce-scatter.11.cloned.1.call-start = ((), (), s32[]{:S(2)}) async-start(), calls=%async_computation.12 | async-start | bytes 7864320 | tf_op jit(solution)/shard_map/reduce_scatter | solution.py:149
  688.8 8.8 copy-start.9
  688.8 8.8 copy-start.13
  688.8 8.8 copy-start.51
  698.9 6.2 copy-start.2
  775.7 9.8 copy-start.7
  775.7 9.8 copy-start.11
  775.7 9.8 copy-start.17
  775.7 9.8 copy-start.54
  855.8 6.4 copy-start.21
  855.8 6.4 copy-start.23
  873.8 514.3 %all-reduce.10.cloned.1.call-start = ((), (), s32[]{:S(2)}) async-start(), calls=%async_computation.13 | async-start | bytes 25952256 | tf_op jit(solution)/shard_map/psum | solution.py:224
  873.9 8.5 copy-start.31
  873.9 8.5 copy-start.33
  873.9 8.5 copy-start.62
  882.4 9.1 copy-start.35
  882.4 9.1 copy-start.36
  882.4 9.1 copy-start.63
  898.6 45.4 %copy-start.15 = (bf16[512,768]{1,0:T(8,128)(2,1)S(1)}, bf16[512,768]{1,0:T(8,128)(2,1)}, u32[]{:S(2)}) copy-start(bf16[512,768]{1,0:T(8,128)(2,1)} %param.19) | copy-start | bytes 2359300
  898.6 45.4 %copy-start.56 = (f32[768]{0:T(1024)S(1)}, f32[768]{0:T(1024)}, u32[]{:S(2)}) copy-start(f32[768]{0:T(1024)} %param.20) | copy-start | bytes 9220
  898.6 45.4 %copy-start.58 = (f32[512]{0:T(512)S(1)}, f32[512]{0:T(512)}, u32[]{:S(2)}) copy-start(f32[512]{0:T(512)} %copy-done.57) | copy-start | bytes 6148
  898.6 50.0 %copy-start.59 = (f32[768]{0:T(1024)S(1)}, f32[768]{0:T(1024)}, u32[]{:S(2)}) copy-start(f32[768]{0:T(1024)} %get-tuple-element.361) | copy-start | bytes 9220
  898.6 94.6 %copy-start.60 = (f32[512]{0:T(512)S(1)}, f32[512]{0:T(512)}, u32[]{:S(2)}) copy-start(f32[512]{0:T(512)} %get-tuple-element.479) | copy-start | bytes 6148
  944.1 49.2 %copy-start.28 = (f32[512,768]{1,0:T(8,128)S(1)}, f32[512,768]{1,0:T(8,128)}, u32[]{:S(2)}) copy-start(f32[512,768]{1,0:T(8,128)} %reduce-scatter.11.cloned.1.call-done) | copy-start | bytes 4718596
  (40 other events, 124.5 us)
Sparse Core Ops, SparseCore 0:
  14.4 46.4 all-gather.4
  68.2 32.1 all-reduce.7
  192.2 71.2 reduce-scatter.4
  265.2 43.8 all-gather.8
  311.3 43.8 all-gather.6
  367.8 82.5 all-reduce.11
  477.2 71.2 reduce-scatter.8
  551.5 70.0 reduce-scatter.6
  625.9 43.8 all-gather.10
  874.0 70.0 reduce-scatter.10
  948.1 440.0 all-reduce.9
where the time goes:
time: 1420 us; the launch traced here: 1410 us
  waiting for transfers between devices  918 us (65%)
  matrix products  176 us (12%)
  local copies, waits for them, and re-layouts  161 us (11%)
  other arithmetic  69.4 us (5%)
  blocking collectives  66.8 us (5%)
  between operations  14.9 us (1%)
    psum x1, waiting for transfers between devices, on_device(): lax.psum((gw_down, gw_gateup, gw_in, gw_out), 'dp')  392 us
    reduce_scatter x4, waiting for transfers between devices, token_sum(): lax.psum_scatter(jnp.einsum('tj,jc->tc', source, weight, preferred_elemen...  247 us
    all_gather x4, waiting for transfers between devices, gather_tokens(): return lax.all_gather(values, 'row', axis=0, tiled=True)  165 us
    psum x2, waiting for transfers between devices, width_sum(): return lax.psum(values, 'col')  114 us
    dynamic_update_slice x16, local copies, waits for them, and re-layouts, attend_forward(): mixed, logsum = lax.map(one_block, (query_seq, jnp.arange(count)))  70.9 us
    psum x1, blocking collectives, on_device(): gain_a, gain_f = lax.psum((part_gain_attn, part_gain_ffn), ('dp', 'row'))  44.6 us
    dot_general x4, matrix products, token_sum(): jnp.einsum('tj,jc->tc', source, weight, preferred_element_type=jnp.float32)  31.1 us
  transfers between devices with their start and end apart: 11, of which 11 were waited for; matrix products, arithmetic and copies ran while one was open for 4% of the time, Pallas kernels for 0%

commit v1 on v0

v1 whole, which is shorter than its diff:
```python
import jax
import jax.numpy as jnp
import numpy as np
from jax import lax
from jax.experimental import pallas as pl
from jax.experimental.pallas import tpu as pltpu
from jax.sharding import PartitionSpec as P

HD = 96
HALF = HD // 2
LENGTH = 1024
EPS = 1e-05
THETA = 100000.0
SCALE = HD ** (-0.5)
LANE = 128
PIECE = 256

BF = jnp.bfloat16
F32 = jnp.float32
MESH = pl.DeviceIdType.MESH
VM = pl.BlockSpec(memory_space=pltpu.VMEM)
ANY = pl.BlockSpec(memory_space=pl.ANY)
DMA = pltpu.SemaphoreType.DMA


def nn(a, b):
    return lax.dot_general(a, b, (((1,), (0,)), ((), ())), preferred_element_type=F32)


def nt(a, b):
    return lax.dot_general(a, b, (((1,), (1,)), ((), ())), preferred_element_type=F32)


def place():
    r = lax.axis_index("row")
    k = lax.axis_index("col")
    return r, k, r + 1 - 2 * (r % 2), (r + 2) % 4, 3 - r


def greet(rx, ry, k):
    bar = pltpu.get_barrier_semaphore()
    for device in ({"row": rx}, {"row": ry}, {"col": 1 - k}):
        pl.semaphore_signal(bar, inc=1, device_id=device, device_id_type=MESH)
    pl.semaphore_wait(bar, 3)


def remote(src, dst, send, recv, device):
    return pltpu.make_async_remote_copy(
        src_ref=src, dst_ref=dst, send_sem=send, recv_sem=recv, device_id=device, device_id_type=MESH
    )


def rows_of(half):
    return pl.ds(pl.multiple_of(half * PIECE, PIECE), PIECE)


GATHER_SEMS = [DMA((6,)), DMA((6,)), DMA((8,)), DMA((8,)), DMA]


class Gather:
    def __init__(self, own, buf, sems):
        self.own, self.buf = own, buf
        self.isend, self.irecv, self.dsend, self.drecv, self.lsem = sems
        self.r, self.k, self.rx, self.ry, self.r3 = place()

    def piece(self, i):
        side = jnp.where(i % 2 == 0, self.rx, self.ry)
        row = jnp.where(i < 2, self.r, jnp.where(i < 6, side, self.r3))
        half = jnp.where(i // 2 == 2, 1 - i % 2, i % 2)
        return row, half

    def ici(self, sem, row, half, device, src=None):
        dst = self.buf.at[self.k, row, rows_of(half)]
        return remote(dst if src is None else src, dst, self.isend.at[sem], self.irecv.at[sem], {"row": device})

    def pair(self, i, core, row, half, src=None):
        dst = self.buf.at[core, row, rows_of(half)]
        return remote(dst if src is None else src, dst, self.dsend.at[i], self.drecv.at[i], {"col": 1 - self.k})

    def start(self):
        first, second = self.own.at[pl.ds(0, PIECE)], self.own.at[pl.ds(PIECE, PIECE)]
        self.ici(0, self.r, 0, self.rx, first).start()
        self.ici(1, self.r, 1, self.ry, second).start()
        self.ici(2, self.r, 1, self.rx, second).start()
        self.ici(3, self.r, 0, self.ry, first).start()
        self.pair(0, self.k, self.r, 0, first).start()
        self.pair(1, self.k, self.r, 1, second).start()
        self.local = pltpu.make_async_copy(self.own, self.buf.at[self.k, self.r], self.lsem)
        self.local.start()

    def arrive(self, i):
        row, half = self.piece(i)
        self.ici(i - 2, row, half, self.rx).wait_recv()

        @pl.when(i == 2)
        def _():
            self.ici(4, row, half, self.ry).start()

        @pl.when(i == 3)
        def _():
            self.ici(5, row, half, self.rx).start()

        self.pair(i, self.k, row, half).start()

    def ready(self, i):
        row, half = self.piece(i)
        self.pair(i, 1 - self.k, row, half).wait_recv()

    def run(self, compute):
        self.local.wait()

        def step(i, carry):
            self.ready(i)
            row, half = self.piece(i)
            compute(i, row, half)

            @pl.when(i < 6)
            def _():
                self.arrive(i + 2)

            return carry

        lax.fori_loop(0, 8, step, 0)
        self.finish()

    def finish(self):
        for i in range(6):
            self.ici(i, self.r, 0, self.rx).wait_send()
        for i in range(8):
            self.pair(i, self.k, self.r, 0).wait_send()


def sum_scratch(width):
    return [
        pltpu.VMEM((4, PIECE, width), F32),
        pltpu.VMEM((8, PIECE, width), BF),
        pltpu.VMEM((8, PIECE, width), BF),
        pltpu.VMEM((6, PIECE, width), BF),
        pltpu.VMEM((6, PIECE, width), BF),
        DMA((8,)),
        DMA((8,)),
        DMA((6,)),
        DMA((6,)),
    ]


class Sum:
    def __init__(self, scratch):
        self.own, self.ds, self.dr, self.ist, self.irt = scratch[:5]
        self.dsend, self.drecv, self.isend, self.irecv = scratch[5:]
        self.r, self.k, self.rx, self.ry, self.r3 = place()

    def piece(self, j):
        mid = jnp.where(j == 2, self.ry, jnp.where(j == 5, self.ry, self.rx))
        row = jnp.where(j < 2, self.r3, jnp.where(j < 6, mid, self.r))
        return row, j % 2

    def pair(self, j):
        return remote(self.ds.at[j], self.dr.at[j], self.dsend.at[j], self.drecv.at[j], {"col": 1 - self.k})

    def ici(self, j):
        device = jnp.where(j == 0, self.ry, jnp.where(j == 2, self.ry, jnp.where(j == 5, self.ry, self.rx)))
        return remote(self.ist.at[j], self.irt.at[j], self.isend.at[j], self.irecv.at[j], {"row": device})

    def put(self, j, kept, given):
        self.own[j % 4] = kept
        self.ds[j] = given.astype(BF)
        self.pair(j).start()

    def chip(self, j):
        self.pair(j).wait_recv()
        return self.own[j % 4] + self.dr[j].astype(F32)

    def forward(self, j):
        self.ist[j] = self.chip(j).astype(BF)
        self.ici(j).start()

    def relay(self, j):
        value = self.chip(j)
        self.ici(j - 4).wait_recv()
        self.ist[j] = (value + self.irt[j - 4].astype(F32)).astype(BF)
        self.ici(j).start()

    def last(self, j):
        value = self.chip(j)
        self.ici(j - 4).wait_recv()
        value = value + self.irt[j - 4].astype(F32)
        self.ici(j - 2).wait_recv()
        return value + self.irt[j - 2].astype(F32)

    def send_all(self, compute):
        def step(j, carry):
            row, half = self.piece(j)
            kept, given = compute(row, half)
            self.put(j, kept, given)

            @pl.when(j > 0)
            def _():
                @pl.when(j < 5)
                def _():
                    self.forward(j - 1)

            return carry

        lax.fori_loop(0, 8, step, 0)

    def finish(self):
        for j in range(8):
            self.pair(j).wait_send()
        for j in range(6):
            self.ici(j).wait_send()


def call(kernel, cid, outs, ins, args, scratch, flops, vmem=44):
    moved = sum(int(np.prod(a.shape)) * a.dtype.itemsize for a in list(args) + list(outs))
    return pl.pallas_call(
        kernel,
        out_shape=outs,
        in_specs=ins,
        out_specs=[VM] * len(outs),
        scratch_shapes=scratch,
        compiler_params=pltpu.CompilerParams(
            collective_id=cid, has_side_effects=True, vmem_limit_bytes=vmem << 20
        ),
        cost_estimate=pl.CostEstimate(flops=int(flops), bytes_accessed=moved, transcendentals=0),
    )(*args)


def sds(shape, dtype):
    return jax.ShapeDtypeStruct(shape, dtype)


def head_index(iota):
    head, lane = iota // LANE, iota % LANE
    index = jnp.where(lane < HALF, lane, lane - (LANE // 2 - HALF))
    pad = lane % (LANE // 2) >= HALF
    return jnp.where(pad, -1, head * HD + index)


def spread(rows, cols, first):
    source = head_index(lax.broadcasted_iota(jnp.int32, (rows, cols), 1))
    at = lax.broadcasted_iota(jnp.int32, (rows, cols), 0)
    return jnp.where((source >= 0) & (at == source + first), 1.0, 0.0).astype(BF)


def spread_t(rows, cols, first):
    source = head_index(lax.broadcasted_iota(jnp.int32, (rows, cols), 0))
    at = lax.broadcasted_iota(jnp.int32, (rows, cols), 1)
    return jnp.where((source >= 0) & (at == source + first), 1.0, 0.0).astype(BF)


def angle_tables():
    lane = np.arange(LANE)
    freq = np.where(
        lane % (LANE // 2) < HALF, THETA ** (-2.0 * (lane % (LANE // 2)) / HD), 0.0
    )
    fine = np.arange(32)[:, None] * freq[None]
    coarse = fine * 32.0
    return [f(t).astype(np.float32) for t in (coarse, fine) for f in (np.cos, np.sin)]


def project_kernel(
    x, gain, wq, wk, wv, wo, wg, wu, wd, cc, sc, cf, sf,
    normed, qkv, kvt, wqkv_o, wo_o, wg_o, wu_o, wd_o, cos_o, sin_o, rstd_o,
    raw, gains, give_in, give_out, wsem, wrecv, csem, *sems,
):
    r, k, rx, ry, r3 = place()
    width = x.shape[1]
    f_half = wg.shape[1] // 2
    greet(rx, ry, k)
    gather = Gather(x, raw, sems)
    gather.start()
    mate = {"col": 1 - k}
    mine = pl.ds(pl.multiple_of(k * f_half, f_half), f_half)
    his = pl.ds(pl.multiple_of((1 - k) * f_half, f_half), f_half)
    keep = [
        pltpu.make_async_copy(gain, gains.at[k], csem.at[0]),
        pltpu.make_async_copy(wg.at[:, mine], wg_o.at[k], csem.at[1]),
        pltpu.make_async_copy(wu.at[:, mine], wu_o.at[k], csem.at[2]),
        pltpu.make_async_copy(wd.at[mine], wd_o.at[k], csem.at[3]),
    ]
    for c in keep:
        c.start()

    def give(n, src, dst):
        return remote(src, dst.at[k], wsem.at[n], wrecv.at[n], mate)

    gives = [give(0, gain, gains)]
    gives[0].start()
    heads_q = wq.shape[1] // 2
    heads_k = wk.shape[1] // 2
    nq = heads_q // HD * LANE
    nk = heads_k // HD * LANE
    for core, dst_in, dst_out in ((1 - k, give_in, give_out), (k, wqkv_o.at[k], wo_o.at[k])):
        sq = spread(2 * heads_q, nq, core * heads_q)
        sk = spread(2 * heads_k, nk, core * heads_k)
        dst_in[:, 0:nq] = nn(wq[...], sq).astype(BF)
        dst_in[:, nq : nq + nk] = nn(wk[...], sk).astype(BF)
        dst_in[:, nq + nk : nq + 2 * nk] = nn(wv[...], sk).astype(BF)
        dst_out[...] = nn(spread_t(nq, 2 * heads_q, core * heads_q), wo[...]).astype(BF)
    gives += [give(1, give_in, wqkv_o), give(2, give_out, wo_o)]
    gives += [give(3, wg.at[:, his], wg_o), give(4, wu.at[:, his], wu_o), give(5, wd.at[his], wd_o)]
    for g in gives[1:]:
        g.start()
    sign = jnp.where(lax.broadcasted_iota(jnp.int32, (32, LANE), 1) < LANE // 2, -1.0, 1.0)
    for a in range(LENGTH // 32):
        ca, sa = cc[a : a + 1, :], sc[a : a + 1, :]
        cos_o[a * 32 : a * 32 + 32, :] = ca * cf[...] - sa * sf[...]
        sin_o[a * 32 : a * 32 + 32, :] = (sa * cf[...] + ca * sf[...]) * sign
    for c in keep:
        c.wait()
    for n in range(3):
        gives[n].wait_recv()

    def compute(i, row, half):
        at = rows_of(half)
        x0 = raw[0, row, at, :].astype(F32)
        x1 = raw[1, row, at, :].astype(F32)
        total = jnp.sum(x0 * x0, 1, keepdims=True) + jnp.sum(x1 * x1, 1, keepdims=True)
        rstd = lax.rsqrt(total / (2 * width) + EPS)
        n0 = (x0 * rstd * gains[0]).astype(BF)
        n1 = (x1 * rstd * gains[1]).astype(BF)
        normed[0, row, at, :] = n0
        normed[1, row, at, :] = n1

        @pl.when(i < 2)
        def _():
            rstd_o[at, :] = jnp.broadcast_to(rstd, (PIECE, LANE))

        got = nn(n0, wqkv_o[0]) + nn(n1, wqkv_o[1])
        pos = pl.ds(pl.multiple_of((row % 2) * 2 * PIECE + half * PIECE, PIECE), PIECE)
        out = pl.ds(pl.multiple_of(row * 2 * PIECE + half * PIECE, PIECE), PIECE)
        cos, sin = cos_o[pos, :], sin_o[pos, :]
        for part in range(4):
            u = got[:, part * LANE : (part + 1) * LANE]
            if part < 3:
                u = u * cos + pltpu.roll(u, LANE // 2, 1) * sin
            qkv[part, out, :] = u.astype(BF)
            if part >= 2:
                kvt[part - 2, :, out] = u.T.astype(BF)

    gather.run(compute)
    for g in gives[3:]:
        g.wait_recv()
    for g in gives:
        g.wait_send()


def project(x, gain, wq, wk, wv, wo, wg, wu, wd):
    tokens, width = x.shape
    f_half = wg.shape[1] // 2
    cols = 4 * LANE
    tables = [jnp.asarray(t) for t in angle_tables()]
    outs = [
        sds((2, 4, tokens, width), BF),
        sds((4, 4 * tokens, LANE), BF),
        sds((2, LANE, 4 * tokens), BF),
        sds((2, width, cols), BF),
        sds((2, 2 * LANE, width), BF),
        sds((2, width, f_half), BF),
        sds((2, width, f_half), BF),
        sds((2, f_half, width), BF),
        sds((LENGTH, LANE), F32),
        sds((LENGTH, LANE), F32),
        sds((tokens, LANE), F32),
    ]
    scratch = [
        pltpu.VMEM((2, 4, tokens, width), BF),
        pltpu.VMEM((2, 1, width), F32),
        pltpu.VMEM((width, cols), BF),
        pltpu.VMEM((2 * LANE, width), BF),
        DMA((6,)),
        DMA((6,)),
        DMA((4,)),
    ] + GATHER_SEMS
    ins = [ANY, VM, VM, VM, VM, VM, ANY, ANY, ANY] + [VM] * 4
    args = [x, gain, wq, wk, wv, wo, wg, wu, wd] + tables
    return call(project_kernel, 0, outs, ins, args, scratch, 3e10)


def exchange(k, stat, sems):
    copy = remote(stat.at[k], stat.at[k], sems.at[0], sems.at[1], {"col": 1 - k})
    copy.start()
    remote(stat.at[1 - k], stat.at[1 - k], sems.at[0], sems.at[1], {"col": 1 - k}).wait_recv()
    copy.wait_send()
    return stat[0][:, 0:1] + stat[1][:, 0:1]


def causal(shape):
    return lax.broadcasted_iota(jnp.int32, shape, 0) <= lax.broadcasted_iota(jnp.int32, shape, 1)


def attend_kernel(
    qkv, kvt, wo, x, gain, dy,
    attn, lse, hidden, normed, rstd_o, all_dy,
    stat, ssem, *rest,
):
    r, k, rx, ry, r3 = place()
    width = x.shape[1]
    greet(rx, ry, k)
    total = Sum(rest[:9])
    gather = Gather(dy, all_dy, rest[9:])
    gather.start()

    def compute(row, half):
        base = pl.multiple_of(row // 2 * LENGTH, LENGTH)
        at = rows_of(half)
        qrow = pl.ds(pl.multiple_of(row * 2 * PIECE + half * PIECE, PIECE), PIECE)
        order = (row % 2) * 2 + half

        def attend(p):
            span = PIECE * (p + 1)
            for head in range(2):
                keys = qkv[2, pl.ds(base, span), :]
                s = nt(keys, qkv[head, qrow, :])
                tail = jnp.where(causal((PIECE, PIECE)), s[span - PIECE :], -1e30)
                s = tail if p == 0 else jnp.concatenate([s[: span - PIECE], tail], 0)
                top = jnp.max(s, 0, keepdims=True)
                e = jnp.exp((s - top) * SCALE)
                weight = jnp.sum(e, 0, keepdims=True)
                probs = (e * (1.0 / weight)).astype(BF)
                mixed = nn(kvt[1, :, pl.ds(base, span)], probs)
                attn[row, at, head * LANE : (head + 1) * LANE] = mixed.T.astype(BF)
                lse[head, row * 2 + half] = top * SCALE + jnp.log(weight)

        for p in range(4):
            pl.when(order == p)(lambda p=p: attend(p))
        a = attn[row, at, :]
        return nn(a, wo[k]), nn(a, wo[1 - k])

    total.send_all(compute)
    total.relay(4)
    total.relay(5)
    gather.arrive(2)
    gather.arrive(3)
    for half in range(2):
        at = rows_of(half)
        h = x[at, :].astype(F32) + total.last(6 + half)
        hidden[at, :] = h
        stat[k, at, :] = jnp.broadcast_to(jnp.sum(h * h, 1, keepdims=True), (PIECE, LANE))
    rstd = lax.rsqrt(exchange(k, stat, ssem) / (2 * width) + EPS)
    rstd_o[...] = jnp.broadcast_to(rstd, rstd_o.shape)
    normed[...] = (hidden[...] * rstd * gain[...]).astype(BF)
    for i in range(4, 8):
        gather.arrive(i)
    for i in range(8):
        gather.ready(i)
    gather.local.wait()
    gather.finish()
    total.finish()


def attend(qkv, kvt, wo, x, gain, dy):
    tokens, width = x.shape
    outs = [
        sds((4, tokens, 2 * LANE), BF),
        sds((2, 8, 1, PIECE), F32),
        sds((tokens, width), F32),
        sds((tokens, width), BF),
        sds((tokens, LANE), F32),
        sds((2, 4, tokens, width), BF),
    ]
    scratch = [pltpu.VMEM((2, tokens, LANE), F32), DMA((2,))] + sum_scratch(width) + GATHER_SEMS
    return call(
        attend_kernel, 1, outs, [VM] * 5 + [ANY], [qkv, kvt, wo, x, gain, dy], scratch, 3e10
    )


def expand_kernel(nf, all_dy, wg, wu, wd, all_f, middle, d_gate, d_up, *sems):
    r, k, rx, ry, r3 = place()
    greet(rx, ry, k)
    gather = Gather(nf, all_f, sems)
    gather.start()

    def compute(i, row, half):
        at = rows_of(half)
        f0, f1 = all_f[0, row, at, :], all_f[1, row, at, :]
        gate = nn(f0, wg[0]) + nn(f1, wg[1])
        upper = nn(f0, wu[0]) + nn(f1, wu[1])
        d_mid = nt(all_dy[0, row, at, :], wd[0]) + nt(all_dy[1, row, at, :], wd[1])
        sig = 1.0 / (1.0 + jnp.exp(-gate))
        swish = gate * sig
        middle[row, at, :] = (swish * upper).astype(BF)
        d_gate[row, at, :] = (d_mid * upper * sig * (1.0 + gate * (1.0 - sig))).astype(BF)
        d_up[row, at, :] = (d_mid * swish).astype(BF)

    gather.run(compute)


def expand(nf, all_dy, wg, wu, wd):
    tokens, width = nf.shape
    f_half = wg.shape[2]
    outs = [sds((2, 4, tokens, width), BF)] + [sds((4, tokens, f_half), BF)] * 3
    return call(
        expand_kernel, 2, outs, [ANY] + [VM] * 4, [nf, all_dy, wg, wu, wd], list(GATHER_SEMS), 3e10
    )


def contract_kernel(
    d_gate, d_up, wg, wu, hidden, rstd2, gain, dy,
    d_hidden, dya, part,
    stat, ssem, *rest,
):
    r, k, rx, ry, r3 = place()
    width = hidden.shape[1]
    greet(rx, ry, k)
    total = Sum(rest)

    def compute(row, half):
        at = rows_of(half)
        g, u = d_gate[row, at, :], d_up[row, at, :]
        return nt(g, wg[k]) + nt(u, wu[k]), nt(g, wg[1 - k]) + nt(u, wu[1 - k])

    total.send_all(compute)
    total.relay(4)
    total.relay(5)
    gains = jnp.zeros((1, width), F32)
    for half in range(2):
        at = rows_of(half)
        d_nf = total.last(6 + half)
        h = hidden[at, :]
        gains = gains + jnp.sum(d_nf * h * rstd2[at, 0:1], 0, keepdims=True)
        scaled = d_nf * gain[...]
        d_hidden[at, :] = scaled
        stat[k, at, :] = jnp.broadcast_to(jnp.sum(scaled * h, 1, keepdims=True), (PIECE, LANE))
    part[...] = gains
    inner = exchange(k, stat, ssem) / (2 * width)
    rs = rstd2[:, 0:1]
    value = dy[...].astype(F32) + rs * d_hidden[...] - hidden[...] * (rs * rs * rs * inner)
    d_hidden[...] = value
    dya[...] = value.astype(BF)
    total.finish()


def contract(d_gate, d_up, wg, wu, hidden, rstd2, gain, dy):
    tokens, width = hidden.shape
    outs = [sds((tokens, width), F32), sds((tokens, width), BF), sds((1, width), F32)]
    scratch = [pltpu.VMEM((2, tokens, LANE), F32), DMA((2,))] + sum_scratch(width)
    args = [d_gate, d_up, wg, wu, hidden, rstd2, gain, dy]
    return call(contract_kernel, 3, outs, [VM] * 8, args, scratch, 3e10)


def unproject_kernel(dya, wo, all_dya, d_attn, *sems):
    r, k, rx, ry, r3 = place()
    greet(rx, ry, k)
    gather = Gather(dya, all_dya, sems)
    gather.start()

    def compute(i, row, half):
        at = rows_of(half)
        got = nt(all_dya[0, row, at, :], wo[0]) + nt(all_dya[1, row, at, :], wo[1])
        d_attn[row, at, :] = got.astype(BF)

    gather.run(compute)


def unproject(dya, wo):
    tokens, width = dya.shape
    outs = [sds((2, 4, tokens, width), BF), sds((4, tokens, 2 * LANE), BF)]
    return call(unproject_kernel, 4, outs, [ANY, VM], [dya, wo], list(GATHER_SEMS), 3e10)


def backward_kernel(
    qkv, kvt, lse, d_attn, cos, sin, wqkv, middle, wd, hidden, x, rstd1, d_hidden, gain,
    d_proj, output, grad_x, part,
    dk, dv, stat, ssem, *rest,
):
    r, k, rx, ry, r3 = place()
    width = x.shape[1]
    greet(rx, ry, k)
    down = Sum(rest[:9])
    into = Sum(rest[9:])

    def down_piece(row, half):
        m = middle[row, rows_of(half), :]
        return nn(m, wd[k]), nn(m, wd[1 - k])

    down.send_all(down_piece)

    def unrotate(u, p):
        at = pl.ds(p * PIECE, PIECE)
        return u * cos[at, :] - pltpu.roll(u, LANE // 2, 1) * sin[at, :]

    def sequence(seq):
        base = pl.multiple_of(seq * LENGTH, LENGTH)

        def one_head(head, carry):
            for p in range(4):
                span = PIECE * (p + 1)
                row = seq * 2 + p // 2
                at = pl.ds((p % 2) * PIECE, PIECE)
                out = pl.ds(pl.multiple_of(base + p * PIECE, PIECE), PIECE)
                keys = qkv[2, pl.ds(base, span), :]
                q = qkv[head, out, :]
                lane = pl.ds(pl.multiple_of(head * LANE, LANE), LANE)
                do = d_attn[row, at, lane]
                e = jnp.exp(nt(keys, q) * SCALE - lse[head, seq * 4 + p])
                tail = jnp.where(causal((PIECE, PIECE)), e[span - PIECE :], 0.0)
                e = tail if p == 0 else jnp.concatenate([e[: span - PIECE], tail], 0)
                dp = nt(qkv[3, pl.ds(base, span), :], do)
                inner = jnp.sum(e * dp, 0, keepdims=True)
                ds = (e * (dp - inner)).astype(BF)
                dv[0:span, :] += nn(e.astype(BF), do)
                dk[0:span, :] += nn(ds, q)
                dq = nn(kvt[0, :, pl.ds(base, span)], ds).T * SCALE
                d_proj[out, lane] = unrotate(dq, p).astype(BF)
            return carry

        dk[...] = jnp.zeros_like(dk)
        dv[...] = jnp.zeros_like(dv)
        lax.fori_loop(0, 2, one_head, 0)
        for p in range(4):
            at = pl.ds(p * PIECE, PIECE)
            out = pl.ds(pl.multiple_of(base + p * PIECE, PIECE), PIECE)
            d_proj[out, 2 * LANE : 3 * LANE] = unrotate(dk[at, :] * SCALE, p).astype(BF)
            d_proj[out, 3 * LANE : 4 * LANE] = dv[at, :].astype(BF)

    def both(n, carry):
        sequence(jnp.where(n == 0, ry // 2, r // 2))

        @pl.when(n == 0)
        def _():
            down.relay(4)
            down.relay(5)

        return carry

    lax.fori_loop(0, 2, both, 0)

    def into_piece(row, half):
        d = d_proj[pl.ds(pl.multiple_of(row * 2 * PIECE + half * PIECE, PIECE), PIECE), :]
        return nt(d, wqkv[k]), nt(d, wqkv[1 - k])

    into.send_all(into_piece)
    for half in range(2):
        at = rows_of(half)
        output[at, :] = hidden[at, :] + down.last(6 + half)
    into.relay(4)
    into.relay(5)
    gains = jnp.zeros((1, width), F32)
    for half in range(2):
        at = rows_of(half)
        d_na = into.last(6 + half)
        xs = x[at, :].astype(F32)
        gains = gains + jnp.sum(d_na * xs * rstd1[at, 0:1], 0, keepdims=True)
        scaled = d_na * gain[...]
        grad_x[at, :] = scaled
        stat[k, at, :] = jnp.broadcast_to(jnp.sum(scaled * xs, 1, keepdims=True), (PIECE, LANE))
    part[...] = gains
    inner = exchange(k, stat, ssem) / (2 * width)
    rs = rstd1[:, 0:1]
    grad_x[...] = d_hidden[...] + rs * grad_x[...] - x[...].astype(F32) * (rs * rs * rs * inner)
    down.finish()
    into.finish()


def backward(qkv, kvt, lse, d_attn, cos, sin, wqkv, middle, wd, hidden, x, rstd1, d_hidden, gain):
    tokens, width = x.shape
    outs = [
        sds((4 * tokens, 4 * LANE), BF),
        sds((tokens, width), F32),
        sds((tokens, width), F32),
        sds((1, width), F32),
    ]
    scratch = (
        [pltpu.VMEM((LENGTH, LANE), F32)] * 2
        + [pltpu.VMEM((2, tokens, LANE), F32), DMA((2,))]
        + sum_scratch(width)
        + sum_scratch(width)
    )
    args = [qkv, kvt, lse, d_attn, cos, sin, wqkv, middle, wd, hidden, x, rstd1, d_hidden, gain]
    return call(backward_kernel, 5, outs, [VM] * len(args), args, scratch, 5e10)


def gains_kernel(groups, a, f, out, slots, send, recv):
    dp, r = lax.axis_index("dp"), lax.axis_index("row")
    me = dp * 4 + r

    def peer(t):
        other = (me + t) % groups
        return other, {"dp": other // 4, "row": other % 4}

    bar = pltpu.get_barrier_semaphore()

    def hello(t, carry):
        pl.semaphore_signal(bar, inc=1, device_id=peer(t)[1], device_id_type=MESH)
        return carry

    lax.fori_loop(1, groups, hello, 0)
    slots[me, 0:1, :] = a[...]
    slots[me, 1:2, :] = f[...]
    pl.semaphore_wait(bar, groups - 1)

    def start(t, carry):
        remote(slots.at[me], slots.at[me], send.at[t], recv.at[me], peer(t)[1]).start()
        return carry

    lax.fori_loop(1, groups, start, 0)

    def wait(t, carry):
        other, device = peer(t)
        remote(slots.at[me], slots.at[other], send.at[t], recv.at[other], device).wait_recv()
        remote(slots.at[me], slots.at[me], send.at[t], recv.at[me], device).wait_send()
        return carry

    lax.fori_loop(1, groups, wait, 0)
    out[...] = lax.fori_loop(1, groups, lambda g, total: total + slots[g], slots[0])


def gains_total(a, f, groups):
    import functools

    outs = [sds((2, a.shape[1]), F32)]
    scratch = [pltpu.VMEM((groups, 2, a.shape[1]), F32), DMA((groups,)), DMA((groups,))]
    return call(
        functools.partial(gains_kernel, groups), 6, outs, [VM] * 2, [a, f], scratch, 1e6, vmem=8
    )[0]


def dp_total(part):
    n = lax.axis_size("dp")
    z = lax.axis_index("dp")
    mid = n // 2

    def add(a, b):
        return (a.astype(F32) + b.astype(F32)).astype(BF)

    for s in range(mid - 1):
        part = add(part, lax.ppermute(part, "dp", [(s, s + 1), (n - 1 - s, n - 2 - s)]))
    part = add(part, lax.ppermute(part, "dp", [(mid - 1, mid), (mid, mid - 1)]))
    for s in reversed(range(mid - 1)):
        got = lax.ppermute(part, "dp", [(s + 1, s), (n - 2 - s, n - 1 - s)])
        part = jnp.where((z == s) | (z == n - 1 - s), got, part)
    return part


def swap(both, k):
    mine = lax.dynamic_index_in_dim(both, k, 0, False)
    his = lax.dynamic_index_in_dim(both, 1 - k, 0, False)
    return mine, lax.ppermute(his, "col", [(0, 1), (1, 0)])


def weight_grad(left, right):
    return lax.dot_general(left, right, (((0,), (0,)), ((), ())), preferred_element_type=F32).astype(BF)


def side_by_side(mine, his, k, axis):
    first = jnp.where(k == 0, mine, his)
    second = jnp.where(k == 0, his, mine)
    return jnp.concatenate([first, second], axis)


def on_device(
    layer_input, gain_attn, gain_ffn, w_query, w_key, w_value, w_out, w_gate, w_up, w_down, cotangent
):
    k = lax.axis_index("col")
    tokens, width = layer_input.shape
    q_cols, k_cols = w_query.shape[1], w_key.shape[1]
    gain_a, gain_f = gain_attn[None], gain_ffn[None]
    normed, qkv, kvt, wqkv, wo, wg, wu, wd, cos, sin, rstd1 = project(
        layer_input, gain_a, w_query, w_key, w_value, w_out, w_gate, w_up, w_down
    )
    attn, lse, hidden, nf, rstd2, all_dy = attend(qkv, kvt, wo, layer_input, gain_f, cotangent)
    all_f, middle, d_gate, d_up = expand(nf, all_dy, wg, wu, wd)

    def flat(a):
        return a.reshape(4 * tokens, a.shape[-1])

    def grads_of(gathered, right):
        return jnp.stack([weight_grad(flat(gathered[h]), flat(right)) for h in range(2)])

    mid = flat(middle)
    g_down = jnp.stack([weight_grad(mid, flat(all_dy[h])) for h in range(2)])
    down = dp_total(side_by_side(*swap(g_down, k), k, 0))
    gate = dp_total(side_by_side(*swap(grads_of(all_f, d_gate), k), k, 1))
    up = dp_total(side_by_side(*swap(grads_of(all_f, d_up), k), k, 1))

    d_hidden, dya, part_f = contract(d_gate, d_up, wg, wu, hidden, rstd2, gain_f, cotangent)
    all_dya, d_attn = unproject(dya, wo)
    g_out = jnp.stack([weight_grad(flat(attn), flat(all_dya[h])) for h in range(2)])
    d_proj, output, grad_x, part_a = backward(
        qkv, kvt, lse, d_attn, cos, sin, wqkv, middle, wd, hidden, layer_input, rstd1, d_hidden, gain_a
    )
    gains = gains_total(part_a, part_f, lax.axis_size("dp") * 4)

    mine, his = swap(g_out, k)
    n = 2 * LANE
    out = nn(spread(q_cols, n, k * q_cols // 2), mine) + nn(
        spread(q_cols, n, (1 - k) * q_cols // 2), his
    )
    mine, his = swap(grads_of(normed, d_proj), k)

    def columns(core):
        part = [
            jnp.pad(spread_t(n, q_cols, core * q_cols // 2), ((0, 0), (0, 2 * k_cols))),
            jnp.pad(spread_t(LANE, k_cols, core * k_cols // 2), ((0, 0), (q_cols, k_cols))),
            jnp.pad(spread_t(LANE, k_cols, core * k_cols // 2), ((0, 0), (q_cols + k_cols, 0))),
        ]
        return jnp.concatenate(part, 0)

    into = nn(mine, columns(k)) + nn(his, columns(1 - k))
    last = dp_total(jnp.concatenate([out.astype(BF), into.astype(BF)], 0))
    out, into = last[:q_cols].astype(F32), last[q_cols:].astype(F32)
    return (
        output,
        grad_x,
        gains[0],
        gains[1],
        into[:, :q_cols],
        into[:, q_cols : q_cols + k_cols],
        into[:, q_cols + k_cols :],
        out,
        gate.astype(F32),
        up.astype(F32),
        down.astype(F32),
    )


def solution(mesh):
    assert mesh.shape["row"] == 4 and mesh.shape["col"] == 2
    tokens = P(("dp", "row"), "col")
    wide = P("col", "row")
    tall = P("row", "col")
    return jax.shard_map(
        on_device,
        mesh=mesh,
        in_specs=(tokens, P("col"), P("col"), wide, wide, wide, tall, wide, wide, tall, tokens),
        out_specs=(tokens, tokens, P("col"), P("col"), wide, wide, wide, tall, wide, wide, tall),
        check_vma=False,
    )
```

time: 1420 us -> 687 us (0.48)
  waiting for transfers between devices: 918 us -> 125 us
  Pallas kernels: 0 us -> 405 us
  matrix products: 176 us -> 36 us
  local copies, waits for them, and re-layouts: 161 us -> 51.9 us
  blocking collectives: 66.8 us -> 0 us
  other arithmetic: 69.4 us -> 39.8 us
  starting transfers between devices: 0.45 us -> 18.1 us
    psum x3 -> x0, waiting for transfers between devices: 505 us -> none  [the longest x1 392 us: on_device(): lax.psum((gw_down, gw_gateup, gw_in, gw_out), 'dp')]
    pallas_call x0 -> x7, Pallas kernels: none -> 405 us  [call(): pl.pallas_call(kernel, out_shape=outs, in_specs=ins, out_specs=[VM] * len...]
    reduce_scatter x4 -> x0, waiting for transfers between devices: 247 us -> none  [token_sum(): lax.psum_scatter(jnp.einsum('tj,jc->tc', source, weight, preferred_elemen...]
    all_gather x4 -> x0, waiting for transfers between devices: 165 us -> none  [gather_tokens(): return lax.all_gather(values, 'row', axis=0, tiled=True)]
    dot_general x40 -> x14, matrix products: 176 us -> 36 us  [the longest x10 26.4 us: weight_grad(): lax.dot_general(left, right, (((0,), (0,)), ((), ())), preferred_element_...]
    ppermute x0 -> x17, waiting for transfers between devices: none -> 125 us  [the longest x4 125 us: dp_total(): lax.ppermute(part, 'dp', [(s, s + 1), (n - 1 - s, n - 2 - s)])]
    dynamic_update_slice x16 -> x0, local copies, waits for them, and re-layouts: 70.9 us -> none  [attend_forward(): mixed, logsum = lax.map(one_block, (query_seq, jnp.arange(count)))]
    psum x6 -> x0, blocking collectives: 66.8 us -> none  [the longest x1 44.6 us: on_device(): gain_a, gain_f = lax.psum((part_gain_attn, part_gain_ffn), ('dp', 'row'))]
  transfers between devices with their start and end apart: 11 -> 17, of which waited for: 11 -> 4; matrix products, arithmetic and copies ran while one was open for 4% -> 11% of each run, Pallas kernels for 0% -> 40%
where the time goes in v1:
time: 687 us; the launch traced here: 678 us
  Pallas kernels  405 us (59%)
  waiting for transfers between devices  125 us (18%)
  local copies, waits for them, and re-layouts  51.9 us (8%)
  other arithmetic  39.8 us (6%)
  matrix products  36 us (5%)
  starting transfers between devices  18.1 us (3%)
    pallas_call x7, Pallas kernels, call(): pl.pallas_call(kernel, out_shape=outs, in_specs=ins, out_specs=[VM] * len...  405 us
    ppermute x4, waiting for transfers between devices, dp_total(): lax.ppermute(part, 'dp', [(s, s + 1), (n - 1 - s, n - 2 - s)])  125 us
    unnamed x124, local copies, waits for them, and re-layouts  29.6 us
    dot_general x10, matrix products, weight_grad(): lax.dot_general(left, right, (((0,), (0,)), ((), ())), preferred_element_...  26.4 us
  transfers between devices with their start and end apart: 17, of which 4 were waited for; matrix products, arithmetic and copies ran while one was open for 11% of the time, Pallas kernels for 40%

profile of v1, /device:TPU:0, one launch (start us, length us, event | category | flops | bytes accessed | tf_op | source)
XLA Modules:
  0.0 678.0 jit_solution(4570257980650596260)
XLA Ops:
  10.4 38.3 %shard_map.230 = (bf16[2,4,512,768]{3,2,1,0:T(8,128)(2,1)}, bf16[4,2048,128]{2,1,0:T(8,128)(2,1)}, bf16[2,128,2048]{2,1,0:T(8,128)(2,1)S(1)}, bf16[2,768,512]{2,...) custom-call(bf16[512,768]{1,0:T(8,128)(2,1)S(1)} %copy-done.3, ...), custom_call_target="tpu_custom_call" | custom-call | flops 30000001024 | bytes 25168896 | tf_op jit(solution)/shard_map/pallas_call | solution.py:216
  51.5 2.8 copy-done.16
  54.3 58.8 %shard_map.231 = (bf16[4,512,256]{2,1,0:T(8,128)(2,1)S(1)}, f32[2,8,1,256]{3,2,1,0:T(1,128)S(1)}, f32[512,768]{1,0:T(8,128)S(1)}, bf16[512,768]{1,0:T(8,128)(2,1...) custom-call(bf16[4,2048,128]{2,1,0:T(8,128)(2,1)S(1)} %copy-done.16, ...), custom_call_target="tpu_custom_call" | custom-call | flops 30000001024 | bytes 15485952 | tf_op jit(solution)/shard_map/pallas_call | solution.py:216
  113.2 5.5 fusion.116
  118.7 39.6 %shard_map.232 = (bf16[2,4,512,768]{3,2,1,0:T(8,128)(2,1)}, bf16[4,512,512]{2,1,0:T(8,128)(2,1)S(1)}, bf16[4,512,512]{2,1,0:T(8,128)(2,1)S(1)}, bf16[4,512,512]{2,1,0:T(8,128)(2,1)}) custom-call(bf16[512,768]{1,0:T(8,128)(2,1)S(1)} %get-tuple-element.45.nf, bf16[2,4,512,768]{3,2,1,0:T(8,128)(2,1)} %get-tuple-element.46.all_dy, ...), custom_call_target="tpu_custom_call" | custom-call | flops 30000001024 | bytes 24379392 | tf_op jit(solution)/shard_map/pallas_call | solution.py:216
  158.3 5.2 fusion.12
  163.6 2.7 fusion.13
  166.3 2.3 fusion.30
  168.6 3.4 fusion.117
  172.0 2.7 fusion.10
  174.8 2.7 fusion.11
  177.5 2.8 fusion.8
  180.3 2.8 fusion.9
  183.1 4.4 fusion.34
  187.4 2.3 copy.35
  191.5 1.6 copy-done.11
  193.1 1.4 copy-done.19
  194.5 1.4 copy-done.21
  197.3 36.5 %shard_map.233 = (f32[512,768]{1,0:T(8,128)S(1)}, bf16[512,768]{1,0:T(8,128)(2,1)S(1)}, f32[1,768]{1,0:T(1,128)S(1)}) custom-call(bf16[4,512,512]{2,1,0:T(8,128)(2,1)S(1)} %copy-done.11, bf16[4,512,512]{2,1,0:T(8,128)(2,1)} %get-tuple-element.51.d_up, bf16[2,768,512]{2,1,0:T(8,128)(2,1)S(1)} %copy-done.19, bf16[2,768,512]{2,1,0:T(8,128)(2,1)S(1)} %copy-done.21, ...), custom_call_target="tpu_custom_call" | custom-call | flops 30000001024 | bytes 12326912 | tf_op jit(solution)/shard_map/pallas_call | solution.py:216
  234.9 30.4 %shard_map.234 = (bf16[2,4,512,768]{3,2,1,0:T(8,128)(2,1)S(1)}, bf16[4,512,256]{2,1,0:T(8,128)(2,1)S(1)}) custom-call(bf16[512,768]{1,0:T(8,128)(2,1)S(1)} %get-tuple-element.54.dya, bf16[2,256,768]{2,1,0:T(8,128)(2,1)S(1)} %copy-done.30), custom_call_target="tpu_custom_call" | custom-call | flops 30000001024 | bytes 8912896 | tf_op jit(solution)/shard_map/pallas_call | solution.py:216
  271.8 64.1 %shard_map.235 = (bf16[2048,512]{1,0:T(8,128)(2,1)}, f32[512,768]{1,0:T(8,128)S(1)}, f32[512,768]{1,0:T(8,128)S(1)}, f32[1,768]{1,0:T(1,128)S(1)}) custom-call(bf16[4,2048,128]{2,1,0:T(8,128)(2,1)} %get-tuple-element.41.qkv, bf16[2,128,2048]{2,1,0:T(8,128)(2,1)S(1)} %copy-done.28, f32[2,8,1,256]{3,2,1,0:T(1,128)S(1)} %get-tuple-element.44.lse, ...), custom_call_target="tpu_custom_call" | custom-call | flops 49999998976 | bytes 19945472 | tf_op jit(solution)/shard_map/pallas_call | solution.py:216
  335.9 3.5 fusion.7
  339.5 1.8 fusion.6
  345.1 2.5 fusion.58
  348.5 1.6 select_convert_fusion.9
  350.1 3.4 fusion.20
  353.5 2.3 copy.34
  355.8 2.3 copy.32
  358.1 1.8 fusion.5
  360.0 1.5 broadcast_select_fusion.2
  361.6 3.7 collective-permute-start.14
  369.8 1.5 collective-permute-start.6
  371.3 1.9 add_convert_fusion.8
  374.8 25.2 %collective-permute-done.14 = bf16[1024,768]{1,0:T(8,128)(2,1)S(1)} collective-permute-done((bf16[1024,768]{1,0:T(8,128)(2,1)S(1)}, bf16[1024,768]{1,0:T(8,128)(2,1)S(1)}, u32[]{:S(2)}, u32[]{:S(2)}) %collective-permute-start.14) | collective-permute-done | bytes 1572896 | tf_op jit(solution)/shard_map/ppermute | solution.py:729
  401.5 32.3 %collective-permute-done.10 = bf16[768,1024]{1,0:T(8,128)(2,1)S(1)} collective-permute-done((bf16[768,1024]{1,0:T(8,128)(2,1)S(1)}, bf16[768,1024]{1,0:T(8,128)(2,1)S(1)}, u32[]{:S(2)}, u32[]{:S(2)}) %collective-permute-start.10) | collective-permute-done | bytes 1572896 | tf_op jit(solution)/shard_map/ppermute | solution.py:729
  435.1 32.4 %collective-permute-done.6 = bf16[768,1024]{1,0:T(8,128)(2,1)S(1)} collective-permute-done((bf16[768,1024]{1,0:T(8,128)(2,1)S(1)}, bf16[768,1024]{1,0:T(8,128)(2,1)S(1)}, u32[]{:S(2)}, u32[]{:S(2)}) %collective-permute-start.6) | collective-permute-done | bytes 1572896 | tf_op jit(solution)/shard_map/ppermute | solution.py:729
  468.8 35.4 %collective-permute-done.2 = bf16[1152,768]{1,0:T(8,128)(2,1)S(1)} collective-permute-done((bf16[1152,768]{1,0:T(8,128)(2,1)S(1)}, bf16[1152,768]{1,0:T(8,128)(2,1)S(1)}, u32[]{:S(2)}, u32[]{:S(2)}) %collective-permute-start.2) | collective-permute-done | bytes 1769504 | tf_op jit(solution)/shard_map/ppermute | solution.py:729
  505.5 1.6 add_convert_fusion.2
  508.4 1.8 add_convert_fusion.4
  511.5 1.8 add_convert_fusion.6
  514.6 1.7 add_convert_fusion
  517.6 137.4 %shard_map.236 = f32[2,768]{1,0:T(2,128)S(1)} custom-call(f32[1,768]{1,0:T(1,128)S(1)} %get-tuple-element.64.a, f32[1,768]{1,0:T(1,128)S(1)} %get-tuple-element.65.f), custom_call_target="tpu_custom_call" | custom-call | flops 1000000 | bytes 12288 | tf_op jit(solution)/shard_map/pallas_call | solution.py:216
  655.6 3.3 select_convert_fusion
  658.9 3.3 select_convert_fusion.1
  662.2 3.3 select_convert_fusion.2
  665.5 1.7 broadcast_select_fusion
  670.9 2.2 copy.36
  673.1 2.2 copy.37
  (178 shorter events, 51.1 us)
Async XLA Ops:
  1.3 47.4 %copy-start = (f32[1,768]{1,0:T(1,128)}, f32[1,768]{1,0:T(1,128)S(1)}, u32[]{:S(2)}) copy-start(f32[1,768]{1,0:T(1,128)S(1)} %broadcast_in_dim.57.gain) | copy-start | bytes 9220
  10.4 41.1 %copy-start.2 = (bf16[512,768]{1,0:T(8,128)(2,1)S(1)}, bf16[512,768]{1,0:T(8,128)(2,1)}, u32[]{:S(2)}) copy-start(bf16[512,768]{1,0:T(8,128)(2,1)} %dy.3) | copy-start | bytes 2359300
  10.4 41.1 %copy-start.4 = (bf16[512,768]{1,0:T(8,128)(2,1)S(1)}, bf16[512,768]{1,0:T(8,128)(2,1)}, u32[]{:S(2)}) copy-start(bf16[512,768]{1,0:T(8,128)(2,1)} %x.17) | copy-start | bytes 2359300
  51.5 61.6 %copy-start.27 = (bf16[2,128,2048]{2,1,0:T(8,128)(2,1)}, bf16[2,128,2048]{2,1,0:T(8,128)(2,1)S(1)}, u32[]{:S(2)}) copy-start(bf16[2,128,2048]{2,1,0:T(8,128)(2,1)S(1)} %get-tuple-element.42.kvt) | copy-start | bytes 3145732
  51.5 61.6 %copy-start.29 = (bf16[2,256,768]{2,1,0:T(8,128)(2,1)}, bf16[2,256,768]{2,1,0:T(8,128)(2,1)S(1)}, u32[]{:S(2)}) copy-start(bf16[2,256,768]{2,1,0:T(8,128)(2,1)S(1)} %get-tuple-element.43.wo) | copy-start | bytes 2359300
  51.5 67.2 %copy-start.18 = (bf16[2,768,512]{2,1,0:T(8,128)(2,1)}, bf16[2,768,512]{2,1,0:T(8,128)(2,1)S(1)}, u32[]{:S(2)}) copy-start(bf16[2,768,512]{2,1,0:T(8,128)(2,1)S(1)} %get-tuple-element.47.wg) | copy-start | bytes 4718596
  51.5 2.8 copy-start.16
  113.1 5.5 copy-start.22
  113.1 5.5 copy-start.17
  113.2 5.5 copy-start.20
  158.3 5.3 copy-start.9
  158.3 5.3 copy-start.8
  163.5 2.7 copy-start.36
  168.6 191.4 %collective-permute-start.13 = (bf16[512,768]{1,0:T(8,128)(2,1)}, bf16[512,768]{1,0:T(8,128)(2,1)}, u32[]{:S(2)}, u32[]{:S(2)}) collective-permute-start(bf16[512,768]{1,0:T(8,128)(2,1)} %fusion.30), channel_id=1, source_target_pairs={{0,1},{1,0},{2,3},{3,2},{4,5},{5,4},{6,7},{7,6},{8,9},{9,8},{10,11... | collective-permute-start | bytes 2359304 | tf_op jit(solution)/shard_map/ppermute | solution.py:740
  168.6 3.4 copy-start.55
  174.8 2.7 copy-start.10
  189.7 175.6 %collective-permute-start.9 = (bf16[768,512]{1,0:T(8,128)(2,1)}, bf16[768,512]{1,0:T(8,128)(2,1)}, u32[]{:S(2)}, u32[]{:S(2)}) collective-permute-start(bf16[768,512]{1,0:T(8,128)(2,1)} %bitcast.99), channel_id=1, source_target_pairs={{0,1},{1,0},{2,3},{3,2},{4,5},{5,4},{6,7},{7,6},{8,9},{9,8},{10,11... | collective-permute-start | bytes 2359304 | tf_op jit(solution)/shard_map/ppermute | solution.py:740
  191.5 176.8 %collective-permute-start.5 = (bf16[768,512]{1,0:T(8,128)(2,1)}, bf16[768,512]{1,0:T(8,128)(2,1)}, u32[]{:S(2)}, u32[]{:S(2)}) collective-permute-start(bf16[768,512]{1,0:T(8,128)(2,1)} %bitcast.98), channel_id=1, source_target_pairs={{0,1},{1,0},{2,3},{3,2},{4,5},{5,4},{6,7},{7,6},{8,9},{9,8},{10,11... | collective-permute-start | bytes 2359304 | tf_op jit(solution)/shard_map/ppermute | solution.py:740
  197.3 37.6 %copy-start.30 = (bf16[2,256,768]{2,1,0:T(8,128)(2,1)S(1)}, bf16[2,256,768]{2,1,0:T(8,128)(2,1)}, u32[]{:S(2)}) copy-start(bf16[2,256,768]{2,1,0:T(8,128)(2,1)} %copy-done.29) | copy-start | bytes 2359300
  197.3 72.3 %slice-start = ((s8[6291456]{0:T(1024)(128)(4,1)}), s8[4194304]{0:T(1024)(128)(4,1)S(1)}, s32[]{:S(2)}) async-start(s8[6291456]{0:T(1024)(128)(4,1)} %bitcast.88), calls=%async_computation | async-start | bytes 8388608
  234.9 34.6 %slice-start.1 = ((s8[6291456]{0:T(1024)(128)(4,1)}), s8[2097152]{0:T(1024)(128)(4,1)S(1)}, s32[]{:S(2)}) async-start(s8[6291456]{0:T(1024)(128)(4,1)} %bitcast.88), calls=%async_computation.1 | async-start | bytes 4194304
  267.8 2.2 copy-start.45
  268.7 89.4 %collective-permute-start = (bf16[256,768]{1,0:T(8,128)(2,1)}, bf16[256,768]{1,0:T(8,128)(2,1)}, u32[]{:S(2)}, u32[]{:S(2)}) collective-permute-start(bf16[256,768]{1,0:T(8,128)(2,1)} %fusion.55), channel_id=1, source_target_pairs={{0,1},{1,0},{2,3},{3,2},{4,5},{5,4},{6,7},{7,6},{8,9},{9,8},{10,11... | collective-permute-start | bytes 1179656 | tf_op jit(solution)/shard_map/ppermute | solution.py:740
  269.6 2.2 copy-start.34
  335.9 3.6 copy-start.35
  341.3 3.8 copy-start.44
  342.5 28.8 %collective-permute-start.1 = (bf16[768,512]{1,0:T(8,128)(2,1)}, bf16[768,512]{1,0:T(8,128)(2,1)}, u32[]{:S(2)}, u32[]{:S(2)}) collective-permute-start(bf16[768,512]{1,0:T(8,128)(2,1)} %fusion.38), channel_id=1, source_target_pairs={{0,1},{1,0},{2,3},{3,2},{4,5},{5,4},{6,7},{7,6},{8,9},{9,8},{10,11... | collective-permute-start | bytes 2359304 | tf_op jit(solution)/shard_map/ppermute | solution.py:740
  345.1 2.5 copy-start.47
  345.1 2.5 copy-start.49
  345.1 2.5 copy-start.51
  345.1 2.5 copy-start.53
  353.5 4.6 copy-start.48
  353.5 4.6 copy-start.50
  353.5 4.6 copy-start.52
  353.5 4.6 copy-start.54
  361.5 3.9 copy-start.42
  361.6 38.4 %collective-permute-start.14 = (bf16[1024,768]{1,0:T(8,128)(2,1)S(1)}, bf16[1024,768]{1,0:T(8,128)(2,1)S(1)}, u32[]{:S(2)}, u32[]{:S(2)}) collective-permute-start(bf16[1024,768]{1,0:T(8,128)(2,1)S(1)} %pad_maximum_fusion.3), channel_id=1, source_target_pairs={{0,8},{24,16},{1,9},{25,17},{2,10},{26,18},{3,11},{27,19},{4,12},{... | collective-permute-start | bytes 4718600 | tf_op jit(solution)/shard_map/ppermute | solution.py:729
  366.9 66.9 %collective-permute-start.10 = (bf16[768,1024]{1,0:T(8,128)(2,1)S(1)}, bf16[768,1024]{1,0:T(8,128)(2,1)S(1)}, u32[]{:S(2)}, u32[]{:S(2)}) collective-permute-start(bf16[768,1024]{1,0:T(8,128)(2,1)S(1)} %pad_maximum_fusion.2), channel_id=1, source_target_pairs={{0,8},{24,16},{1,9},{25,17},{2,10},{26,18},{3,11},{27,19},{4,12},{... | collective-permute-start | bytes 4718600 | tf_op jit(solution)/shard_map/ppermute | solution.py:729
  369.8 97.6 %collective-permute-start.6 = (bf16[768,1024]{1,0:T(8,128)(2,1)S(1)}, bf16[768,1024]{1,0:T(8,128)(2,1)S(1)}, u32[]{:S(2)}, u32[]{:S(2)}) collective-permute-start(bf16[768,1024]{1,0:T(8,128)(2,1)S(1)} %pad_maximum_fusion.1), channel_id=1, source_target_pairs={{0,8},{24,16},{1,9},{25,17},{2,10},{26,18},{3,11},{27,19},{4,12},{... | collective-permute-start | bytes 4718600 | tf_op jit(solution)/shard_map/ppermute | solution.py:729
  373.4 130.8 %collective-permute-start.2 = (bf16[1152,768]{1,0:T(8,128)(2,1)S(1)}, bf16[1152,768]{1,0:T(8,128)(2,1)S(1)}, u32[]{:S(2)}, u32[]{:S(2)}) collective-permute-start(bf16[1152,768]{1,0:T(8,128)(2,1)S(1)} %pad_maximum_fusion), channel_id=1, source_target_pairs={{0,8},{24,16},{1,9},{25,17},{2,10},{26,18},{3,11},{27,19},{4,12},{... | collective-permute-start | bytes 5308424 | tf_op jit(solution)/shard_map/ppermute | solution.py:729
  400.4 105.0 %collective-permute-start.15 = (bf16[1024,768]{1,0:T(8,128)(2,1)S(1)}, bf16[1024,768]{1,0:T(8,128)(2,1)S(1)}, u32[]{:S(2)}, u32[]{:S(2)}) collective-permute-start(bf16[1024,768]{1,0:T(8,128)(2,1)S(1)} %add_convert_fusion.3), channel_id=1, source_target_pairs={{8,16},{16,8},{9,17},{17,9},{10,18},{18,10},{11,19},{19,11},{12,20... | collective-permute-start | bytes 4718600 | tf_op jit(solution)/shard_map/ppermute | solution.py:730
  434.3 74.0 %collective-permute-start.11 = (bf16[768,1024]{1,0:T(8,128)(2,1)S(1)}, bf16[768,1024]{1,0:T(8,128)(2,1)S(1)}, u32[]{:S(2)}, u32[]{:S(2)}) collective-permute-start(bf16[768,1024]{1,0:T(8,128)(2,1)S(1)} %add_convert_fusion.5), channel_id=1, source_target_pairs={{8,16},{16,8},{9,17},{17,9},{10,18},{18,10},{11,19},{19,11},{12,20... | collective-permute-start | bytes 4718600 | tf_op jit(solution)/shard_map/ppermute | solution.py:730
  468.0 43.5 %collective-permute-start.7 = (bf16[768,1024]{1,0:T(8,128)(2,1)S(1)}, bf16[768,1024]{1,0:T(8,128)(2,1)S(1)}, u32[]{:S(2)}, u32[]{:S(2)}) collective-permute-start(bf16[768,1024]{1,0:T(8,128)(2,1)S(1)} %add_convert_fusion.7), channel_id=1, source_target_pairs={{8,16},{16,8},{9,17},{17,9},{10,18},{18,10},{11,19},{19,11},{12,20... | collective-permute-start | bytes 4718600 | tf_op jit(solution)/shard_map/ppermute | solution.py:730
  504.7 9.9 %collective-permute-start.3 = (bf16[1152,768]{1,0:T(8,128)(2,1)S(1)}, bf16[1152,768]{1,0:T(8,128)(2,1)S(1)}, u32[]{:S(2)}, u32[]{:S(2)}) collective-permute-start(bf16[1152,768]{1,0:T(8,128)(2,1)S(1)} %add_convert_fusion.1), channel_id=1, source_target_pairs={{8,16},{16,8},{9,17},{17,9},{10,18},{18,10},{11,19},{19,11},{12,20... | collective-permute-start | bytes 5308424 | tf_op jit(solution)/shard_map/ppermute | solution.py:730
  507.1 148.6 %collective-permute-start.16 = (bf16[1024,768]{1,0:T(8,128)(2,1)}, bf16[1024,768]{1,0:T(8,128)(2,1)}, u32[]{:S(2)}, u32[]{:S(2)}) collective-permute-start(bf16[1024,768]{1,0:T(8,128)(2,1)} %add_convert_fusion.2), channel_id=1, source_target_pairs={{8,0},{16,24},{9,1},{17,25},{10,2},{18,26},{11,3},{19,27},{12,4},{... | collective-permute-start | bytes 4718600 | tf_op jit(solution)/shard_map/ppermute | solution.py:732
  510.2 148.7 %collective-permute-start.12 = (bf16[768,1024]{1,0:T(8,128)(2,1)}, bf16[768,1024]{1,0:T(8,128)(2,1)}, u32[]{:S(2)}, u32[]{:S(2)}) collective-permute-start(bf16[768,1024]{1,0:T(8,128)(2,1)} %add_convert_fusion.4), channel_id=1, source_target_pairs={{8,0},{16,24},{9,1},{17,25},{10,2},{18,26},{11,3},{19,27},{12,4},{... | collective-permute-start | bytes 4718600 | tf_op jit(solution)/shard_map/ppermute | solution.py:732
  513.3 148.9 %collective-permute-start.8 = (bf16[768,1024]{1,0:T(8,128)(2,1)}, bf16[768,1024]{1,0:T(8,128)(2,1)}, u32[]{:S(2)}, u32[]{:S(2)}) collective-permute-start(bf16[768,1024]{1,0:T(8,128)(2,1)} %add_convert_fusion.6), channel_id=1, source_target_pairs={{8,0},{16,24},{9,1},{17,25},{10,2},{18,26},{11,3},{19,27},{12,4},{... | collective-permute-start | bytes 4718600 | tf_op jit(solution)/shard_map/ppermute | solution.py:732
  516.3 149.2 %collective-permute-start.4 = (bf16[1152,768]{1,0:T(8,128)(2,1)}, bf16[1152,768]{1,0:T(8,128)(2,1)}, u32[]{:S(2)}, u32[]{:S(2)}) collective-permute-start(bf16[1152,768]{1,0:T(8,128)(2,1)} %add_convert_fusion), channel_id=1, source_target_pairs={{8,0},{16,24},{9,1},{17,25},{10,2},{18,26},{11,3},{19,27},{12,4},{... | collective-permute-start | bytes 5308424 | tf_op jit(solution)/shard_map/ppermute | solution.py:732
  (28 other events, 36.4 us)

commit v2 on v1

--- a/solution.py
+++ b/solution.py
@@ -1,3 +1,5 @@
+import functools
+
 import jax
 import jax.numpy as jnp
 import numpy as np
@@ -37,11 +39,47 @@
     return r, k, r + 1 - 2 * (r % 2), (r + 2) % 4, 3 - r
 
 
-def greet(rx, ry, k):
+def tn(a, b):
+    return lax.dot_general(a, b, (((0,), (0,)), ((), ())), preferred_element_type=F32)
+
+
+def line_place():
+    n = lax.axis_size("dp")
+    z = lax.axis_index("dp")
+    left = z < n // 2
+    step = jnp.where(left, 1, -1)
+    return n, jnp.where(left, z, n - 1 - z), z + step, z - step
+
+
+def greet(rx, ry, k, line=False, groups=False):
     bar = pltpu.get_barrier_semaphore()
+
+    def hello(device):
+        pl.semaphore_signal(bar, inc=1, device_id=device, device_id_type=MESH)
+
     for device in ({"row": rx}, {"row": ry}, {"col": 1 - k}):
-        pl.semaphore_signal(bar, inc=1, device_id=device, device_id_type=MESH)
-    pl.semaphore_wait(bar, 3)
+        hello(device)
+    if not line:
+        pl.semaphore_wait(bar, 3)
+        return
+    n, s, inward, outward = line_place()
+    if groups:
+        z = lax.axis_index("dp")
+
+        def one(t, carry):
+            hello({"dp": (z + t) % n})
+            return carry
+
+        lax.fori_loop(1, n, one, 0)
+        pl.semaphore_wait(bar, 3 + n - 1)
+        return
+    hello({"dp": inward})
+
+    @pl.when(s > 0)
+    def _():
+        hello({"dp": outward})
+
+    pl.semaphore_wait(bar, jnp.where(s > 0, 5, 4))
 
 
 def remote(src, dst, send, recv, device):
@@ -106,21 +144,28 @@
         row, half = self.piece(i)
         self.pair(i, 1 - self.k, row, half).wait_recv()
 
-    def run(self, compute):
+    def run(self, compute, before=None, after=None):
         self.local.wait()
 
-        def step(i, carry):
-            self.ready(i)
-            row, half = self.piece(i)
-            compute(i, row, half)
-
-            @pl.when(i < 6)
+        def pair(q, carry):
+            for u in range(2):
+                i = 2 * q + u
+                self.ready(i)
+                row, half = self.piece(i)
+                compute(i, row, half)
+            if before is not None:
+                before(q)
+
+            @pl.when(q < 3)
             def _():
-                self.arrive(i + 2)
-
+                self.arrive(2 * q + 2)
+                self.arrive(2 * q + 3)
+
+            if after is not None:
+                after(q)
             return carry
 
-        lax.fori_loop(0, 8, step, 0)
+        lax.fori_loop(0, 4, pair, 0)
         self.finish()
 
     def finish(self):
@@ -133,7 +178,7 @@
 def sum_scratch(width):
     return [
         pltpu.VMEM((4, PIECE, width), F32),
-        pltpu.VMEM((8, PIECE, width), BF),
+        pltpu.VMEM((4, PIECE, width), BF),
         pltpu.VMEM((8, PIECE, width), BF),
         pltpu.VMEM((6, PIECE, width), BF),
         pltpu.VMEM((6, PIECE, width), BF),
@@ -156,15 +201,19 @@
         return row, j % 2
 
     def pair(self, j):
-        return remote(self.ds.at[j], self.dr.at[j], self.dsend.at[j], self.drecv.at[j], {"col": 1 - self.k})
+        return remote(self.ds.at[j % 4], self.dr.at[j], self.dsend.at[j], self.drecv.at[j], {"col": 1 - self.k})
 
     def ici(self, j):
         device = jnp.where(j == 0, self.ry, jnp.where(j == 2, self.ry, jnp.where(j == 5, self.ry, self.rx)))
         return remote(self.ist.at[j], self.irt.at[j], self.isend.at[j], self.irecv.at[j], {"row": device})
 
     def put(self, j, kept, given):
+        @pl.when(j >= 4)
+        def _():
+            self.pair(j - 4).wait_send()
+
         self.own[j % 4] = kept
-        self.ds[j] = given.astype(BF)
+        self.ds[j % 4] = given.astype(BF)
         self.pair(j).start()
 
     def chip(self, j):
@@ -188,7 +237,7 @@
         self.ici(j - 2).wait_recv()
         return value + self.irt[j - 2].astype(F32)
 
-    def send_all(self, compute):
+    def send_all(self, compute, hook=None):
         def step(j, carry):
             row, half = self.piece(j)
             kept, given = compute(row, half)
@@ -200,24 +249,197 @@
                 def _():
                     self.forward(j - 1)
 
+            if hook is not None:
+                hook(j)
             return carry
 
         lax.fori_loop(0, 8, step, 0)
 
     def finish(self):
-        for j in range(8):
+        for j in range(4, 8):
             self.pair(j).wait_send()
         for j in range(6):
             self.ici(j).wait_send()
 
 
-def call(kernel, cid, outs, ins, args, scratch, flops, vmem=44):
+TALL, WIDE = 128, 768
+CHUNK = TALL // 2
+DOWN_CHUNKS, MLP_CHUNKS, OUT_CHUNKS, ALL_CHUNKS = 16, 48, 54, 66
+RING = 6
+LAG = 2
+
+
+def line_ring(n):
+    return LAG * (2 * (n // 2) - 2) + 6
+
+
+def line_ticks(n):
+    return ALL_CHUNKS + LAG * (2 * (n // 2) - 2)
+
+
+def line_outs(ticks):
+    return [sds((ticks, CHUNK, WIDE), BF)] + [sds((LAG, CHUNK, WIDE), BF)] * 2
+
+
+def line_scratch(n, ticks):
+    slots = (RING, line_ring(n), line_ring(n), RING)
+    return [pltpu.VMEM((count, CHUNK, WIDE), BF) for count in slots] + [DMA((ticks,))] * 6
+
+
+class Line:
+    def __init__(self, parts, totals, carry, scratch, first, ticks, before=None):
+        self.parts, self.totals, self.carry = parts, totals, carry
+        self.acc, self.tot, self.rin, self.rxb = scratch[:4]
+        self.si, self.ri, self.rx, self.so, self.ro, self.out_sem = scratch[4:]
+        self.first, self.ticks = first, ticks
+        self.n, self.s, self.inward, self.outward = line_place()
+        self.mid = self.n // 2
+        self.ring = line_ring(self.n)
+        if before is not None:
+
+            @pl.when(self.s > 0)
+            def _():
+                for b in range(LAG):
+                    self.acc[b] = before[0][b]
+                    self.tot[b] = before[1][b]
+
+    def valid(self, c):
+        return (c >= 0) & (c < ALL_CHUNKS)
+
+    def sends(self, j):
+        s, mid, slot, near = self.s, self.mid, j % self.ring, j % RING
+        to = {"dp": self.inward}
+        c = self.first + j - LAG * s
+        moves = []
+        inward = (self.rin.at[slot], self.ri.at[j])
+        across = (self.rxb.at[near], self.rx.at[j])
+        for lo, hi, ref in self.parts:
+            ok = (s == 0) & (c >= lo) & (c < hi)
+            moves.append((ok, ref, c - lo, across if mid == 1 else inward))
+        if mid > 1:
+            ok = self.valid(c)
+            moves.append((ok & (s == mid - 1), self.acc, near, across))
+            if mid > 2:
+                moves.append((ok & (s > 0) & (s < mid - 1), self.acc, near, inward))
+        out = [
+            (cond, lambda ref=ref, at=at, way=way: remote(ref.at[at], way[0], self.si.at[j], way[1], to))
+            for cond, ref, at, way in moves
+        ]
+        if mid > 1:
+            c = self.first + j - LAG * (2 * mid - 1 - s)
+            out.append(((s > 0) & self.valid(c), lambda: self.outer(j)))
+        return out
+
+    def outer(self, j):
+        return remote(
+            self.tot.at[j % self.ring], self.tot.at[(j + LAG) % self.ring],
+            self.so.at[j], self.ro.at[j], {"dp": self.outward},
+        )
+
+    def begin(self, j):
+        for cond, copy in self.sends(j):
+
+            @pl.when(cond)
+            def _(copy=copy):
+                copy().start()
+
+    def total_of(self, j):
+        copy = lambda: pltpu.make_async_copy(
+            self.tot.at[(j + LAG) % self.ring], self.totals.at[j], self.out_sem.at[j]
+        )
+        return self.valid(self.first + j - LAG * (2 * self.mid - 2 - self.s)), copy
+
+    def settle(self, j):
+        for cond, copy in self.sends(j):
+
+            @pl.when(cond)
+            def _(copy=copy):
+                copy().wait_send()
+
+        cond, copy = self.total_of(j)
+
+        @pl.when(cond)
+        def _():
+            copy().wait()
+
+    def end(self, j):
+        t, s, mid = self.first + j, self.s, self.mid
+        slot, later = j % self.ring, (j + LAG) % self.ring
+        near, next_near = j % RING, (j + LAG) % RING
+
+        @pl.when(j >= 2)
+        def _():
+            self.settle(j - 2)
+
+        def came(buf, at, sem):
+            remote(buf.at[at], buf.at[at], self.si.at[j], sem.at[j], {"dp": self.inward}).wait_recv()
+
+        def add_part(c, buf, at, dst, to):
+            for lo, hi, ref in self.parts:
+
+                @pl.when((c >= lo) & (c < hi))
+                def _(ref=ref, lo=lo):
+                    dst[to] = (ref[c - lo].astype(F32) + buf[at].astype(F32)).astype(BF)
+
+        if mid > 1:
+            c = t - LAG * (s - 1)
+
+            @pl.when((s > 0) & self.valid(c))
+            def _():
+                came(self.rin, slot, self.ri)
+                add_part(c, self.rin, slot, self.acc, next_near)
+
+        @pl.when((s == mid - 1) & self.valid(t - LAG * (mid - 1)))
+        def _():
+            came(self.rxb, near, self.rx)
+            if mid > 1:
+                self.tot[later] = (self.acc[near].astype(F32) + self.rxb[near].astype(F32)).astype(BF)
+            else:
+                add_part(t, self.rxb, near, self.tot, later)
+
+        cond, copy = self.total_of(j)
+        if mid > 1:
+
+            @pl.when((s < mid - 1) & cond)
+            def _():
+                self.outer(j).wait_recv()
+
+        @pl.when(cond)
+        def _():
+            copy().start()
+
+    def open(self):
+        for j in range(min(LAG, self.ticks)):
+            self.begin(j)
+
+    def step(self, j):
+        self.end(j)
+
+        @pl.when(j + LAG < self.ticks)
+        def _():
+            self.begin(j + LAG)
+
+    def rest(self, j):
+        def one(t, carry):
+            self.step(t)
+            return carry
+
+        lax.fori_loop(j, self.ticks, one, 0)
+        for t in range(max(self.ticks - 2, 0), self.ticks):
+            self.settle(t)
+        if self.carry is not None:
+            for b in range(LAG):
+                self.carry[0][b] = self.acc[(self.ticks + b) % RING]
+                self.carry[1][b] = self.tot[(self.ticks + b) % self.ring]
+
+
+def call(kernel, cid, outs, ins, args, scratch, flops, vmem=44, out_specs=None):
     moved = sum(int(np.prod(a.shape)) * a.dtype.itemsize for a in list(args) + list(outs))
     return pl.pallas_call(
         kernel,
         out_shape=outs,
         in_specs=ins,
-        out_specs=[VM] * len(outs),
+        out_specs=out_specs or [VM] * len(outs),
         scratch_shapes=scratch,
         compiler_params=pltpu.CompilerParams(
             collective_id=cid, has_side_effects=True, vmem_limit_bytes=vmem << 20
@@ -260,9 +482,9 @@
 
 
 def project_kernel(
-    x, gain, wq, wk, wv, wo, wg, wu, wd, cc, sc, cf, sf,
+    x, gain, wq_h, wk_h, wv_h, wo_h, wg, wu, wd, tables,
     normed, qkv, kvt, wqkv_o, wo_o, wg_o, wu_o, wd_o, cos_o, sin_o, rstd_o,
-    raw, gains, give_in, give_out, wsem, wrecv, csem, *sems,
+    raw, gains, give_in, give_out, wq, wk, wv, wo, wsem, wrecv, csem, *sems,
 ):
     r, k, rx, ry, r3 = place()
     width = x.shape[1]
@@ -279,7 +501,11 @@
         pltpu.make_async_copy(wu.at[:, mine], wu_o.at[k], csem.at[2]),
         pltpu.make_async_copy(wd.at[mine], wd_o.at[k], csem.at[3]),
     ]
-    for c in keep:
+    first = [
+        pltpu.make_async_copy(src, dst, csem.at[4 + n])
+        for n, (src, dst) in enumerate(((wq_h, wq), (wk_h, wk), (wv_h, wv), (wo_h, wo)))
+    ]
+    for c in first + keep:
         c.start()
 
     def give(n, src, dst):
@@ -288,25 +514,28 @@
     gives = [give(0, gain, gains)]
     gives[0].start()
     heads_q = wq.shape[1] // 2
-    heads_k = wk.shape[1] // 2
+    heads_k = wk.shape[0] // 2
     nq = heads_q // HD * LANE
     nk = heads_k // HD * LANE
+    for c in first:
+        c.wait()
     for core, dst_in, dst_out in ((1 - k, give_in, give_out), (k, wqkv_o.at[k], wo_o.at[k])):
         sq = spread(2 * heads_q, nq, core * heads_q)
         sk = spread(2 * heads_k, nk, core * heads_k)
         dst_in[:, 0:nq] = nn(wq[...], sq).astype(BF)
-        dst_in[:, nq : nq + nk] = nn(wk[...], sk).astype(BF)
-        dst_in[:, nq + nk : nq + 2 * nk] = nn(wv[...], sk).astype(BF)
+        dst_in[:, nq : nq + nk] = tn(wk[...], sk).astype(BF)
+        dst_in[:, nq + nk : nq + 2 * nk] = tn(wv[...], sk).astype(BF)
         dst_out[...] = nn(spread_t(nq, 2 * heads_q, core * heads_q), wo[...]).astype(BF)
     gives += [give(1, give_in, wqkv_o), give(2, give_out, wo_o)]
     gives += [give(3, wg.at[:, his], wg_o), give(4, wu.at[:, his], wu_o), give(5, wd.at[his], wd_o)]
     for g in gives[1:]:
         g.start()
     sign = jnp.where(lax.broadcasted_iota(jnp.int32, (32, LANE), 1) < LANE // 2, -1.0, 1.0)
+    cf, sf = tables[2], tables[3]
     for a in range(LENGTH // 32):
-        ca, sa = cc[a : a + 1, :], sc[a : a + 1, :]
-        cos_o[a * 32 : a * 32 + 32, :] = ca * cf[...] - sa * sf[...]
-        sin_o[a * 32 : a * 32 + 32, :] = (sa * cf[...] + ca * sf[...]) * sign
+        ca, sa = tables[0, a : a + 1, :], tables[1, a : a + 1, :]
+        cos_o[a * 32 : a * 32 + 32, :] = ca * cf - sa * sf
+        sin_o[a * 32 : a * 32 + 32, :] = (sa * cf + ca * sf) * sign
     for c in keep:
         c.wait()
     for n in range(3):
@@ -350,7 +579,6 @@
     tokens, width = x.shape
     f_half = wg.shape[1] // 2
     cols = 4 * LANE
-    tables = [jnp.asarray(t) for t in angle_tables()]
     outs = [
         sds((2, 4, tokens, width), BF),
         sds((4, 4 * tokens, LANE), BF),
@@ -369,12 +597,16 @@
         pltpu.VMEM((2, 1, width), F32),
         pltpu.VMEM((width, cols), BF),
         pltpu.VMEM((2 * LANE, width), BF),
+        pltpu.VMEM(wq.shape, BF),
+        pltpu.VMEM(wk.shape, BF),
+        pltpu.VMEM(wv.shape, BF),
+        pltpu.VMEM(wo.shape, BF),
         DMA((6,)),
         DMA((6,)),
-        DMA((4,)),
+        DMA((8,)),
     ] + GATHER_SEMS
-    ins = [ANY, VM, VM, VM, VM, VM, ANY, ANY, ANY] + [VM] * 4
-    args = [x, gain, wq, wk, wv, wo, wg, wu, wd] + tables
+    ins = [ANY, VM] + [ANY] * 7 + [VM]
+    args = [x, gain, wq, wk, wv, wo, wg, wu, wd, jnp.asarray(np.stack(angle_tables()))]
     return call(project_kernel, 0, outs, ins, args, scratch, 3e10)
 
 
@@ -466,7 +698,9 @@
     )
 
 
-def expand_kernel(nf, all_dy, wg, wu, wd, all_f, middle, d_gate, d_up, *sems):
+def expand_kernel(
+    nf, all_dy, wg, wu, wd, all_f, middle, d_gate, d_up, part, grad, give, gsend, grecv, *sems
+):
     r, k, rx, ry, r3 = place()
     greet(rx, ry, k)
     gather = Gather(nf, all_f, sems)
@@ -475,45 +709,131 @@
     def compute(i, row, half):
         at = rows_of(half)
         f0, f1 = all_f[0, row, at, :], all_f[1, row, at, :]
+        dy0, dy1 = all_dy[0, row, at, :], all_dy[1, row, at, :]
         gate = nn(f0, wg[0]) + nn(f1, wg[1])
         upper = nn(f0, wu[0]) + nn(f1, wu[1])
-        d_mid = nt(all_dy[0, row, at, :], wd[0]) + nt(all_dy[1, row, at, :], wd[1])
+        d_mid = nt(dy0, wd[0]) + nt(dy1, wd[1])
         sig = 1.0 / (1.0 + jnp.exp(-gate))
         swish = gate * sig
-        middle[row, at, :] = (swish * upper).astype(BF)
+        mid = (swish * upper).astype(BF)
+        middle[row, at, :] = mid
         d_gate[row, at, :] = (d_mid * upper * sig * (1.0 + gate * (1.0 - sig))).astype(BF)
         d_up[row, at, :] = (d_mid * swish).astype(BF)
+        g0, g1 = tn(mid, dy0), tn(mid, dy1)
+
+        @pl.when(i == 0)
+        def _():
+            grad[0] = g0
+            grad[1] = g1
+
+        @pl.when(i > 0)
+        def _():
+            grad[0] += g0
+            grad[1] += g1
 
     gather.run(compute)
+    half = DOWN_CHUNKS // 4
+
+    def swap(j, core):
+        return remote(give.at[pl.ds(2 * j, 2)], part.at[pl.ds(2 * (half * core + j), 2)], gsend.at[j], grecv.at[j], {"col": 1 - k})
+
+    for j in range(half):
+        for h in range(2):
+            give[2 * j + h] = grad[1 - k, j * TALL + h * CHUNK : j * TALL + (h + 1) * CHUNK, :].astype(BF)
+        swap(j, k).start()
+    for j in range(half):
+        for h in range(2):
+            rows = slice(j * TALL + h * CHUNK, j * TALL + (h + 1) * CHUNK)
+            part[2 * (half * k + j) + h] = grad[k, rows, :].astype(BF)
+    for j in range(half):
+        swap(j, 1 - k).wait_recv()
+    for j in range(half):
+        swap(j, k).wait_send()
 
 
 def expand(nf, all_dy, wg, wu, wd):
     tokens, width = nf.shape
     f_half = wg.shape[2]
     outs = [sds((2, 4, tokens, width), BF)] + [sds((4, tokens, f_half), BF)] * 3
-    return call(
-        expand_kernel, 2, outs, [ANY] + [VM] * 4, [nf, all_dy, wg, wu, wd], list(GATHER_SEMS), 3e10
-    )
+    outs += [sds((DOWN_CHUNKS, CHUNK, WIDE), BF)]
+    half = DOWN_CHUNKS // 4
+    scratch = [pltpu.VMEM((2, f_half, width), F32), pltpu.VMEM((2 * half, CHUNK, WIDE), BF), DMA((half,)), DMA((half,))]
+    args = [nf, all_dy, wg, wu, wd]
+    return call(expand_kernel, 2, outs, [ANY] + [VM] * 4, args, scratch + GATHER_SEMS, 3e10)
+
+
+TICKS = 35
+
+
+def flat(ref, h, m=None):
+    got = ref[h] if m is None else ref[h, :, :, pl.ds(pl.multiple_of(m * 256, 256), 256)]
+    return got.reshape(-1, got.shape[-1])
 
 
 def contract_kernel(
-    d_gate, d_up, wg, wu, hidden, rstd2, gain, dy,
-    d_hidden, dya, part,
-    stat, ssem, *rest,
+    d_gate, d_up, wg, wu, hidden, rstd2, gain, dy, wo, attn, part_d, f_any,
+    d_hidden, gains_o, part, part_o, d_attn, totals, acc_c, tot_c,
+    stat, ssem, give, gsend, grecv, gathered, dya, grad, give_o, his_o, gsem, fsem, *rest,
 ):
     r, k, rx, ry, r3 = place()
     width = hidden.shape[1]
-    greet(rx, ry, k)
-    total = Sum(rest)
+    fetch = pltpu.make_async_copy(f_any, gathered, fsem)
+    fetch.start()
+    greet(rx, ry, k, True)
+    total = Sum(rest[:9])
+    gather = Gather(dya, gathered, rest[9:14])
+    parts = [(0, DOWN_CHUNKS, part_d), (DOWN_CHUNKS, MLP_CHUNKS, part), (MLP_CHUNKS, OUT_CHUNKS, part_o)]
+    line = Line(parts, totals, (acc_c, tot_c), rest[14:], 0, TICKS)
+    line.open()
 
     def compute(row, half):
         at = rows_of(half)
         g, u = d_gate[row, at, :], d_up[row, at, :]
         return nt(g, wg[k]) + nt(u, wu[k]), nt(g, wg[1 - k]) + nt(u, wu[1 - k])
 
-    total.send_all(compute)
+    def early(j):
+        @pl.when(j % 2 == 1)
+        def _():
+            line.step(j // 2)
+
+    total.send_all(compute, early)
+
+    def swap(e, core):
+        to = part.at[pl.ds(2 * (e // 4 * 8 + 4 * core + e % 4), 2)]
+        return remote(give.at[pl.ds(2 * e, 2)], to, gsend.at[e], grecv.at[e], {"col": 1 - k})
+
+    def wide_part(h, right, dst, first):
+        def one(m, carry):
+            got = tn(flat(gathered, h, m), right[...].reshape(-1, right.shape[2])).astype(BF)
+            for b in range(2):
+                lanes = pl.ds(pl.multiple_of((2 * m + b) * TALL, TALL), TALL)
+                for j in range(4):
+                    for u in range(2):
+                        rows = slice(b * TALL + u * CHUNK, b * TALL + (u + 1) * CHUNK)
+                        dst[2 * (first + j) + u, :, lanes] = got[rows, j * TALL : (j + 1) * TALL]
+            return carry
+
+        lax.fori_loop(0, width // 256, one, 0)
+
+    fetch.wait()
+    wide_part(1 - k, d_gate, give, 0)
+    for e in range(4):
+        swap(e, k).start()
+    line.step(4)
+    wide_part(k, d_gate, part, 4 * k)
+    line.step(5)
+    wide_part(1 - k, d_up, give, 4)
+    for e in range(4, 8):
+        swap(e, k).start()
+    line.step(6)
+    wide_part(k, d_up, part, 8 + 4 * k)
+    line.step(7)
     total.relay(4)
     total.relay(5)
+    for e in range(8):
+        swap(e, 1 - k).wait_recv()
+    for j in range(8, 13):
+        line.step(j)
     gains = jnp.zeros((1, width), F32)
     for half in range(2):
         at = rows_of(half)
@@ -523,59 +843,127 @@
         scaled = d_nf * gain[...]
         d_hidden[at, :] = scaled
         stat[k, at, :] = jnp.broadcast_to(jnp.sum(scaled * h, 1, keepdims=True), (PIECE, LANE))
-    part[...] = gains
+    gains_o[...] = gains
     inner = exchange(k, stat, ssem) / (2 * width)
     rs = rstd2[:, 0:1]
     value = dy[...].astype(F32) + rs * d_hidden[...] - hidden[...] * (rs * rs * rs * inner)
     d_hidden[...] = value
     dya[...] = value.astype(BF)
+    gather.start()
+
+    def piece(i, row, half):
+        at = rows_of(half)
+        d0, d1 = gathered[0, row, at, :], gathered[1, row, at, :]
+        d_attn[row, at, :] = (nt(d0, wo[0]) + nt(d1, wo[1])).astype(BF)
+        a = attn[row, at, :]
+        g0, g1 = tn(a, d0), tn(a, d1)
+
+        @pl.when(i == 0)
+        def _():
+            grad[0] = g0
+            grad[1] = g1
+
+        @pl.when(i > 0)
+        def _():
+            grad[0] += g0
+            grad[1] += g1
+
+    def before(q):
+        @pl.when(q == 0)
+        def _():
+            for j in range(13, 15):
+                line.step(j)
+
+        for j in range(3):
+            line.step(15 + 4 * q + j)
+
+    def after(q):
+        line.step(18 + 4 * q)
+
+    gather.run(piece, before, after)
+    give_o[...] = grad[1 - k].astype(BF)
+    give_out = remote(give_o, his_o, gsem.at[0], gsem.at[1], {"col": 1 - k})
+    give_out.start()
+    q_cols = part_o.shape[0] * CHUNK
+    mine = nn(spread(q_cols, 2 * LANE, k * (q_cols // 2)), grad[k].astype(BF))
+    give_out.wait_recv()
+    out = mine + nn(spread(q_cols, 2 * LANE, (1 - k) * (q_cols // 2)), his_o[...])
+    for c in range(q_cols // CHUNK):
+        part_o[c] = out[c * CHUNK : (c + 1) * CHUNK].astype(BF)
+    line.rest(31)
+    for e in range(8):
+        swap(e, k).wait_send()
+    give_out.wait_send()
     total.finish()
 
 
-def contract(d_gate, d_up, wg, wu, hidden, rstd2, gain, dy):
+def contract(d_gate, d_up, wg, wu, hidden, rstd2, gain, dy, wo, attn, part_d, all_f):
     tokens, width = hidden.shape
-    outs = [sds((tokens, width), F32), sds((tokens, width), BF), sds((1, width), F32)]
-    scratch = [pltpu.VMEM((2, tokens, LANE), F32), DMA((2,))] + sum_scratch(width)
-    args = [d_gate, d_up, wg, wu, hidden, rstd2, gain, dy]
-    return call(contract_kernel, 3, outs, [VM] * 8, args, scratch, 3e10)
-
-
-def unproject_kernel(dya, wo, all_dya, d_attn, *sems):
-    r, k, rx, ry, r3 = place()
-    greet(rx, ry, k)
-    gather = Gather(dya, all_dya, sems)
-    gather.start()
-
-    def compute(i, row, half):
-        at = rows_of(half)
-        got = nt(all_dya[0, row, at, :], wo[0]) + nt(all_dya[1, row, at, :], wo[1])
-        d_attn[row, at, :] = got.astype(BF)
-
-    gather.run(compute)
-
-
-def unproject(dya, wo):
-    tokens, width = dya.shape
-    outs = [sds((2, 4, tokens, width), BF), sds((4, tokens, 2 * LANE), BF)]
-    return call(unproject_kernel, 4, outs, [ANY, VM], [dya, wo], list(GATHER_SEMS), 3e10)
+    n = lax.axis_size("dp")
+    outs = [sds((tokens, width), F32), sds((1, width), F32)]
+    outs += [sds((MLP_CHUNKS - DOWN_CHUNKS, CHUNK, WIDE), BF), sds((OUT_CHUNKS - MLP_CHUNKS, CHUNK, WIDE), BF)]
+    outs += [sds((4, tokens, 2 * LANE), BF)] + line_outs(TICKS)
+    out_specs = [VM] * 5 + [ANY] + [VM] * 2
+    scratch = [pltpu.VMEM((2, tokens, LANE), F32), DMA((2,))]
+    scratch += [pltpu.VMEM((16, CHUNK, WIDE), BF), DMA((8,)), DMA((8,))]
+    scratch += [pltpu.VMEM((2, 4, tokens, width), BF), pltpu.VMEM((tokens, width), BF)]
+    scratch += [pltpu.VMEM((2, 2 * LANE, width), F32)] + [pltpu.VMEM((2 * LANE, width), BF)] * 2
+    scratch += [DMA((2,)), DMA]
+    scratch += sum_scratch(width) + GATHER_SEMS + line_scratch(n, TICKS)
+    args = [d_gate, d_up, wg, wu, hidden, rstd2, gain, dy, wo, attn, part_d, all_f]
+    ins = [VM] * 11 + [ANY]
+    return call(contract_kernel, 3, outs, ins, args, scratch, 5e10, vmem_limit(n), out_specs)
+
+
+def vmem_limit(n):
+    return 60 if n <= 4 else 63
+
+
+def columns(rows, cols, core, q_cols, k_cols):
+    i = lax.broadcasted_iota(jnp.int32, (rows, cols), 0)
+    at = lax.broadcasted_iota(jnp.int32, (rows, cols), 1)
+    part, lane = i // LANE, i % LANE
+    index = jnp.where(lane < HALF, lane, lane - (LANE // 2 - HALF))
+    q = core * (q_cols // 2) + part * HD
+    kv = q_cols + (part - 2) * k_cols + core * (k_cols // 2)
+    to = jnp.where(part < 2, q, kv) + index
+    pad = lane % (LANE // 2) >= HALF
+    return jnp.where((at == to) & (pad == False), 1.0, 0.0).astype(BF)
 
 
 def backward_kernel(
-    qkv, kvt, lse, d_attn, cos, sin, wqkv, middle, wd, hidden, x, rstd1, d_hidden, gain,
-    d_proj, output, grad_x, part,
-    dk, dv, stat, ssem, *rest,
+    q_cols, k_cols,
+    qkv, kvt, lse, d_attn, cos, sin, middle, wd, hidden, wqkv, x, rstd1, d_hidden, gain, gains_f,
+    part_m, part_o, acc_c, tot_c, normed_any,
+    output, grad_x, gains_o, totals,
+    dk, dv, d_proj, normed, part, mine, give, his, gsem, stat, ssem, free, fsem,
+    mine_g, pair_g, slots, gsend, grecv, *rest,
 ):
     r, k, rx, ry, r3 = place()
     width = x.shape[1]
-    greet(rx, ry, k)
-    down = Sum(rest[:9])
-    into = Sum(rest[9:])
+    n = lax.axis_size("dp")
+    z = lax.axis_index("dp")
+    fetch = pltpu.make_async_copy(normed_any, normed, fsem)
+    fetch.start()
+    greet(rx, ry, k, True, True)
+    sums = rest[:5]
+    down = Sum(sums + rest[5:9])
+    into = Sum(sums + rest[9:13])
+    ticks = line_ticks(n) - TICKS
+    parts = [(DOWN_CHUNKS, MLP_CHUNKS, part_m), (MLP_CHUNKS, OUT_CHUNKS, part_o), (OUT_CHUNKS, ALL_CHUNKS, part)]
+    line = Line(parts, totals, None, rest[13:], TICKS, ticks, (acc_c, tot_c))
+    line.open()
 
     def down_piece(row, half):
         m = middle[row, rows_of(half), :]
         return nn(m, wd[k]), nn(m, wd[1 - k])
 
-    down.send_all(down_piece)
+    def early(j):
+        @pl.when(j % 3 == 1)
+        def _():
+            line.step(j // 3)
+
+    down.send_all(down_piece, early)
 
     def unrotate(u, p):
         at = pl.ds(p * PIECE, PIECE)
@@ -604,6 +992,12 @@
                 dk[0:span, :] += nn(ds, q)
                 dq = nn(kvt[0, :, pl.ds(base, span)], ds).T * SCALE
                 d_proj[out, lane] = unrotate(dq, p).astype(BF)
+                tick = 3 + seq * 8 + head * 4 + p
+
+                @pl.when(tick < OUT_CHUNKS - LAG - TICKS)
+                def _(tick=tick):
+                    line.step(tick)
+
             return carry
 
         dk[...] = jnp.zeros_like(dk)
@@ -615,10 +1009,10 @@
             d_proj[out, 2 * LANE : 3 * LANE] = unrotate(dk[at, :] * SCALE, p).astype(BF)
             d_proj[out, 3 * LANE : 4 * LANE] = dv[at, :].astype(BF)
 
-    def both(n, carry):
-        sequence(jnp.where(n == 0, ry // 2, r // 2))
-
-        @pl.when(n == 0)
+    def both(seq, carry):
+        sequence(seq)
+
+        @pl.when(seq == 0)
         def _():
             down.relay(4)
             down.relay(5)
@@ -626,17 +1020,50 @@
         return carry
 
     lax.fori_loop(0, 2, both, 0)
+    for half in range(2):
+        at = rows_of(half)
+        output[at, :] = hidden[at, :] + down.last(6 + half)
+    down.finish()
+    for device in ({"row": rx}, {"row": ry}, {"col": 1 - k}):
+        pl.semaphore_signal(free, inc=1, device_id=device, device_id_type=MESH)
+    pl.semaphore_wait(free, 3)
+
+    fetch.wait()
+
+    def in_part(h, dst):
+        def one(m, carry):
+            dst[pl.ds(pl.multiple_of(m * 256, 256), 256), :] = tn(flat(normed, h, m), d_proj[...]).astype(BF)
+            return carry
+
+        lax.fori_loop(0, width // 256, one, 0)
+
+    in_part(1 - k, give)
+    swap = remote(give, his, gsem.at[0], gsem.at[1], {"col": 1 - k})
+    swap.start()
+    in_part(k, mine)
+    cols = q_cols + 2 * k_cols
+    got = nn(mine[...], columns(4 * LANE, cols, k, q_cols, k_cols))
+    swap.wait_recv()
+    got = got + nn(his[...], columns(4 * LANE, cols, 1 - k, q_cols, k_cols))
+    for c in range(width // CHUNK):
+        part[c] = got[c * CHUNK : (c + 1) * CHUNK].astype(BF)
 
     def into_piece(row, half):
         d = d_proj[pl.ds(pl.multiple_of(row * 2 * PIECE + half * PIECE, PIECE), PIECE), :]
         return nt(d, wqkv[k]), nt(d, wqkv[1 - k])
 
-    into.send_all(into_piece)
-    for half in range(2):
-        at = rows_of(half)
-        output[at, :] = hidden[at, :] + down.last(6 + half)
+    def beside(j):
+        @pl.when(j % 2 == 1)
+        def _():
+            line.step(17 + j // 2)
+
+    into.send_all(into_piece, beside)
+    for j in range(21, 24):
+        line.step(j)
     into.relay(4)
     into.relay(5)
+    for j in range(24, 29):
+        line.step(j)
     gains = jnp.zeros((1, width), F32)
     for half in range(2):
         at = rows_of(half)
@@ -646,174 +1073,183 @@
         scaled = d_na * gain[...]
         grad_x[at, :] = scaled
         stat[k, at, :] = jnp.broadcast_to(jnp.sum(scaled * xs, 1, keepdims=True), (PIECE, LANE))
-    part[...] = gains
+
+    def row_total(step, device):
+        copy = remote(mine_g.at[step], pair_g.at[step], gsend.at[n + step], grecv.at[n + step], {"row": device})
+        copy.start()
+        return copy
+
+    mine_g[0, 0:1] = gains
+    mine_g[0, 1:2] = gains_f[...]
+    over_x = row_total(0, rx)
     inner = exchange(k, stat, ssem) / (2 * width)
     rs = rstd1[:, 0:1]
+    over_x.wait_recv()
+    mine_g[1] = mine_g[0] + pair_g[0]
+    over_y = row_total(1, ry)
     grad_x[...] = d_hidden[...] + rs * grad_x[...] - x[...].astype(F32) * (rs * rs * rs * inner)
-    down.finish()
+    over_y.wait_recv()
+    slots[z] = mine_g[1] + pair_g[1]
+
+    def over_dp(t, mine):
+        other = (z + t) % n
+        g = z if mine else other
+        return remote(slots.at[g], slots.at[g], gsend.at[t], grecv.at[g], {"dp": other})
+
+    def start(t, carry):
+        over_dp(t, True).start()
+        return carry
+
+    lax.fori_loop(1, n, start, 0)
+    line.rest(29)
+
+    def wait(t, carry):
+        over_dp(t, False).wait_recv()
+        over_dp(t, True).wait_send()
+        return carry
+
+    lax.fori_loop(1, n, wait, 0)
+    gains_o[...] = lax.fori_loop(1, n, lambda g, total: total + slots[g], slots[0])
+    over_x.wait_send()
+    over_y.wait_send()
+    swap.wait_send()
     into.finish()
 
 
-def backward(qkv, kvt, lse, d_attn, cos, sin, wqkv, middle, wd, hidden, x, rstd1, d_hidden, gain):
+def backward(
+    qkv, kvt, lse, d_attn, cos, sin, middle, wd, hidden, wqkv, x, rstd1, d_hidden, gain, gains_f,
+    part_m, part_o, acc, tot, normed, q_cols, k_cols,
+):
     tokens, width = x.shape
-    outs = [
-        sds((4 * tokens, 4 * LANE), BF),
-        sds((tokens, width), F32),
-        sds((tokens, width), F32),
-        sds((1, width), F32),
-    ]
-    scratch = (
-        [pltpu.VMEM((LENGTH, LANE), F32)] * 2
-        + [pltpu.VMEM((2, tokens, LANE), F32), DMA((2,))]
-        + sum_scratch(width)
-        + sum_scratch(width)
-    )
-    args = [qkv, kvt, lse, d_attn, cos, sin, wqkv, middle, wd, hidden, x, rstd1, d_hidden, gain]
-    return call(backward_kernel, 5, outs, [VM] * len(args), args, scratch, 5e10)
-
-
-def gains_kernel(groups, a, f, out, slots, send, recv):
-    dp, r = lax.axis_index("dp"), lax.axis_index("row")
-    me = dp * 4 + r
-
-    def peer(t):
-        other = (me + t) % groups
-        return other, {"dp": other // 4, "row": other % 4}
-
-    bar = pltpu.get_barrier_semaphore()
-
-    def hello(t, carry):
-        pl.semaphore_signal(bar, inc=1, device_id=peer(t)[1], device_id_type=MESH)
-        return carry
-
-    lax.fori_loop(1, groups, hello, 0)
-    slots[me, 0:1, :] = a[...]
-    slots[me, 1:2, :] = f[...]
-    pl.semaphore_wait(bar, groups - 1)
-
-    def start(t, carry):
-        remote(slots.at[me], slots.at[me], send.at[t], recv.at[me], peer(t)[1]).start()
-        return carry
-
-    lax.fori_loop(1, groups, start, 0)
-
-    def wait(t, carry):
-        other, device = peer(t)
-        remote(slots.at[me], slots.at[other], send.at[t], recv.at[other], device).wait_recv()
-        remote(slots.at[me], slots.at[me], send.at[t], recv.at[me], device).wait_send()
-        return carry
-
-    lax.fori_loop(1, groups, wait, 0)
-    out[...] = lax.fori_loop(1, groups, lambda g, total: total + slots[g], slots[0])
-
-
-def gains_total(a, f, groups):
-    import functools
-
-    outs = [sds((2, a.shape[1]), F32)]
-    scratch = [pltpu.VMEM((groups, 2, a.shape[1]), F32), DMA((groups,)), DMA((groups,))]
-    return call(
-        functools.partial(gains_kernel, groups), 6, outs, [VM] * 2, [a, f], scratch, 1e6, vmem=8
-    )[0]
-
-
-def dp_total(part):
     n = lax.axis_size("dp")
-    z = lax.axis_index("dp")
+    ticks = line_ticks(n) - TICKS
+    outs = [sds((tokens, width), F32)] * 2 + [sds((2, width), F32), sds((ticks, CHUNK, WIDE), BF)]
+    scratch = [pltpu.VMEM((LENGTH, LANE), F32)] * 2 + [pltpu.VMEM((4 * tokens, 4 * LANE), BF)]
+    scratch += [pltpu.VMEM((2, 4, tokens, width), BF), pltpu.VMEM((ALL_CHUNKS - OUT_CHUNKS, CHUNK, WIDE), BF)]
+    scratch += [pltpu.VMEM((width, 4 * LANE), BF)] * 3 + [DMA((2,))]
+    scratch += [pltpu.VMEM((2, tokens, LANE), F32), DMA((2,)), pltpu.SemaphoreType.REGULAR, DMA]
+    scratch += [pltpu.VMEM((2, 2, width), F32)] * 2 + [pltpu.VMEM((n, 2, width), F32)]
+    scratch += [DMA((n + 2,)), DMA((n + 2,))]
+    both = sum_scratch(width)
+    scratch += both + both[5:] + line_scratch(n, ticks)
+    args = [qkv, kvt, lse, d_attn, cos, sin, middle, wd, hidden, wqkv, x, rstd1, d_hidden, gain, gains_f]
+    args += [part_m, part_o, acc, tot, normed]
+    kernel = functools.partial(backward_kernel, q_cols, k_cols)
+    ins = [VM] * (len(args) - 1) + [ANY]
+    return call(kernel, 5, outs, ins, args, scratch, 5e10, vmem_limit(n), [VM] * 3 + [ANY])
+
+
+def unpack_kernel(ticks, q_cols, k_cols, *rest):
+    tots, (down, gate, up, out, q_o, k_o, v_o), rest = rest[: len(ticks)], rest[len(ticks) : len(ticks) + 7], rest[len(ticks) + 7 :]
+    chunks, wide, parts, isem, osem = rest
+    n, s, _, _ = line_place()
     mid = n // 2
-
-    def add(a, b):
-        return (a.astype(F32) + b.astype(F32)).astype(BF)
-
-    for s in range(mid - 1):
-        part = add(part, lax.ppermute(part, "dp", [(s, s + 1), (n - 1 - s, n - 2 - s)]))
-    part = add(part, lax.ppermute(part, "dp", [(mid - 1, mid), (mid, mid - 1)]))
-    for s in reversed(range(mid - 1)):
-        got = lax.ppermute(part, "dp", [(s + 1, s), (n - 2 - s, n - 1 - s)])
-        part = jnp.where((z == s) | (z == n - 1 - s), got, part)
-    return part
-
-
-def swap(both, k):
-    mine = lax.dynamic_index_in_dim(both, k, 0, False)
-    his = lax.dynamic_index_in_dim(both, 1 - k, 0, False)
-    return mine, lax.ppermute(his, "col", [(0, 1), (1, 0)])
-
-
-def weight_grad(left, right):
-    return lax.dot_general(left, right, (((0,), (0,)), ((), ())), preferred_element_type=F32).astype(BF)
-
-
-def side_by_side(mine, his, k, axis):
-    first = jnp.where(k == 0, mine, his)
-    second = jnp.where(k == 0, his, mine)
-    return jnp.concatenate([first, second], axis)
+    off = LAG * (2 * mid - 2 - s)
+    offs = [LAG * o for o in range(mid - 1, 2 * mid - 1)]
+
+    def source(t):
+        for tot, count in zip(tots, ticks):
+            if t < count:
+                return tot.at[t]
+            t -= count
+
+    def load(c):
+        for o in offs:
+
+            @pl.when(off == o)
+            def _(o=o):
+                for u in range(2):
+                    dst = chunks.at[c % 4, pl.ds(u * CHUNK, CHUNK)]
+                    pltpu.make_async_copy(source(2 * c + u + o), dst, isem.at[c % 4, u]).start()
+
+    def stored(c):
+        slot = c % 4
+        buf = wide.at[slot]
+        if c < 8:
+            return [pltpu.make_async_copy(buf, down.at[pl.ds(c * TALL, TALL)], osem.at[slot, 0])]
+        if c < MLP_CHUNKS // 2:
+            to, lanes = (gate, up)[c // 8 - 1], pl.ds(c % 8 * TALL, TALL)
+            return [
+                pltpu.make_async_copy(
+                    buf.at[:, pl.ds(b * TALL, TALL)], to.at[pl.ds(b * TALL, TALL), lanes], osem.at[slot, b]
+                )
+                for b in range(WIDE // TALL)
+            ]
+        if c < OUT_CHUNKS // 2:
+            return [pltpu.make_async_copy(buf, out.at[pl.ds((c - MLP_CHUNKS // 2) * TALL, TALL)], osem.at[slot, 0])]
+        rows = pl.ds((c - OUT_CHUNKS // 2) * TALL, TALL)
+        return [
+            pltpu.make_async_copy(buf.at[:, pl.ds(0, q_cols)], q_o.at[rows], osem.at[slot, 0]),
+            pltpu.make_async_copy(parts.at[0, slot], k_o.at[:, rows], osem.at[slot, 1]),
+            pltpu.make_async_copy(parts.at[1, slot], v_o.at[:, rows], osem.at[slot, 2]),
+        ]
+
+    for c in range(3):
+        load(c)
+    for c in range(ALL_CHUNKS // 2):
+        if c + 3 < ALL_CHUNKS // 2:
+            load(c + 3)
+        if c >= 4:
+            for copy in stored(c - 4):
+                copy.wait()
+        for u in range(2):
+            dst = chunks.at[c % 4, pl.ds(u * CHUNK, CHUNK)]
+            pltpu.make_async_copy(dst, dst, isem.at[c % 4, u]).wait()
+        value = chunks[c % 4].astype(F32)
+        wide[c % 4] = value
+        if c >= OUT_CHUNKS // 2:
+            parts[0, c % 4] = value[:, q_cols : q_cols + k_cols].T
+            parts[1, c % 4] = value[:, q_cols + k_cols :].T
+        for copy in stored(c):
+            copy.start()
+    for c in range(ALL_CHUNKS // 2 - 4, ALL_CHUNKS // 2):
+        for copy in stored(c):
+            copy.wait()
+
+
+def unpack(tots, q_cols, k_cols):
+    n = lax.axis_size("dp")
+    ticks = [TICKS, line_ticks(n) - TICKS]
+    outs = [sds((8 * TALL, WIDE), F32), sds((WIDE, 8 * TALL), F32), sds((WIDE, 8 * TALL), F32)]
+    outs += [sds((q_cols, WIDE), F32), sds((WIDE, q_cols), F32), sds((k_cols, WIDE), F32), sds((k_cols, WIDE), F32)]
+    moved = 6 * ALL_CHUNKS // 2 * TALL * WIDE
+    return pl.pallas_call(
+        functools.partial(unpack_kernel, ticks, q_cols, k_cols),
+        out_shape=outs,
+        in_specs=[ANY] * len(tots),
+        out_specs=[ANY] * len(outs),
+        scratch_shapes=[
+            pltpu.VMEM((4, TALL, WIDE), BF),
+            pltpu.VMEM((4, TALL, WIDE), F32),
+            pltpu.VMEM((2, 4, k_cols, TALL), F32),
+            DMA((4, 2)),
+            DMA((4, WIDE // TALL)),
+        ],
+        compiler_params=pltpu.CompilerParams(vmem_limit_bytes=16 << 20),
+        cost_estimate=pl.CostEstimate(flops=0, bytes_accessed=moved, transcendentals=0),
+    )(*tots)
 
 
 def on_device(
     layer_input, gain_attn, gain_ffn, w_query, w_key, w_value, w_out, w_gate, w_up, w_down, cotangent
 ):
-    k = lax.axis_index("col")
     tokens, width = layer_input.shape
     q_cols, k_cols = w_query.shape[1], w_key.shape[1]
     gain_a, gain_f = gain_attn[None], gain_ffn[None]
     normed, qkv, kvt, wqkv, wo, wg, wu, wd, cos, sin, rstd1 = project(
-        layer_input, gain_a, w_query, w_key, w_value, w_out, w_gate, w_up, w_down
+        layer_input, gain_a, w_query, w_key.T, w_value.T, w_out, w_gate, w_up, w_down
     )
     attn, lse, hidden, nf, rstd2, all_dy = attend(qkv, kvt, wo, layer_input, gain_f, cotangent)
-    all_f, middle, d_gate, d_up = expand(nf, all_dy, wg, wu, wd)
-
-    def flat(a):
-        return a.reshape(4 * tokens, a.shape[-1])
-
-    def grads_of(gathered, right):
-        return jnp.stack([weight_grad(flat(gathered[h]), flat(right)) for h in range(2)])
-
-    mid = flat(middle)
-    g_down = jnp.stack([weight_grad(mid, flat(all_dy[h])) for h in range(2)])
-    down = dp_total(side_by_side(*swap(g_down, k), k, 0))
-    gate = dp_total(side_by_side(*swap(grads_of(all_f, d_gate), k), k, 1))
-    up = dp_total(side_by_side(*swap(grads_of(all_f, d_up), k), k, 1))
-
-    d_hidden, dya, part_f = contract(d_gate, d_up, wg, wu, hidden, rstd2, gain_f, cotangent)
-    all_dya, d_attn = unproject(dya, wo)
-    g_out = jnp.stack([weight_grad(flat(attn), flat(all_dya[h])) for h in range(2)])
-    d_proj, output, grad_x, part_a = backward(
-        qkv, kvt, lse, d_attn, cos, sin, wqkv, middle, wd, hidden, layer_input, rstd1, d_hidden, gain_a
+    all_f, middle, d_gate, d_up, part_d = expand(nf, all_dy, wg, wu, wd)
+    d_hidden, gains_f, part_m, part_o, d_attn, tot1, acc, tot = contract(
+        d_gate, d_up, wg, wu, hidden, rstd2, gain_f, cotangent, wo, attn, part_d, all_f
     )
-    gains = gains_total(part_a, part_f, lax.axis_size("dp") * 4)
-
-    mine, his = swap(g_out, k)
-    n = 2 * LANE
-    out = nn(spread(q_cols, n, k * q_cols // 2), mine) + nn(
-        spread(q_cols, n, (1 - k) * q_cols // 2), his
+    output, grad_x, gains, tot2 = backward(
+        qkv, kvt, lse, d_attn, cos, sin, middle, wd, hidden, wqkv, layer_input, rstd1, d_hidden,
+        gain_a, gains_f, part_m, part_o, acc, tot, normed, q_cols, k_cols,
     )
-    mine, his = swap(grads_of(normed, d_proj), k)
-
-    def columns(core):
-        part = [
-            jnp.pad(spread_t(n, q_cols, core * q_cols // 2), ((0, 0), (0, 2 * k_cols))),
-            jnp.pad(spread_t(LANE, k_cols, core * k_cols // 2), ((0, 0), (q_cols, k_cols))),
-            jnp.pad(spread_t(LANE, k_cols, core * k_cols // 2), ((0, 0), (q_cols + k_cols, 0))),
-        ]
-        return jnp.concatenate(part, 0)
-
-    into = nn(mine, columns(k)) + nn(his, columns(1 - k))
-    last = dp_total(jnp.concatenate([out.astype(BF), into.astype(BF)], 0))
-    out, into = last[:q_cols].astype(F32), last[q_cols:].astype(F32)
-    return (
-        output,
-        grad_x,
-        gains[0],
-        gains[1],
-        into[:, :q_cols],
-        into[:, q_cols : q_cols + k_cols],
-        into[:, q_cols + k_cols :],
-        out,
-        gate.astype(F32),
-        up.astype(F32),
-        down.astype(F32),
-    )
+    down, gate, up, out, g_q, g_k, g_v = unpack([tot1, tot2], q_cols, k_cols)
+    return output, grad_x, gains[0], gains[1], g_q, g_k.T, g_v.T, out, gate, up, down
 
 
 def solution(mesh):

time: 687 us -> 398 us (0.58)
  waiting for transfers between devices: 125 us -> 0 us
  other arithmetic: 39.8 us -> 0 us
  Pallas kernels: 405 us -> 367 us
  matrix products: 36 us -> 0 us
  local copies, waits for them, and re-layouts: 51.9 us -> 25 us
  starting transfers between devices: 18.1 us -> 0 us
    ppermute x17 -> x0, waiting for transfers between devices: 125 us -> none  [the longest x4 125 us: dp_total(): lax.ppermute(part, 'dp', [(s, s + 1), (n - 1 - s, n - 2 - s)])]
    pallas_call x7 -> x6, Pallas kernels: 405 us -> 367 us  [the longest x5 355 us: call(): pl.pallas_call(kernel, out_shape=outs, in_specs=ins, out_specs=out_specs...]
    dot_general x14 -> x0, matrix products: 36 us -> none  [the longest x10 26.4 us: weight_grad(): lax.dot_general(left, right, (((0,), (0,)), ((), ())), preferred_element_...]
    convert_element_type x15 -> x0, other arithmetic: 22 us -> none  [the longest x8 8.97 us: add(): return (a.astype(F32) + b.astype(F32)).astype(BF)]
    ppermute x17 -> x0, starting transfers between devices: 18.1 us -> none  [the longest x4 8.03 us: dp_total(): lax.ppermute(part, 'dp', [(s, s + 1), (n - 1 - s, n - 2 - s)])]
    slice x6 -> x0, local copies, waits for them, and re-layouts: 12.2 us -> none  [the longest x1 5.51 us: on_device(): g_down = jnp.stack([weight_grad(mid, flat(all_dy[h])) for h in range(2)])]
    dynamic_slice x4 -> x0, local copies, waits for them, and re-layouts: 8.13 us -> none  [the longest x2 4.6 us: swap(): mine = lax.dynamic_index_in_dim(both, k, 0, False)]
    unnamed x124 -> x60, local copies, waits for them, and re-layouts: 29.6 us -> 22.3 us
  transfers between devices with their start and end apart: 17 -> 0, of which waited for: 4 -> 0; matrix products, arithmetic and copies ran while one was open for 11% -> 0% of each run, Pallas kernels for 40% -> 0%
where the time goes in v2:
time: 398 us; the launch traced here: 393 us
  Pallas kernels  367 us (92%)
  local copies, waits for them, and re-layouts  25 us (6%)
    pallas_call x5, Pallas kernels, call(): pl.pallas_call(kernel, out_shape=outs, in_specs=ins, out_specs=out_specs...  355 us
    unnamed x60, local copies, waits for them, and re-layouts  22.3 us
    pallas_call x1, Pallas kernels, unpack(): pl.pallas_call(functools.partial(unpack_kernel, ticks, q_cols, k_cols), o...  11.3 us

profile of v2, /device:TPU:0, one launch (start us, length us, event | category | flops | bytes accessed | tf_op | source)
XLA Modules:
  0.0 392.7 jit_solution(4844425738907356428)
XLA Ops:
  0.6 0.7 broadcast_in_dim.6.gain
  1.3 0.7 broadcast_in_dim.7.gain
  2.0 0.0 copy-start.5
  2.0 1.1 copy-done.5
  3.2 0.0 copy-start.6
  3.2 1.1 copy-done.6
  4.2 1.1 copy-done.7
  5.3 1.0 copy-done.8
  6.3 1.0 copy-done.9
  7.2 0.8 copy-done.10
  8.1 37.3 %shard_map.203 = (bf16[2,4,512,768]{3,2,1,0:T(8,128)(2,1)}, bf16[4,2048,128]{2,1,0:T(8,128)(2,1)}, bf16[2,128,2048]{2,1,0:T(8,128)(2,1)S(1)}, bf16[2,768,512]{2,...) custom-call(bf16[512,768]{1,0:T(8,128)(2,1)S(1)} %copy-done.5, ...), custom_call_target="tpu_custom_call" | custom-call | flops 30000001024 | bytes 25168896 | tf_op jit(solution)/shard_map/pallas_call | solution.py:438
  45.4 0.0 copy-done.2
  45.4 0.0 copy-start.17
  45.4 1.1 copy-done.17
  46.6 0.8 copy-done.22
  47.3 0.8 copy-done.23
  48.1 0.7 copy-done.24
  48.8 0.0 copy-done.3
  48.8 0.0 copy-done.4
  48.8 0.0 copy-start.12
  48.9 2.8 copy-done.12
  51.7 59.2 %shard_map.204 = (bf16[4,512,256]{2,1,0:T(8,128)(2,1)S(1)}, f32[2,8,1,256]{3,2,1,0:T(1,128)S(1)}, f32[512,768]{1,0:T(8,128)S(1)}, bf16[512,768]{1,0:T(8,128)(2,1...) custom-call(bf16[4,2048,128]{2,1,0:T(8,128)(2,1)S(1)} %copy-done.12, ...), custom_call_target="tpu_custom_call" | custom-call | flops 30000001024 | bytes 15485952 | tf_op jit(solution)/shard_map/pallas_call | solution.py:438
  110.9 0.0 copy-done.19
  110.9 0.0 copy-done.21
  110.9 0.0 copy-start.18
  110.9 1.1 copy-done.18
  112.1 0.7 copy-done.25
  112.8 0.6 copy-done.26
  113.4 0.0 copy-done.14
  113.4 0.0 copy-done.13
  113.4 0.0 copy-done.15
  113.4 44.0 %shard_map.205 = (bf16[2,4,512,768]{3,2,1,0:T(8,128)(2,1)}, bf16[4,512,512]{2,1,0:T(8,128)(2,1)S(1)}, bf16[4,512,512]{2,1,0:T(8,128)(2,1)}, bf16[4,512,512]{2,1,0:T(8,128)(2,1)}, bf16[16,64,768]{2,1,0:T(8,128)(2,1)S(1)}) custom-call(bf16[512,768]{1,0:T(8,128)(2,1)S(1)} %get-tuple-element.56.nf, bf16[2,4,512,768]{3,2,1,0:T(8,128)(2,1)} %get-tuple-element.57.all_dy, ...), custom_call_target="tpu_custom_call" | custom-call | flops 30000001024 | bytes 25952256 | tf_op jit(solution)/shard_map/pallas_call | solution.py:438
  157.4 0.0 copy-done.20
  157.4 0.0 copy-start.11
  157.4 1.3 copy-done.11
  158.8 1.1 copy-done.16
  159.9 98.4 %shard_map.206 = (f32[512,768]{1,0:T(8,128)}, f32[1,768]{1,0:T(1,128)}, bf16[32,64,768]{2,1,0:T(8,128)(2,1)}, bf16[6,64,768]{2,1,0:T(8,128)(2,1)}, bf16[4,512,25...) custom-call(bf16[4,512,512]{2,1,0:T(8,128)(2,1)} %get-tuple-element.6, ...), custom_call_target="tpu_custom_call" | custom-call | flops 49999998976 | bytes 29857792 | tf_op jit(solution)/shard_map/pallas_call | solution.py:438
  258.3 0.0 copy-start
  258.3 116.3 %shard_map.207 = (f32[512,768]{1,0:T(8,128)}, f32[512,768]{1,0:T(8,128)}, f32[2,768]{1,0:T(2,128)}, bf16[35,64,768]{2,1,0:T(8,128)(2,1)}) custom-call(bf16[4,2048,128]{2,1,0:T(8,128)(2,1)} %get-tuple-element.52.qkv, bf16[2,128,2048]{2,1,0:T(8,128)(2,1)} %copy-done.19, f32[2,8,1,256]{3,2,1,0:T(1,128)} %copy-done.26, ...), custom_call_target="tpu_custom_call" | custom-call | flops 49999998976 | bytes 31715328 | tf_op jit(solution)/shard_map/pallas_call | solution.py:438
  374.7 1.4 slice_reduce_fusion
  376.1 0.0 copy-done
  376.1 2.0 copy-done.1
  378.0 11.3 %shard_map.208 = (f32[1024,768]{1,0:T(8,128)}, f32[768,1024]{1,0:T(8,128)}, f32[768,1024]{1,0:T(8,128)}, f32[384,768]{1,0:T(8,128)}, f32[768,384]{1,0:T(8,128)}, /*index=5*/f32[192,768]{1,0:T(8,128)}, f32[192,768]{1,0:T(8,128)}) custom-call(bf16[35,64,768]{2,1,0:T(8,128)(2,1)S(1)} %copy-done, bf16[35,64,768]{2,1,0:T(8,128)(2,1)S(1)} %copy-done.1), custom_call_target="tpu_custom_call" | custom-call | bytes 19464192 | tf_op jit(solution)/shard_map/pallas_call | solution.py:1216
  389.4 0.0 copy-done.28
  389.4 0.0 copy-start.27
  389.4 1.1 copy.25
  390.6 0.8 copy-done.27
  391.4 1.1 copy.26
  (21 shorter events, 0.0 us)
Async XLA Ops:
  1.3 44.1 %copy-start.2 = (f32[1,768]{1,0:T(1,128)}, f32[1,768]{1,0:T(1,128)S(1)}, u32[]{:S(2)}) copy-start(f32[1,768]{1,0:T(1,128)S(1)} %broadcast_in_dim.6.gain) | copy-start | bytes 9220
  2.0 1.1 copy-start.5
  3.2 1.1 copy-start.6
  4.2 1.1 copy-start.7
  5.3 1.0 copy-start.8
  6.3 1.0 copy-start.9
  7.2 0.8 copy-start.10
  8.1 40.8 %copy-start.3 = (f32[1,768]{1,0:T(1,128)}, f32[1,768]{1,0:T(1,128)S(1)}, u32[]{:S(2)}) copy-start(f32[1,768]{1,0:T(1,128)S(1)} %broadcast_in_dim.7.gain) | copy-start | bytes 9220
  8.1 40.8 %copy-start.4 = (bf16[512,768]{1,0:T(8,128)(2,1)S(1)}, bf16[512,768]{1,0:T(8,128)(2,1)}, u32[]{:S(2)}) copy-start(bf16[512,768]{1,0:T(8,128)(2,1)} %dy.3) | copy-start | bytes 2359300
  45.4 1.1 copy-start.17
  46.5 0.8 copy-start.22
  47.3 0.8 copy-start.23
  48.1 0.7 copy-start.24
  48.8 62.1 %copy-start.19 = (bf16[2,128,2048]{2,1,0:T(8,128)(2,1)}, bf16[2,128,2048]{2,1,0:T(8,128)(2,1)S(1)}, u32[]{:S(2)}) copy-start(bf16[2,128,2048]{2,1,0:T(8,128)(2,1)S(1)} %get-tuple-element.53.kvt) | copy-start | bytes 3145732
  48.8 62.1 %copy-start.21 = (bf16[2,256,768]{2,1,0:T(8,128)(2,1)}, bf16[2,256,768]{2,1,0:T(8,128)(2,1)S(1)}, u32[]{:S(2)}) copy-start(bf16[2,256,768]{2,1,0:T(8,128)(2,1)S(1)} %get-tuple-element.54.wo) | copy-start | bytes 2359300
  48.8 64.5 %copy-start.14 = (bf16[2,768,512]{2,1,0:T(8,128)(2,1)}, bf16[2,768,512]{2,1,0:T(8,128)(2,1)S(1)}, u32[]{:S(2)}) copy-start(bf16[2,768,512]{2,1,0:T(8,128)(2,1)S(1)} %get-tuple-element.58.wg) | copy-start | bytes 4718596
  48.8 2.8 copy-start.12
  51.7 61.7 %copy-start.13 = (bf16[2,512,768]{2,1,0:T(8,128)(2,1)S(1)}, bf16[2,512,768]{2,1,0:T(8,128)(2,1)}, u32[]{:S(2)}) copy-start(bf16[2,512,768]{2,1,0:T(8,128)(2,1)} %get-tuple-element.60.wd) | copy-start | bytes 4718596
  51.7 61.7 %copy-start.15 = (bf16[2,768,512]{2,1,0:T(8,128)(2,1)S(1)}, bf16[2,768,512]{2,1,0:T(8,128)(2,1)}, u32[]{:S(2)}) copy-start(bf16[2,768,512]{2,1,0:T(8,128)(2,1)} %get-tuple-element.59.wu) | copy-start | bytes 4718596
  110.9 1.1 copy-start.18
  112.1 0.7 copy-start.25
  112.8 0.6 copy-start.26
  113.4 44.1 %copy-start.20 = (bf16[4,512,256]{2,1,0:T(8,128)(2,1)}, bf16[4,512,256]{2,1,0:T(8,128)(2,1)S(1)}, u32[]{:S(2)}) copy-start(bf16[4,512,256]{2,1,0:T(8,128)(2,1)S(1)} %get-tuple-element.65.attn) | copy-start | bytes 3145732
  157.4 1.3 copy-start.11
  158.8 1.1 copy-start.16
  258.3 117.7 %copy-start = (bf16[35,64,768]{2,1,0:T(8,128)(2,1)S(1)}, bf16[35,64,768]{2,1,0:T(8,128)(2,1)}, u32[]{:S(2)}) copy-start(bf16[35,64,768]{2,1,0:T(8,128)(2,1)} %get-tuple-element.84.rest_0_) | copy-start | bytes 10321924
  376.1 2.0 copy-start.1
  378.0 11.3 %copy-start.28 = (f32[512,768]{1,0:T(8,128)S(1)}, f32[512,768]{1,0:T(8,128)}, u32[]{:S(2)}) copy-start(f32[512,768]{1,0:T(8,128)} %get-tuple-element.106) | copy-start | bytes 4718596
  389.4 2.0 copy-start.27

commit v3 on v2

--- a/solution.py
+++ b/solution.py
@@ -115,16 +115,20 @@
         dst = self.buf.at[core, row, rows_of(half)]
         return remote(dst if src is None else src, dst, self.dsend.at[i], self.drecv.at[i], {"col": 1 - self.k})
 
+    def local(self):
+        return pltpu.make_async_copy(self.own, self.buf.at[self.k, self.r], self.lsem)
+
     def start(self):
-        first, second = self.own.at[pl.ds(0, PIECE)], self.own.at[pl.ds(PIECE, PIECE)]
+        own = self.buf.at[self.k, self.r] if self.own is None else self.own
+        first, second = own.at[pl.ds(0, PIECE)], own.at[pl.ds(PIECE, PIECE)]
         self.ici(0, self.r, 0, self.rx, first).start()
         self.ici(1, self.r, 1, self.ry, second).start()
         self.ici(2, self.r, 1, self.rx, second).start()
         self.ici(3, self.r, 0, self.ry, first).start()
         self.pair(0, self.k, self.r, 0, first).start()
         self.pair(1, self.k, self.r, 1, second).start()
-        self.local = pltpu.make_async_copy(self.own, self.buf.at[self.k, self.r], self.lsem)
-        self.local.start()
+        if self.own is not None:
+            self.local().start()
 
     def arrive(self, i):
         row, half = self.piece(i)
@@ -145,7 +149,8 @@
         self.pair(i, 1 - self.k, row, half).wait_recv()
 
     def run(self, compute, before=None, after=None):
-        self.local.wait()
+        if self.own is not None:
+            self.local().wait()
 
         def pair(q, carry):
             for u in range(2):
@@ -481,17 +486,28 @@
     return [f(t).astype(np.float32) for t in (coarse, fine) for f in (np.cos, np.sin)]
 
 
-def project_kernel(
-    x, gain, wq_h, wk_h, wv_h, wo_h, wg, wu, wd, tables,
-    normed, qkv, kvt, wqkv_o, wo_o, wg_o, wu_o, wd_o, cos_o, sin_o, rstd_o,
-    raw, gains, give_in, give_out, wq, wk, wv, wo, wsem, wrecv, csem, *sems,
+def exchange(k, stat, sems):
+    copy = remote(stat.at[k], stat.at[k], sems.at[0], sems.at[1], {"col": 1 - k})
+    copy.start()
+    remote(stat.at[1 - k], stat.at[1 - k], sems.at[0], sems.at[1], {"col": 1 - k}).wait_recv()
+    copy.wait_send()
+    return stat[0][:, 0:1] + stat[1][:, 0:1]
+
+
+def causal(shape):
+    return lax.broadcasted_iota(jnp.int32, shape, 0) <= lax.broadcasted_iota(jnp.int32, shape, 1)
+
+
+def front_kernel(
+    x, dy, gain, gain_f, wq_h, wk_h, wv_h, wo_h, wg, wu, wd, tables,
+    normed_o, f_o, qkv, kvt, wqkv_o, wo_o, wg_o, wu_o, wd_o, cos_o, sin_o, rstd1_o,
+    attn, lse, hidden, rstd2_o, middle, d_gate, d_up, part,
+    buf, dys, stage, gains, give_in, give_out, wq, wk, wv, wo, wsem, wrecv, csem, nsem, fsem,
+    stat, ssem, grad, give, gsend, grecv, *rest,
 ):
     r, k, rx, ry, r3 = place()
     width = x.shape[1]
     f_half = wg.shape[1] // 2
-    greet(rx, ry, k)
-    gather = Gather(x, raw, sems)
-    gather.start()
     mate = {"col": 1 - k}
     mine = pl.ds(pl.multiple_of(k * f_half, f_half), f_half)
     his = pl.ds(pl.multiple_of((1 - k) * f_half, f_half), f_half)
@@ -507,11 +523,17 @@
     ]
     for c in first + keep:
         c.start()
-
-    def give(n, src, dst):
+    greet(rx, ry, k)
+    gather = Gather(x, buf, rest[:5])
+    gather_dy = Gather(dy, dys, rest[5:10])
+    gather_f = Gather(None, buf, rest[10:15])
+    total = Sum(rest[15:])
+    gather.start()
+
+    def give_to(n, src, dst):
         return remote(src, dst.at[k], wsem.at[n], wrecv.at[n], mate)
 
-    gives = [give(0, gain, gains)]
+    gives = [give_to(0, gain, gains)]
     gives[0].start()
     heads_q = wq.shape[1] // 2
     heads_k = wk.shape[0] // 2
@@ -526,8 +548,8 @@
         dst_in[:, nq : nq + nk] = tn(wk[...], sk).astype(BF)
         dst_in[:, nq + nk : nq + 2 * nk] = tn(wv[...], sk).astype(BF)
         dst_out[...] = nn(spread_t(nq, 2 * heads_q, core * heads_q), wo[...]).astype(BF)
-    gives += [give(1, give_in, wqkv_o), give(2, give_out, wo_o)]
-    gives += [give(3, wg.at[:, his], wg_o), give(4, wu.at[:, his], wu_o), give(5, wd.at[his], wd_o)]
+    gives += [give_to(1, give_in, wqkv_o), give_to(2, give_out, wo_o)]
+    gives += [give_to(3, wg.at[:, his], wg_o), give_to(4, wu.at[:, his], wu_o), give_to(5, wd.at[his], wd_o)]
     for g in gives[1:]:
         g.start()
     sign = jnp.where(lax.broadcasted_iota(jnp.int32, (32, LANE), 1) < LANE // 2, -1.0, 1.0)
@@ -541,106 +563,59 @@
     for n in range(3):
         gives[n].wait_recv()
 
-    def compute(i, row, half):
+    def keep_normed(i):
+        row, half = gather.piece(i)
+        return pltpu.make_async_copy(stage.at[i % 2], normed_o.at[:, row, rows_of(half)], nsem.at[i])
+
+    def project(i, row, half):
         at = rows_of(half)
-        x0 = raw[0, row, at, :].astype(F32)
-        x1 = raw[1, row, at, :].astype(F32)
-        total = jnp.sum(x0 * x0, 1, keepdims=True) + jnp.sum(x1 * x1, 1, keepdims=True)
-        rstd = lax.rsqrt(total / (2 * width) + EPS)
+        x0 = buf[0, row, at, :].astype(F32)
+        x1 = buf[1, row, at, :].astype(F32)
+        square = jnp.sum(x0 * x0, 1, keepdims=True) + jnp.sum(x1 * x1, 1, keepdims=True)
+        rstd = lax.rsqrt(square / (2 * width) + EPS)
         n0 = (x0 * rstd * gains[0]).astype(BF)
         n1 = (x1 * rstd * gains[1]).astype(BF)
-        normed[0, row, at, :] = n0
-        normed[1, row, at, :] = n1
+
+        @pl.when(i >= 2)
+        def _():
+            keep_normed(i - 2).wait()
+
+        stage[i % 2, 0] = n0
+        stage[i % 2, 1] = n1
 
         @pl.when(i < 2)
         def _():
-            rstd_o[at, :] = jnp.broadcast_to(rstd, (PIECE, LANE))
+            rstd1_o[at, :] = jnp.broadcast_to(rstd, (PIECE, LANE))
 
         got = nn(n0, wqkv_o[0]) + nn(n1, wqkv_o[1])
+        keep_normed(i).start()
         pos = pl.ds(pl.multiple_of((row % 2) * 2 * PIECE + half * PIECE, PIECE), PIECE)
         out = pl.ds(pl.multiple_of(row * 2 * PIECE + half * PIECE, PIECE), PIECE)
         cos, sin = cos_o[pos, :], sin_o[pos, :]
-        for part in range(4):
-            u = got[:, part * LANE : (part + 1) * LANE]
-            if part < 3:
+        for p in range(4):
+            u = got[:, p * LANE : (p + 1) * LANE]
+            if p < 3:
                 u = u * cos + pltpu.roll(u, LANE // 2, 1) * sin
-            qkv[part, out, :] = u.astype(BF)
-            if part >= 2:
-                kvt[part - 2, :, out] = u.T.astype(BF)
-
-    gather.run(compute)
-    for g in gives[3:]:
-        g.wait_recv()
-    for g in gives:
-        g.wait_send()
-
-
-def project(x, gain, wq, wk, wv, wo, wg, wu, wd):
-    tokens, width = x.shape
-    f_half = wg.shape[1] // 2
-    cols = 4 * LANE
-    outs = [
-        sds((2, 4, tokens, width), BF),
-        sds((4, 4 * tokens, LANE), BF),
-        sds((2, LANE, 4 * tokens), BF),
-        sds((2, width, cols), BF),
-        sds((2, 2 * LANE, width), BF),
-        sds((2, width, f_half), BF),
-        sds((2, width, f_half), BF),
-        sds((2, f_half, width), BF),
-        sds((LENGTH, LANE), F32),
-        sds((LENGTH, LANE), F32),
-        sds((tokens, LANE), F32),
-    ]
-    scratch = [
-        pltpu.VMEM((2, 4, tokens, width), BF),
-        pltpu.VMEM((2, 1, width), F32),
-        pltpu.VMEM((width, cols), BF),
-        pltpu.VMEM((2 * LANE, width), BF),
-        pltpu.VMEM(wq.shape, BF),
-        pltpu.VMEM(wk.shape, BF),
-        pltpu.VMEM(wv.shape, BF),
-        pltpu.VMEM(wo.shape, BF),
-        DMA((6,)),
-        DMA((6,)),
-        DMA((8,)),
-    ] + GATHER_SEMS
-    ins = [ANY, VM] + [ANY] * 7 + [VM]
-    args = [x, gain, wq, wk, wv, wo, wg, wu, wd, jnp.asarray(np.stack(angle_tables()))]
-    return call(project_kernel, 0, outs, ins, args, scratch, 3e10)
-
-
-def exchange(k, stat, sems):
-    copy = remote(stat.at[k], stat.at[k], sems.at[0], sems.at[1], {"col": 1 - k})
-    copy.start()
-    remote(stat.at[1 - k], stat.at[1 - k], sems.at[0], sems.at[1], {"col": 1 - k}).wait_recv()
-    copy.wait_send()
-    return stat[0][:, 0:1] + stat[1][:, 0:1]
-
-
-def causal(shape):
-    return lax.broadcasted_iota(jnp.int32, shape, 0) <= lax.broadcasted_iota(jnp.int32, shape, 1)
-
-
-def attend_kernel(
-    qkv, kvt, wo, x, gain, dy,
-    attn, lse, hidden, normed, rstd_o, all_dy,
-    stat, ssem, *rest,
-):
-    r, k, rx, ry, r3 = place()
-    width = x.shape[1]
-    greet(rx, ry, k)
-    total = Sum(rest[:9])
-    gather = Gather(dy, all_dy, rest[9:])
-    gather.start()
-
-    def compute(row, half):
+            qkv[p, out, :] = u.astype(BF)
+            if p >= 2:
+                kvt[p - 2, :, out] = u.T.astype(BF)
+
+    def dy_too(q):
+        @pl.when(q == 0)
+        def _():
+            gather_dy.start()
+
+    gather.run(project, None, dy_too)
+    for i in (6, 7):
+        keep_normed(i).wait()
+
+    def attend(row, half):
         base = pl.multiple_of(row // 2 * LENGTH, LENGTH)
         at = rows_of(half)
         qrow = pl.ds(pl.multiple_of(row * 2 * PIECE + half * PIECE, PIECE), PIECE)
         order = (row % 2) * 2 + half
 
-        def attend(p):
+        def queries(p):
             span = PIECE * (p + 1)
             for head in range(2):
                 keys = qkv[2, pl.ds(base, span), :]
@@ -656,63 +631,66 @@
                 lse[head, row * 2 + half] = top * SCALE + jnp.log(weight)
 
         for p in range(4):
-            pl.when(order == p)(lambda p=p: attend(p))
+            pl.when(order == p)(lambda p=p: queries(p))
         a = attn[row, at, :]
-        return nn(a, wo[k]), nn(a, wo[1 - k])
-
-    total.send_all(compute)
+        return nn(a, wo_o[k]), nn(a, wo_o[1 - k])
+
+    def dy_arrive(j):
+        @pl.when(j == 3)
+        def _():
+            gather_dy.arrive(2)
+            gather_dy.arrive(3)
+
+        @pl.when(j == 7)
+        def _():
+            gather_dy.arrive(4)
+            gather_dy.arrive(5)
+
+    total.send_all(attend, dy_arrive)
+    for g in gives[3:]:
+        g.wait_recv()
+    gather_dy.local().wait()
+
+    def mid_pair(q, carry):
+        for u in range(2):
+            i = 2 * q + u
+            gather_dy.ready(i)
+            row, half = gather_dy.piece(i)
+            at = rows_of(half)
+            d_mid = nt(dys[0, row, at, :], wd_o[0]) + nt(dys[1, row, at, :], wd_o[1])
+            d_gate[row, at, :] = d_mid.astype(BF)
+        return carry
+
+    lax.fori_loop(0, 3, mid_pair, 0)
+    gather_dy.arrive(6)
+    gather_dy.arrive(7)
     total.relay(4)
     total.relay(5)
-    gather.arrive(2)
-    gather.arrive(3)
+    mid_pair(3, 0)
+    gather_dy.finish()
     for half in range(2):
         at = rows_of(half)
-        h = x[at, :].astype(F32) + total.last(6 + half)
+        h = buf[k, r, at, :].astype(F32) + total.last(6 + half)
         hidden[at, :] = h
         stat[k, at, :] = jnp.broadcast_to(jnp.sum(h * h, 1, keepdims=True), (PIECE, LANE))
-    rstd = lax.rsqrt(exchange(k, stat, ssem) / (2 * width) + EPS)
-    rstd_o[...] = jnp.broadcast_to(rstd, rstd_o.shape)
-    normed[...] = (hidden[...] * rstd * gain[...]).astype(BF)
-    for i in range(4, 8):
-        gather.arrive(i)
-    for i in range(8):
-        gather.ready(i)
-    gather.local.wait()
-    gather.finish()
-    total.finish()
-
-
-def attend(qkv, kvt, wo, x, gain, dy):
-    tokens, width = x.shape
-    outs = [
-        sds((4, tokens, 2 * LANE), BF),
-        sds((2, 8, 1, PIECE), F32),
-        sds((tokens, width), F32),
-        sds((tokens, width), BF),
-        sds((tokens, LANE), F32),
-        sds((2, 4, tokens, width), BF),
-    ]
-    scratch = [pltpu.VMEM((2, tokens, LANE), F32), DMA((2,))] + sum_scratch(width) + GATHER_SEMS
-    return call(
-        attend_kernel, 1, outs, [VM] * 5 + [ANY], [qkv, kvt, wo, x, gain, dy], scratch, 3e10
-    )
-
-
-def expand_kernel(
-    nf, all_dy, wg, wu, wd, all_f, middle, d_gate, d_up, part, grad, give, gsend, grecv, *sems
-):
-    r, k, rx, ry, r3 = place()
-    greet(rx, ry, k)
-    gather = Gather(nf, all_f, sems)
-    gather.start()
-
-    def compute(i, row, half):
+    rstd2 = lax.rsqrt(exchange(k, stat, ssem) / (2 * width) + EPS)
+    buf[k, r] = (hidden[...] * rstd2 * gain_f[...]).astype(BF)
+    rstd2_o[...] = jnp.broadcast_to(rstd2, rstd2_o.shape)
+    gather_f.start()
+
+    def keep_f(i):
+        row, half = gather_f.piece(i)
         at = rows_of(half)
-        f0, f1 = all_f[0, row, at, :], all_f[1, row, at, :]
-        dy0, dy1 = all_dy[0, row, at, :], all_dy[1, row, at, :]
-        gate = nn(f0, wg[0]) + nn(f1, wg[1])
-        upper = nn(f0, wu[0]) + nn(f1, wu[1])
-        d_mid = nt(dy0, wd[0]) + nt(dy1, wd[1])
+        return pltpu.make_async_copy(buf.at[:, row, at], f_o.at[:, row, at], fsem.at[i])
+
+    def expand(i, row, half):
+        at = rows_of(half)
+        keep_f(i).start()
+        f0, f1 = buf[0, row, at, :], buf[1, row, at, :]
+        dy0, dy1 = dys[0, row, at, :], dys[1, row, at, :]
+        gate = nn(f0, wg_o[0]) + nn(f1, wg_o[1])
+        upper = nn(f0, wu_o[0]) + nn(f1, wu_o[1])
+        d_mid = d_gate[row, at, :].astype(F32)
         sig = 1.0 / (1.0 + jnp.exp(-gate))
         swish = gate * sig
         mid = (swish * upper).astype(BF)
@@ -731,11 +709,13 @@
             grad[0] += g0
             grad[1] += g1
 
-    gather.run(compute)
+    gather_f.run(expand)
     half = DOWN_CHUNKS // 4
 
     def swap(j, core):
-        return remote(give.at[pl.ds(2 * j, 2)], part.at[pl.ds(2 * (half * core + j), 2)], gsend.at[j], grecv.at[j], {"col": 1 - k})
+        return remote(
+            give.at[pl.ds(2 * j, 2)], part.at[pl.ds(2 * (half * core + j), 2)], gsend.at[j], grecv.at[j], mate
+        )
 
     for j in range(half):
         for h in range(2):
@@ -745,21 +725,42 @@
         for h in range(2):
             rows = slice(j * TALL + h * CHUNK, j * TALL + (h + 1) * CHUNK)
             part[2 * (half * k + j) + h] = grad[k, rows, :].astype(BF)
+    for i in range(8):
+        keep_f(i).wait()
     for j in range(half):
         swap(j, 1 - k).wait_recv()
     for j in range(half):
         swap(j, k).wait_send()
-
-
-def expand(nf, all_dy, wg, wu, wd):
-    tokens, width = nf.shape
-    f_half = wg.shape[2]
-    outs = [sds((2, 4, tokens, width), BF)] + [sds((4, tokens, f_half), BF)] * 3
-    outs += [sds((DOWN_CHUNKS, CHUNK, WIDE), BF)]
+    for g in gives:
+        g.wait_send()
+    total.finish()
+
+
+def front(x, dy, gain, gain_f, wq, wk, wv, wo, wg, wu, wd):
+    tokens, width = x.shape
+    f_half = wg.shape[1] // 2
+    cols = 4 * LANE
+    gathered = (2, 4, tokens, width)
+    outs = [sds(gathered, BF), sds(gathered, BF)]
+    outs += [sds((4, 4 * tokens, LANE), BF), sds((2, LANE, 4 * tokens), BF)]
+    outs += [sds((2, width, cols), BF), sds((2, 2 * LANE, width), BF)]
+    outs += [sds((2, width, f_half), BF)] * 2 + [sds((2, f_half, width), BF)]
+    outs += [sds((LENGTH, LANE), F32)] * 2 + [sds((tokens, LANE), F32)]
+    outs += [sds((4, tokens, 2 * LANE), BF), sds((2, 8, 1, PIECE), F32)]
+    outs += [sds((tokens, width), F32), sds((tokens, LANE), F32)]
+    outs += [sds((4, tokens, f_half), BF)] * 3 + [sds((DOWN_CHUNKS, CHUNK, WIDE), BF)]
     half = DOWN_CHUNKS // 4
-    scratch = [pltpu.VMEM((2, f_half, width), F32), pltpu.VMEM((2 * half, CHUNK, WIDE), BF), DMA((half,)), DMA((half,))]
-    args = [nf, all_dy, wg, wu, wd]
-    return call(expand_kernel, 2, outs, [ANY] + [VM] * 4, args, scratch + GATHER_SEMS, 3e10)
+    scratch = [pltpu.VMEM(gathered, BF)] * 2 + [pltpu.VMEM((2, 2, PIECE, width), BF)]
+    scratch += [pltpu.VMEM((2, 1, width), F32), pltpu.VMEM((width, cols), BF), pltpu.VMEM((2 * LANE, width), BF)]
+    scratch += [pltpu.VMEM(w.shape, BF) for w in (wq, wk, wv, wo)]
+    scratch += [DMA((6,)), DMA((6,)), DMA((8,)), DMA((8,)), DMA((8,))]
+    scratch += [pltpu.VMEM((2, tokens, LANE), F32), DMA((2,)), pltpu.VMEM((2, f_half, width), F32)]
+    scratch += [pltpu.VMEM((2 * half, CHUNK, WIDE), BF), DMA((half,)), DMA((half,))]
+    scratch += GATHER_SEMS * 3 + sum_scratch(width)
+    ins = [ANY] * 2 + [VM] * 2 + [ANY] * 7 + [VM]
+    args = [x, dy, gain, gain_f, wq, wk, wv, wo, wg, wu, wd, jnp.asarray(np.stack(angle_tables()))]
+    out_specs = [ANY] * 2 + [VM] * (len(outs) - 2)
+    return call(front_kernel, 0, outs, ins, args, scratch, 9e10, 60, out_specs)
 
 
 TICKS = 35
@@ -1236,11 +1237,13 @@
     tokens, width = layer_input.shape
     q_cols, k_cols = w_query.shape[1], w_key.shape[1]
     gain_a, gain_f = gain_attn[None], gain_ffn[None]
-    normed, qkv, kvt, wqkv, wo, wg, wu, wd, cos, sin, rstd1 = project(
-        layer_input, gain_a, w_query, w_key.T, w_value.T, w_out, w_gate, w_up, w_down
+    (
+        normed, all_f, qkv, kvt, wqkv, wo, wg, wu, wd, cos, sin, rstd1,
+        attn, lse, hidden, rstd2, middle, d_gate, d_up, part_d,
+    ) = front(
+        layer_input, cotangent, gain_a, gain_f,
+        w_query, w_key.T, w_value.T, w_out, w_gate, w_up, w_down,
     )
-    attn, lse, hidden, nf, rstd2, all_dy = attend(qkv, kvt, wo, layer_input, gain_f, cotangent)
-    all_f, middle, d_gate, d_up, part_d = expand(nf, all_dy, wg, wu, wd)
     d_hidden, gains_f, part_m, part_o, d_attn, tot1, acc, tot = contract(
         d_gate, d_up, wg, wu, hidden, rstd2, gain_f, cotangent, wo, attn, part_d, all_f
     )

time: 398 us -> 370 us (0.930)
  local copies, waits for them, and re-layouts: 25 us -> 9.01 us
  Pallas kernels: 367 us -> 355 us
    unnamed x60 -> x10, local copies, waits for them, and re-layouts: 22.3 us -> 5.09 us
    pallas_call x5 -> x3, Pallas kernels: 355 us -> 344 us  [call(): pl.pallas_call(kernel, out_shape=outs, in_specs=ins, out_specs=out_specs...]
where the time goes in v3:
time: 370 us; the launch traced here: 365 us
  Pallas kernels  355 us (96%)
  local copies, waits for them, and re-layouts  9.01 us (2%)
    pallas_call x3, Pallas kernels, call(): pl.pallas_call(kernel, out_shape=outs, in_specs=ins, out_specs=out_specs...  344 us
    pallas_call x1, Pallas kernels, unpack(): pl.pallas_call(functools.partial(unpack_kernel, ticks, q_cols, k_cols), o...  11.3 us

profile of v3, /device:TPU:0, one launch (start us, length us, event | category | flops | bytes accessed | tf_op | source)
XLA Modules:
  0.0 365.2 jit_solution(5390155790078704982)
XLA Ops:
  0.6 1.3 broadcast_in_dim.6.gain
  1.9 1.3 broadcast_in_dim.7.gain_f.gain
  3.2 129.1 %shard_map.203 = (bf16[2,4,512,768]{3,2,1,0:T(8,128)(2,1)}, bf16[2,4,512,768]{3,2,1,0:T(8,128)(2,1)}, bf16[4,2048,128]{2,1,0:T(8,128)(2,1)}, bf16[2,128,2048]{2,...) custom-call(bf16[512,768]{1,0:T(8,128)(2,1)} %x.3, ...), custom_call_target="tpu_custom_call" | custom-call | flops 89999998976 | bytes 43014144 | tf_op jit(solution)/shard_map/pallas_call | solution.py:443
  132.2 98.5 %shard_map.204 = (f32[512,768]{1,0:T(8,128)}, f32[1,768]{1,0:T(1,128)}, bf16[32,64,768]{2,1,0:T(8,128)(2,1)}, bf16[6,64,768]{2,1,0:T(8,128)(2,1)}, bf16[4,512,25...) custom-call(bf16[4,512,512]{2,1,0:T(8,128)(2,1)} %get-tuple-element.5, ...), custom_call_target="tpu_custom_call" | custom-call | flops 49999998976 | bytes 29857792 | tf_op jit(solution)/shard_map/pallas_call | solution.py:443
  230.7 0.0 copy-start
  230.7 116.4 %shard_map.205 = (f32[512,768]{1,0:T(8,128)}, f32[512,768]{1,0:T(8,128)}, f32[2,768]{1,0:T(2,128)}, bf16[35,64,768]{2,1,0:T(8,128)(2,1)}) custom-call(bf16[4,2048,128]{2,1,0:T(8,128)(2,1)} %get-tuple-element.50.qkv, bf16[2,128,2048]{2,1,0:T(8,128)(2,1)} %get-tuple-element.51.kvt, f32[2,8,1,256]{3,2,1,0:T(1,128)} %get-tuple-element.52.lse, ...), custom_call_target="tpu_custom_call" | custom-call | flops 49999998976 | bytes 31715328 | tf_op jit(solution)/shard_map/pallas_call | solution.py:443
  347.1 1.4 slice_reduce_fusion
  348.5 0.0 copy-done
  348.5 0.0 copy-start.1
  348.5 2.0 copy-done.1
  350.5 0.0 copy-start.3
  350.5 11.3 %shard_map.206 = (f32[1024,768]{1,0:T(8,128)}, f32[768,1024]{1,0:T(8,128)}, f32[768,1024]{1,0:T(8,128)}, f32[384,768]{1,0:T(8,128)}, f32[768,384]{1,0:T(8,128)}, /*index=5*/f32[192,768]{1,0:T(8,128)}, f32[192,768]{1,0:T(8,128)}) custom-call(bf16[35,64,768]{2,1,0:T(8,128)(2,1)S(1)} %copy-done, bf16[35,64,768]{2,1,0:T(8,128)(2,1)S(1)} %copy-done.1), custom_call_target="tpu_custom_call" | custom-call | bytes 19464192 | tf_op jit(solution)/shard_map/pallas_call | solution.py:1217
  361.8 0.0 copy-done.3
  361.8 0.0 copy-start.2
  361.9 1.1 copy.25
  363.0 0.8 copy-done.2
  363.8 1.1 copy.26
Async XLA Ops:
  230.7 117.8 %copy-start = (bf16[35,64,768]{2,1,0:T(8,128)(2,1)S(1)}, bf16[35,64,768]{2,1,0:T(8,128)(2,1)}, u32[]{:S(2)}) copy-start(bf16[35,64,768]{2,1,0:T(8,128)(2,1)} %get-tuple-element.80.rest_0_) | copy-start | bytes 10321924
  348.5 2.0 copy-start.1
  350.5 11.3 %copy-start.3 = (f32[512,768]{1,0:T(8,128)S(1)}, f32[512,768]{1,0:T(8,128)}, u32[]{:S(2)}) copy-start(f32[512,768]{1,0:T(8,128)} %get-tuple-element.102) | copy-start | bytes 4718596
  361.8 2.0 copy-start.2

commit v4 on v3

--- a/solution.py
+++ b/solution.py
@@ -414,8 +414,11 @@
             copy().start()
 
     def open(self):
-        for j in range(min(LAG, self.ticks)):
+        def one(j, carry):
             self.begin(j)
+            return carry
+
+        lax.fori_loop(0, min(LAG, self.ticks), one, 0)
 
     def step(self, j):
         self.end(j)
@@ -424,28 +427,96 @@
         def _():
             self.begin(j + LAG)
 
-    def rest(self, j):
+    def steps(self, start, stop):
         def one(t, carry):
             self.step(t)
             return carry
 
-        lax.fori_loop(j, self.ticks, one, 0)
-        for t in range(max(self.ticks - 2, 0), self.ticks):
+        lax.fori_loop(start, stop, one, 0)
+
+    def rest(self, j):
+        self.steps(j, self.ticks)
+
+        def settle(t, carry):
             self.settle(t)
+            return carry
+
+        lax.fori_loop(max(self.ticks - 2, 0), self.ticks, settle, 0)
         if self.carry is not None:
             for b in range(LAG):
                 self.carry[0][b] = self.acc[(self.ticks + b) % RING]
                 self.carry[1][b] = self.tot[(self.ticks + b) % self.ring]
 
 
-def call(kernel, cid, outs, ins, args, scratch, flops, vmem=44, out_specs=None):
+class Io:
+    def __init__(self):
+        self.coming, self.later, self.going = [], [], []
+
+    def more(self):
+        for entry in self.later:
+            entry[1].start()
+        self.coming += self.later
+        self.later = []
+
+    def need(self, *bufs):
+        for buf in bufs:
+            for at, (ref, copy) in enumerate(self.coming):
+                if ref is buf:
+                    copy.wait()
+                    del self.coming[at]
+                    break
+
+    def spill(self, *bufs):
+        for buf in bufs:
+            for entry in self.going:
+                if entry[0] is buf and not entry[2]:
+                    entry[1].start()
+                    entry[2] = True
+
+    def finish(self):
+        self.more()
+        self.need(*[ref for ref, _ in self.coming])
+        self.spill(*[entry[0] for entry in self.going])
+        for _, copy, _ in self.going:
+            copy.wait()
+
+
+def staged(kernel, n_in, fetch, spill, early):
+    def wrapped(*refs):
+        refs, sems = list(refs[:-1]), refs[-1]
+        count = len(fetch) + len(spill)
+        refs, bufs = refs[:-count], refs[-count:]
+        io = Io()
+        for n, i in enumerate(fetch):
+            copy = pltpu.make_async_copy(refs[i], bufs[n], sems.at[n])
+            if n < early:
+                copy.start()
+            (io.coming if n < early else io.later).append((bufs[n], copy))
+            refs[i] = bufs[n]
+        for n, o in enumerate(spill, len(fetch)):
+            io.going.append([bufs[n], pltpu.make_async_copy(bufs[n], refs[n_in + o], sems.at[n]), False])
+            refs[n_in + o] = bufs[n]
+        kernel(io, *refs)
+        io.finish()
+
+    return wrapped
+
+
+def call(kernel, cid, outs, ins, args, scratch, flops, vmem, out_specs, fetch, spill, early=0):
     moved = sum(int(np.prod(a.shape)) * a.dtype.itemsize for a in list(args) + list(outs))
+    ins, out_specs = list(ins), list(out_specs)
+    held = [pltpu.VMEM(args[i].shape, args[i].dtype) for i in fetch]
+    held += [pltpu.VMEM(outs[o].shape, outs[o].dtype) for o in spill]
+    for i in fetch:
+        ins[i] = ANY
+    for o in spill:
+        out_specs[o] = ANY
     return pl.pallas_call(
-        kernel,
+        staged(kernel, len(args), fetch, spill, early),
         out_shape=outs,
         in_specs=ins,
-        out_specs=out_specs or [VM] * len(outs),
-        scratch_shapes=scratch,
+        out_specs=out_specs,
+        scratch_shapes=list(scratch) + held + [DMA((len(held),))],
         compiler_params=pltpu.CompilerParams(
             collective_id=cid, has_side_effects=True, vmem_limit_bytes=vmem << 20
         ),
@@ -499,11 +570,12 @@
 
 
 def front_kernel(
+    io,
     x, dy, gain, gain_f, wq_h, wk_h, wv_h, wo_h, wg, wu, wd, tables,
     normed_o, f_o, qkv, kvt, wqkv_o, wo_o, wg_o, wu_o, wd_o, cos_o, sin_o, rstd1_o,
-    attn, lse, hidden, rstd2_o, middle, d_gate, d_up, part,
+    attn, lse, hidden, rstd2_o, part, mid_o, gate_o, up_o,
     buf, dys, stage, gains, give_in, give_out, wq, wk, wv, wo, wsem, wrecv, csem, nsem, fsem,
-    stat, ssem, grad, give, gsend, grecv, *rest,
+    stat, ssem, grad, give, gsend, grecv, middle, d_gate, d_up, msem, *rest,
 ):
     r, k, rx, ry, r3 = place()
     width = x.shape[1]
@@ -512,7 +584,6 @@
     mine = pl.ds(pl.multiple_of(k * f_half, f_half), f_half)
     his = pl.ds(pl.multiple_of((1 - k) * f_half, f_half), f_half)
     keep = [
-        pltpu.make_async_copy(gain, gains.at[k], csem.at[0]),
         pltpu.make_async_copy(wg.at[:, mine], wg_o.at[k], csem.at[1]),
         pltpu.make_async_copy(wu.at[:, mine], wu_o.at[k], csem.at[2]),
         pltpu.make_async_copy(wd.at[mine], wd_o.at[k], csem.at[3]),
@@ -528,12 +599,13 @@
     gather_dy = Gather(dy, dys, rest[5:10])
     gather_f = Gather(None, buf, rest[10:15])
     total = Sum(rest[15:])
+    gains[k] = gain[...].reshape(1, width)
     gather.start()
 
     def give_to(n, src, dst):
         return remote(src, dst.at[k], wsem.at[n], wrecv.at[n], mate)
 
-    gives = [give_to(0, gain, gains)]
+    gives = [give_to(0, gains.at[k], gains)]
     gives[0].start()
     heads_q = wq.shape[1] // 2
     heads_k = wk.shape[0] // 2
@@ -647,8 +719,10 @@
             gather_dy.arrive(5)
 
     total.send_all(attend, dy_arrive)
+    io.spill(qkv, kvt, cos_o, sin_o, attn, wqkv_o, wo_o)
     for g in gives[3:]:
         g.wait_recv()
+    io.spill(wg_o, wu_o, wd_o)
     gather_dy.local().wait()
 
     def mid_pair(q, carry):
@@ -674,9 +748,18 @@
         hidden[at, :] = h
         stat[k, at, :] = jnp.broadcast_to(jnp.sum(h * h, 1, keepdims=True), (PIECE, LANE))
     rstd2 = lax.rsqrt(exchange(k, stat, ssem) / (2 * width) + EPS)
-    buf[k, r] = (hidden[...] * rstd2 * gain_f[...]).astype(BF)
+    buf[k, r] = (hidden[...] * rstd2 * gain_f[...].reshape(1, width)).astype(BF)
     rstd2_o[...] = jnp.broadcast_to(rstd2, rstd2_o.shape)
     gather_f.start()
+    io.spill(hidden)
+
+    def keep_mids(i):
+        row, half = gather_f.piece(i)
+        at = rows_of(half)
+        return [
+            pltpu.make_async_copy(src.at[row, at], dst.at[row, at], msem.at[n, i])
+            for n, (src, dst) in enumerate(((middle, mid_o), (d_gate, gate_o), (d_up, up_o)))
+        ]
 
     def keep_f(i):
         row, half = gather_f.piece(i)
@@ -686,6 +769,12 @@
     def expand(i, row, half):
         at = rows_of(half)
         keep_f(i).start()
+
+        @pl.when(i > 0)
+        def _():
+            for c in keep_mids(i - 1):
+                c.start()
+
         f0, f1 = buf[0, row, at, :], buf[1, row, at, :]
         dy0, dy1 = dys[0, row, at, :], dys[1, row, at, :]
         gate = nn(f0, wg_o[0]) + nn(f1, wg_o[1])
@@ -710,6 +799,8 @@
             grad[1] += g1
 
     gather_f.run(expand)
+    for c in keep_mids(7):
+        c.start()
     half = DOWN_CHUNKS // 4
 
     def swap(j, core):
@@ -725,10 +816,17 @@
         for h in range(2):
             rows = slice(j * TALL + h * CHUNK, j * TALL + (h + 1) * CHUNK)
             part[2 * (half * k + j) + h] = grad[k, rows, :].astype(BF)
-    for i in range(8):
-        keep_f(i).wait()
     for j in range(half):
         swap(j, 1 - k).wait_recv()
+    io.spill(part)
+
+    def kept(i, carry):
+        keep_f(i).wait()
+        for c in keep_mids(i):
+            c.wait()
+        return carry
+
+    lax.fori_loop(0, 8, kept, 0)
     for j in range(half):
         swap(j, k).wait_send()
     for g in gives:
@@ -748,7 +846,7 @@
     outs += [sds((LENGTH, LANE), F32)] * 2 + [sds((tokens, LANE), F32)]
     outs += [sds((4, tokens, 2 * LANE), BF), sds((2, 8, 1, PIECE), F32)]
     outs += [sds((tokens, width), F32), sds((tokens, LANE), F32)]
-    outs += [sds((4, tokens, f_half), BF)] * 3 + [sds((DOWN_CHUNKS, CHUNK, WIDE), BF)]
+    outs += [sds((DOWN_CHUNKS, CHUNK, WIDE), BF)] + [sds((4, tokens, f_half), BF)] * 3
     half = DOWN_CHUNKS // 4
     scratch = [pltpu.VMEM(gathered, BF)] * 2 + [pltpu.VMEM((2, 2, PIECE, width), BF)]
     scratch += [pltpu.VMEM((2, 1, width), F32), pltpu.VMEM((width, cols), BF), pltpu.VMEM((2 * LANE, width), BF)]
@@ -756,11 +854,13 @@
     scratch += [DMA((6,)), DMA((6,)), DMA((8,)), DMA((8,)), DMA((8,))]
     scratch += [pltpu.VMEM((2, tokens, LANE), F32), DMA((2,)), pltpu.VMEM((2, f_half, width), F32)]
     scratch += [pltpu.VMEM((2 * half, CHUNK, WIDE), BF), DMA((half,)), DMA((half,))]
+    scratch += [pltpu.VMEM((4, tokens, f_half), BF)] * 3 + [DMA((3, 8))]
     scratch += GATHER_SEMS * 3 + sum_scratch(width)
     ins = [ANY] * 2 + [VM] * 2 + [ANY] * 7 + [VM]
     args = [x, dy, gain, gain_f, wq, wk, wv, wo, wg, wu, wd, jnp.asarray(np.stack(angle_tables()))]
-    out_specs = [ANY] * 2 + [VM] * (len(outs) - 2)
-    return call(front_kernel, 0, outs, ins, args, scratch, 9e10, 60, out_specs)
+    out_specs = [ANY] * 2 + [VM] * (len(outs) - 5) + [ANY] * 3
+    spill = [2, 3, 4, 5, 6, 7, 8, 9, 10, 12, 14, 16]
+    return call(front_kernel, 0, outs, ins, args, scratch, 9e10, 61, out_specs, [], spill)
 
 
 TICKS = 35
@@ -772,6 +872,7 @@
 
 
 def contract_kernel(
+    io,
     d_gate, d_up, wg, wu, hidden, rstd2, gain, dy, wo, attn, part_d, f_any,
     d_hidden, gains_o, part, part_o, d_attn, totals, acc_c, tot_c,
     stat, ssem, give, gsend, grecv, gathered, dya, grad, give_o, his_o, gsem, fsem, *rest,
@@ -779,13 +880,15 @@
     r, k, rx, ry, r3 = place()
     width = hidden.shape[1]
     fetch = pltpu.make_async_copy(f_any, gathered, fsem)
-    fetch.start()
     greet(rx, ry, k, True)
     total = Sum(rest[:9])
     gather = Gather(dya, gathered, rest[9:14])
     parts = [(0, DOWN_CHUNKS, part_d), (DOWN_CHUNKS, MLP_CHUNKS, part), (MLP_CHUNKS, OUT_CHUNKS, part_o)]
     line = Line(parts, totals, (acc_c, tot_c), rest[14:], 0, TICKS)
+    io.need(d_gate, d_up, wg, wu, part_d)
     line.open()
+    fetch.start()
+    io.more()
 
     def compute(row, half):
         at = rows_of(half)
@@ -820,28 +923,26 @@
     wide_part(1 - k, d_gate, give, 0)
     for e in range(4):
         swap(e, k).start()
-    line.step(4)
     wide_part(k, d_gate, part, 4 * k)
-    line.step(5)
+    line.steps(4, 6)
     wide_part(1 - k, d_up, give, 4)
     for e in range(4, 8):
         swap(e, k).start()
-    line.step(6)
     wide_part(k, d_up, part, 8 + 4 * k)
-    line.step(7)
     total.relay(4)
     total.relay(5)
     for e in range(8):
         swap(e, 1 - k).wait_recv()
-    for j in range(8, 13):
-        line.step(j)
+    io.spill(part)
+    io.need(hidden, dy, wo, attn)
+    line.steps(6, 13)
     gains = jnp.zeros((1, width), F32)
     for half in range(2):
         at = rows_of(half)
         d_nf = total.last(6 + half)
         h = hidden[at, :]
         gains = gains + jnp.sum(d_nf * h * rstd2[at, 0:1], 0, keepdims=True)
-        scaled = d_nf * gain[...]
+        scaled = d_nf * gain[...].reshape(1, width)
         d_hidden[at, :] = scaled
         stat[k, at, :] = jnp.broadcast_to(jnp.sum(scaled * h, 1, keepdims=True), (PIECE, LANE))
     gains_o[...] = gains
@@ -851,6 +952,7 @@
     d_hidden[...] = value
     dya[...] = value.astype(BF)
     gather.start()
+    io.spill(d_hidden)
 
     def piece(i, row, half):
         at = rows_of(half)
@@ -870,13 +972,7 @@
             grad[1] += g1
 
     def before(q):
-        @pl.when(q == 0)
-        def _():
-            for j in range(13, 15):
-                line.step(j)
-
-        for j in range(3):
-            line.step(15 + 4 * q + j)
+        line.steps(jnp.where(q == 0, 13, 15 + 4 * q), 18 + 4 * q)
 
     def after(q):
         line.step(18 + 4 * q)
@@ -913,7 +1009,10 @@
     scratch += sum_scratch(width) + GATHER_SEMS + line_scratch(n, TICKS)
     args = [d_gate, d_up, wg, wu, hidden, rstd2, gain, dy, wo, attn, part_d, all_f]
     ins = [VM] * 11 + [ANY]
-    return call(contract_kernel, 3, outs, ins, args, scratch, 5e10, vmem_limit(n), out_specs)
+    fetch = [0, 1, 2, 3, 10, 4, 7, 8, 9]
+    return call(
+        contract_kernel, 1, outs, ins, args, scratch, 5e10, vmem_limit(n), out_specs, fetch, [0, 2, 3, 4], 5
+    )
 
 
 def vmem_limit(n):
@@ -934,6 +1033,7 @@
 
 def backward_kernel(
     q_cols, k_cols,
+    io,
     qkv, kvt, lse, d_attn, cos, sin, middle, wd, hidden, wqkv, x, rstd1, d_hidden, gain, gains_f,
     part_m, part_o, acc_c, tot_c, normed_any,
     output, grad_x, gains_o, totals,
@@ -945,7 +1045,6 @@
     n = lax.axis_size("dp")
     z = lax.axis_index("dp")
     fetch = pltpu.make_async_copy(normed_any, normed, fsem)
-    fetch.start()
     greet(rx, ry, k, True, True)
     sums = rest[:5]
     down = Sum(sums + rest[5:9])
@@ -953,7 +1052,9 @@
     ticks = line_ticks(n) - TICKS
     parts = [(DOWN_CHUNKS, MLP_CHUNKS, part_m), (MLP_CHUNKS, OUT_CHUNKS, part_o), (OUT_CHUNKS, ALL_CHUNKS, part)]
     line = Line(parts, totals, None, rest[13:], TICKS, ticks, (acc_c, tot_c))
+    io.need(part_m, part_o, middle, wd)
     line.open()
+    io.more()
 
     def down_piece(row, half):
         m = middle[row, rows_of(half), :]
@@ -965,6 +1066,9 @@
             line.step(j // 3)
 
     down.send_all(down_piece, early)
+
+    fetch.start()
+    io.need(qkv, kvt, d_attn, cos, sin)
 
     def unrotate(u, p):
         at = pl.ds(p * PIECE, PIECE)
@@ -993,12 +1097,9 @@
                 dk[0:span, :] += nn(ds, q)
                 dq = nn(kvt[0, :, pl.ds(base, span)], ds).T * SCALE
                 d_proj[out, lane] = unrotate(dq, p).astype(BF)
-                tick = 3 + seq * 8 + head * 4 + p
-
-                @pl.when(tick < OUT_CHUNKS - LAG - TICKS)
-                def _(tick=tick):
-                    line.step(tick)
-
+                if p % 2 == 1:
+                    tick = 3 + seq * 8 + head * 4 + p - 1
+                    line.steps(tick, jnp.minimum(tick + 2, OUT_CHUNKS - LAG - TICKS))
             return carry
 
         dk[...] = jnp.zeros_like(dk)
@@ -1021,10 +1122,12 @@
         return carry
 
     lax.fori_loop(0, 2, both, 0)
+    io.need(hidden)
     for half in range(2):
         at = rows_of(half)
         output[at, :] = hidden[at, :] + down.last(6 + half)
     down.finish()
+    io.spill(output)
     for device in ({"row": rx}, {"row": ry}, {"col": 1 - k}):
         pl.semaphore_signal(free, inc=1, device_id=device, device_id_type=MESH)
     pl.semaphore_wait(free, 3)
@@ -1058,20 +1161,20 @@
         def _():
             line.step(17 + j // 2)
 
+    io.need(wqkv)
     into.send_all(into_piece, beside)
-    for j in range(21, 24):
-        line.step(j)
+    line.steps(21, 24)
     into.relay(4)
     into.relay(5)
-    for j in range(24, 29):
-        line.step(j)
+    line.steps(24, 29)
+    io.need(x, d_hidden)
     gains = jnp.zeros((1, width), F32)
     for half in range(2):
         at = rows_of(half)
         d_na = into.last(6 + half)
         xs = x[at, :].astype(F32)
         gains = gains + jnp.sum(d_na * xs * rstd1[at, 0:1], 0, keepdims=True)
-        scaled = d_na * gain[...]
+        scaled = d_na * gain[...].reshape(1, width)
         grad_x[at, :] = scaled
         stat[k, at, :] = jnp.broadcast_to(jnp.sum(scaled * xs, 1, keepdims=True), (PIECE, LANE))
 
@@ -1102,6 +1205,7 @@
         return carry
 
     lax.fori_loop(1, n, start, 0)
+    io.spill(grad_x)
     line.rest(29)
 
     def wait(t, carry):
@@ -1137,7 +1241,10 @@
     args += [part_m, part_o, acc, tot, normed]
     kernel = functools.partial(backward_kernel, q_cols, k_cols)
     ins = [VM] * (len(args) - 1) + [ANY]
-    return call(kernel, 5, outs, ins, args, scratch, 5e10, vmem_limit(n), [VM] * 3 + [ANY])
+    fetch = [15, 16, 6, 7, 0, 1, 3, 4, 5, 8, 9, 10, 12]
+    return call(
+        kernel, 2, outs, ins, args, scratch, 5e10, vmem_limit(n), [VM] * 3 + [ANY], fetch, [0, 1], 4
+    )
 
 
 def unpack_kernel(ticks, q_cols, k_cols, *rest):
@@ -1236,10 +1343,10 @@
 ):
     tokens, width = layer_input.shape
     q_cols, k_cols = w_query.shape[1], w_key.shape[1]
-    gain_a, gain_f = gain_attn[None], gain_ffn[None]
+    gain_a, gain_f = gain_attn, gain_ffn
     (
         normed, all_f, qkv, kvt, wqkv, wo, wg, wu, wd, cos, sin, rstd1,
-        attn, lse, hidden, rstd2, middle, d_gate, d_up, part_d,
+        attn, lse, hidden, rstd2, part_d, middle, d_gate, d_up,
     ) = front(
         layer_input, cotangent, gain_a, gain_f,
         w_query, w_key.T, w_value.T, w_out, w_gate, w_up, w_down,

time: 370 us -> 359 us (0.970)
  Pallas kernels: 355 us -> 349 us
    pallas_call x3, Pallas kernels: 344 us -> 337 us  [call(): pl.pallas_call(staged(kernel, len(args), fetch, spill, early), out_shape=...]
where the time goes in v4:
time: 359 us; the launch traced here: 356 us
  Pallas kernels  349 us (97%)
  local copies, waits for them, and re-layouts  6.48 us (2%)
    pallas_call x3, Pallas kernels, call(): pl.pallas_call(staged(kernel, len(args), fetch, spill, early), out_shape=...  337 us
    pallas_call x1, Pallas kernels, unpack(): pl.pallas_call(functools.partial(unpack_kernel, ticks, q_cols, k_cols), o...  11.3 us

profile of v4, /device:TPU:0, one launch (start us, length us, event | category | flops | bytes accessed | tf_op | source)
XLA Modules:
  0.0 356.2 jit_solution(11151382165146010801)
XLA Ops:
  0.6 123.8 %shard_map.203 = (bf16[2,4,512,768]{3,2,1,0:T(8,128)(2,1)}, bf16[2,4,512,768]{3,2,1,0:T(8,128)(2,1)}, bf16[4,2048,128]{2,1,0:T(8,128)(2,1)}, bf16[2,128,2048]{2,...) custom-call(bf16[512,768]{1,0:T(8,128)(2,1)} %refs_10_.3, ...), custom_call_target="tpu_custom_call" | custom-call | flops 89999998976 | bytes 43014144 | tf_op jit(solution)/shard_map/pallas_call | solution.py:514
  124.4 98.6 %shard_map.204 = (f32[512,768]{1,0:T(8,128)}, f32[1,768]{1,0:T(1,128)}, bf16[32,64,768]{2,1,0:T(8,128)(2,1)}, bf16[6,64,768]{2,1,0:T(8,128)(2,1)}, bf16[4,512,25...) custom-call(bf16[4,512,512]{2,1,0:T(8,128)(2,1)} %get-tuple-element.5, ...), custom_call_target="tpu_custom_call" | custom-call | flops 49999998976 | bytes 29857792 | tf_op jit(solution)/shard_map/pallas_call | solution.py:514
  223.0 0.0 copy-start
  223.0 115.1 %shard_map.205 = (f32[512,768]{1,0:T(8,128)}, f32[512,768]{1,0:T(8,128)}, f32[2,768]{1,0:T(2,128)}, bf16[35,64,768]{2,1,0:T(8,128)(2,1)}) custom-call(bf16[4,2048,128]{2,1,0:T(8,128)(2,1)} %get-tuple-element.50.refs_0_, bf16[2,128,2048]{2,1,0:T(8,128)(2,1)} %get-tuple-element.51.refs_1_, f32[2,8,1,256]{3,2,1,0:T(1,128)} %get-tuple-element.52.refs_2_, ...), custom_call_target="tpu_custom_call" | custom-call | flops 49999998976 | bytes 31715328 | tf_op jit(solution)/shard_map/pallas_call | solution.py:514
  338.2 1.4 slice_reduce_fusion
  339.5 0.0 copy-done
  339.6 0.0 copy-start.1
  339.6 2.0 copy-done.1
  341.5 0.0 copy-start.3
  341.5 11.3 %shard_map.206 = (f32[1024,768]{1,0:T(8,128)}, f32[768,1024]{1,0:T(8,128)}, f32[768,1024]{1,0:T(8,128)}, f32[384,768]{1,0:T(8,128)}, f32[768,384]{1,0:T(8,128)}, /*index=5*/f32[192,768]{1,0:T(8,128)}, f32[192,768]{1,0:T(8,128)}) custom-call(bf16[35,64,768]{2,1,0:T(8,128)(2,1)S(1)} %copy-done, bf16[35,64,768]{2,1,0:T(8,128)(2,1)S(1)} %copy-done.1), custom_call_target="tpu_custom_call" | custom-call | bytes 19464192 | tf_op jit(solution)/shard_map/pallas_call | solution.py:1324
  352.9 0.0 copy-done.3
  352.9 0.0 copy-start.2
  352.9 1.1 copy.25
  354.0 0.8 copy-done.2
  354.9 1.1 copy.26
Async XLA Ops:
  223.0 116.5 %copy-start = (bf16[35,64,768]{2,1,0:T(8,128)(2,1)S(1)}, bf16[35,64,768]{2,1,0:T(8,128)(2,1)}, u32[]{:S(2)}) copy-start(bf16[35,64,768]{2,1,0:T(8,128)(2,1)} %get-tuple-element.80.rest_0_) | copy-start | bytes 10321924
  339.6 2.0 copy-start.1
  341.5 11.3 %copy-start.3 = (f32[512,768]{1,0:T(8,128)S(1)}, f32[512,768]{1,0:T(8,128)}, u32[]{:S(2)}) copy-start(f32[512,768]{1,0:T(8,128)} %get-tuple-element.102) | copy-start | bytes 4718596
  352.9 2.0 copy-start.2

commit v5 on v4

--- a/solution.py
+++ b/solution.py
@@ -270,51 +270,54 @@
 TALL, WIDE = 128, 768
 CHUNK = TALL // 2
 DOWN_CHUNKS, MLP_CHUNKS, OUT_CHUNKS, ALL_CHUNKS = 16, 48, 54, 66
-RING = 6
-LAG = 2
-
-
-def line_ring(n):
-    return LAG * (2 * (n // 2) - 2) + 6
-
-
-def line_ticks(n):
-    return ALL_CHUNKS + LAG * (2 * (n // 2) - 2)
-
-
-def line_outs(ticks):
-    return [sds((ticks, CHUNK, WIDE), BF)] + [sds((LAG, CHUNK, WIDE), BF)] * 2
-
-
-def line_scratch(n, ticks):
-    slots = (RING, line_ring(n), line_ring(n), RING)
+
+
+def lags(n):
+    return (4, 2) if n <= 4 else (2, 1)
+
+
+def line_ring(n, lag):
+    return lag * (2 * (n // 2) - 2) + lag + 4
+
+
+def line_ticks(n, count, lag):
+    return count + lag * (2 * (n // 2) - 2)
+
+
+def line_outs(ticks, lag):
+    return [sds((ticks, CHUNK, WIDE), BF)] + [sds((lag, CHUNK, WIDE), BF)] * 2
+
+
+def line_scratch(n, ticks, lag):
+    near, far = 2 * lag + 2, line_ring(n, lag)
+    slots = (near, far, far, near)
     return [pltpu.VMEM((count, CHUNK, WIDE), BF) for count in slots] + [DMA((ticks,))] * 6
 
 
 class Line:
-    def __init__(self, parts, totals, carry, scratch, first, ticks, before=None):
+    def __init__(self, parts, totals, carry, scratch, first, ticks, count, lag, before=None):
         self.parts, self.totals, self.carry = parts, totals, carry
         self.acc, self.tot, self.rin, self.rxb = scratch[:4]
         self.si, self.ri, self.rx, self.so, self.ro, self.out_sem = scratch[4:]
-        self.first, self.ticks = first, ticks
+        self.first, self.ticks, self.count, self.lag, self.near = first, ticks, count, lag, 2 * lag + 2
         self.n, self.s, self.inward, self.outward = line_place()
         self.mid = self.n // 2
-        self.ring = line_ring(self.n)
+        self.ring = line_ring(self.n, lag)
         if before is not None:
 
             @pl.when(self.s > 0)
             def _():
-                for b in range(LAG):
+                for b in range(self.lag):
                     self.acc[b] = before[0][b]
                     self.tot[b] = before[1][b]
 
     def valid(self, c):
-        return (c >= 0) & (c < ALL_CHUNKS)
+        return (c >= 0) & (c < self.count)
 
     def sends(self, j):
-        s, mid, slot, near = self.s, self.mid, j % self.ring, j % RING
+        s, mid, slot, near = self.s, self.mid, j % self.ring, j % self.near
         to = {"dp": self.inward}
-        c = self.first + j - LAG * s
+        c = self.first + j - self.lag * s
         moves = []
         inward = (self.rin.at[slot], self.ri.at[j])
         across = (self.rxb.at[near], self.rx.at[j])
@@ -331,13 +334,13 @@
             for cond, ref, at, way in moves
         ]
         if mid > 1:
-            c = self.first + j - LAG * (2 * mid - 1 - s)
+            c = self.first + j - self.lag * (2 * mid - 1 - s)
             out.append(((s > 0) & self.valid(c), lambda: self.outer(j)))
         return out
 
     def outer(self, j):
         return remote(
-            self.tot.at[j % self.ring], self.tot.at[(j + LAG) % self.ring],
+            self.tot.at[j % self.ring], self.tot.at[(j + self.lag) % self.ring],
             self.so.at[j], self.ro.at[j], {"dp": self.outward},
         )
 
@@ -350,9 +353,9 @@
 
     def total_of(self, j):
         copy = lambda: pltpu.make_async_copy(
-            self.tot.at[(j + LAG) % self.ring], self.totals.at[j], self.out_sem.at[j]
+            self.tot.at[(j + self.lag) % self.ring], self.totals.at[j], self.out_sem.at[j]
         )
-        return self.valid(self.first + j - LAG * (2 * self.mid - 2 - self.s)), copy
+        return self.valid(self.first + j - self.lag * (2 * self.mid - 2 - self.s)), copy
 
     def settle(self, j):
         for cond, copy in self.sends(j):
@@ -369,8 +372,8 @@
 
     def end(self, j):
         t, s, mid = self.first + j, self.s, self.mid
-        slot, later = j % self.ring, (j + LAG) % self.ring
-        near, next_near = j % RING, (j + LAG) % RING
+        slot, later = j % self.ring, (j + self.lag) % self.ring
+        near, next_near = j % self.near, (j + self.lag) % self.near
 
         @pl.when(j >= 2)
         def _():
@@ -387,14 +390,14 @@
                     dst[to] = (ref[c - lo].astype(F32) + buf[at].astype(F32)).astype(BF)
 
         if mid > 1:
-            c = t - LAG * (s - 1)
+            c = t - self.lag * (s - 1)
 
             @pl.when((s > 0) & self.valid(c))
             def _():
                 came(self.rin, slot, self.ri)
                 add_part(c, self.rin, slot, self.acc, next_near)
 
-        @pl.when((s == mid - 1) & self.valid(t - LAG * (mid - 1)))
+        @pl.when((s == mid - 1) & self.valid(t - self.lag * (mid - 1)))
         def _():
             came(self.rxb, near, self.rx)
             if mid > 1:
@@ -418,14 +421,14 @@
             self.begin(j)
             return carry
 
-        lax.fori_loop(0, min(LAG, self.ticks), one, 0)
+        lax.fori_loop(0, min(self.lag, self.ticks), one, 0)
 
     def step(self, j):
         self.end(j)
 
-        @pl.when(j + LAG < self.ticks)
-        def _():
-            self.begin(j + LAG)
+        @pl.when(j + self.lag < self.ticks)
+        def _():
+            self.begin(j + self.lag)
 
     def steps(self, start, stop):
         def one(t, carry):
@@ -443,8 +446,8 @@
 
         lax.fori_loop(max(self.ticks - 2, 0), self.ticks, settle, 0)
         if self.carry is not None:
-            for b in range(LAG):
-                self.carry[0][b] = self.acc[(self.ticks + b) % RING]
+            for b in range(self.lag):
+                self.carry[0][b] = self.acc[(self.ticks + b) % self.near]
                 self.carry[1][b] = self.tot[(self.ticks + b) % self.ring]
 
 
@@ -863,7 +866,7 @@
     return call(front_kernel, 0, outs, ins, args, scratch, 9e10, 61, out_specs, [], spill)
 
 
-TICKS = 35
+TICKS = 34
 
 
 def flat(ref, h, m=None):
@@ -884,7 +887,8 @@
     total = Sum(rest[:9])
     gather = Gather(dya, gathered, rest[9:14])
     parts = [(0, DOWN_CHUNKS, part_d), (DOWN_CHUNKS, MLP_CHUNKS, part), (MLP_CHUNKS, OUT_CHUNKS, part_o)]
-    line = Line(parts, totals, (acc_c, tot_c), rest[14:], 0, TICKS)
+    lag = lags(lax.axis_size("dp"))[0]
+    line = Line(parts, totals, (acc_c, tot_c), rest[14:], 0, TICKS, OUT_CHUNKS, lag)
     io.need(d_gate, d_up, wg, wu, part_d)
     line.open()
     fetch.start()
@@ -972,12 +976,9 @@
             grad[1] += g1
 
     def before(q):
-        line.steps(jnp.where(q == 0, 13, 15 + 4 * q), 18 + 4 * q)
-
-    def after(q):
-        line.step(18 + 4 * q)
-
-    gather.run(piece, before, after)
+        line.steps(jnp.where(q == 0, 13, 15 + 4 * q), 19 + 4 * q)
+
+    gather.run(piece, before)
     give_o[...] = grad[1 - k].astype(BF)
     give_out = remote(give_o, his_o, gsem.at[0], gsem.at[1], {"col": 1 - k})
     give_out.start()
@@ -999,14 +1000,14 @@
     n = lax.axis_size("dp")
     outs = [sds((tokens, width), F32), sds((1, width), F32)]
     outs += [sds((MLP_CHUNKS - DOWN_CHUNKS, CHUNK, WIDE), BF), sds((OUT_CHUNKS - MLP_CHUNKS, CHUNK, WIDE), BF)]
-    outs += [sds((4, tokens, 2 * LANE), BF)] + line_outs(TICKS)
+    outs += [sds((4, tokens, 2 * LANE), BF)] + line_outs(TICKS, lags(n)[0])
     out_specs = [VM] * 5 + [ANY] + [VM] * 2
     scratch = [pltpu.VMEM((2, tokens, LANE), F32), DMA((2,))]
     scratch += [pltpu.VMEM((16, CHUNK, WIDE), BF), DMA((8,)), DMA((8,))]
     scratch += [pltpu.VMEM((2, 4, tokens, width), BF), pltpu.VMEM((tokens, width), BF)]
     scratch += [pltpu.VMEM((2, 2 * LANE, width), F32)] + [pltpu.VMEM((2 * LANE, width), BF)] * 2
     scratch += [DMA((2,)), DMA]
-    scratch += sum_scratch(width) + GATHER_SEMS + line_scratch(n, TICKS)
+    scratch += sum_scratch(width) + GATHER_SEMS + line_scratch(n, TICKS, lags(n)[0])
     args = [d_gate, d_up, wg, wu, hidden, rstd2, gain, dy, wo, attn, part_d, all_f]
     ins = [VM] * 11 + [ANY]
     fetch = [0, 1, 2, 3, 10, 4, 7, 8, 9]
@@ -1036,7 +1037,7 @@
     io,
     qkv, kvt, lse, d_attn, cos, sin, middle, wd, hidden, wqkv, x, rstd1, d_hidden, gain, gains_f,
     part_m, part_o, acc_c, tot_c, normed_any,
-    output, grad_x, gains_o, totals,
+    output, grad_x, gains_o, totals, totals_in,
     dk, dv, d_proj, normed, part, mine, give, his, gsem, stat, ssem, free, fsem,
     mine_g, pair_g, slots, gsend, grecv, *rest,
 ):
@@ -1049,9 +1050,12 @@
     sums = rest[:5]
     down = Sum(sums + rest[5:9])
     into = Sum(sums + rest[9:13])
-    ticks = line_ticks(n) - TICKS
-    parts = [(DOWN_CHUNKS, MLP_CHUNKS, part_m), (MLP_CHUNKS, OUT_CHUNKS, part_o), (OUT_CHUNKS, ALL_CHUNKS, part)]
-    line = Line(parts, totals, None, rest[13:], TICKS, ticks, (acc_c, tot_c))
+    lag, lag_in = lags(n)
+    count = ALL_CHUNKS - OUT_CHUNKS
+    ticks, ticks_in = line_ticks(n, OUT_CHUNKS, lag) - TICKS, line_ticks(n, count, lag_in)
+    parts = [(DOWN_CHUNKS, MLP_CHUNKS, part_m), (MLP_CHUNKS, OUT_CHUNKS, part_o)]
+    line = Line(parts, totals, None, rest[13:23], TICKS, ticks, OUT_CHUNKS, lag, (acc_c, tot_c))
+    line_in = Line([(0, count, part)], totals_in, None, rest[23:], 0, ticks_in, count, lag_in)
     io.need(part_m, part_o, middle, wd)
     line.open()
     io.more()
@@ -1099,7 +1103,7 @@
                 d_proj[out, lane] = unrotate(dq, p).astype(BF)
                 if p % 2 == 1:
                     tick = 3 + seq * 8 + head * 4 + p - 1
-                    line.steps(tick, jnp.minimum(tick + 2, OUT_CHUNKS - LAG - TICKS))
+                    line.steps(tick, tick + 2)
             return carry
 
         dk[...] = jnp.zeros_like(dk)
@@ -1144,7 +1148,9 @@
     in_part(1 - k, give)
     swap = remote(give, his, gsem.at[0], gsem.at[1], {"col": 1 - k})
     swap.start()
+    line.steps(19, 21)
     in_part(k, mine)
+    line.steps(21, 23)
     cols = q_cols + 2 * k_cols
     got = nn(mine[...], columns(4 * LANE, cols, k, q_cols, k_cols))
     swap.wait_recv()
@@ -1156,17 +1162,25 @@
         d = d_proj[pl.ds(pl.multiple_of(row * 2 * PIECE + half * PIECE, PIECE), PIECE), :]
         return nt(d, wqkv[k]), nt(d, wqkv[1 - k])
 
+    line_in.open()
+
+    def both_lines(t, carry):
+        line.step(23 + t)
+        line_in.step(t)
+        return carry
+
     def beside(j):
         @pl.when(j % 2 == 1)
         def _():
-            line.step(17 + j // 2)
+            both_lines(j // 2, 0)
 
     io.need(wqkv)
     into.send_all(into_piece, beside)
-    line.steps(21, 24)
+    lax.fori_loop(4, 5, both_lines, 0)
+    line_in.steps(5, 7)
     into.relay(4)
     into.relay(5)
-    line.steps(24, 29)
+    line_in.steps(7, 12)
     io.need(x, d_hidden)
     gains = jnp.zeros((1, width), F32)
     for half in range(2):
@@ -1206,7 +1220,8 @@
 
     lax.fori_loop(1, n, start, 0)
     io.spill(grad_x)
-    line.rest(29)
+    line_in.rest(12)
+    line.rest(28)
 
     def wait(t, carry):
         over_dp(t, False).wait_recv()
@@ -1227,8 +1242,11 @@
 ):
     tokens, width = x.shape
     n = lax.axis_size("dp")
-    ticks = line_ticks(n) - TICKS
-    outs = [sds((tokens, width), F32)] * 2 + [sds((2, width), F32), sds((ticks, CHUNK, WIDE), BF)]
+    lag, lag_in = lags(n)
+    ticks = line_ticks(n, OUT_CHUNKS, lag) - TICKS
+    ticks_in = line_ticks(n, ALL_CHUNKS - OUT_CHUNKS, lag_in)
+    outs = [sds((tokens, width), F32)] * 2 + [sds((2, width), F32)]
+    outs += [sds((t, CHUNK, WIDE), BF) for t in (ticks, ticks_in)]
     scratch = [pltpu.VMEM((LENGTH, LANE), F32)] * 2 + [pltpu.VMEM((4 * tokens, 4 * LANE), BF)]
     scratch += [pltpu.VMEM((2, 4, tokens, width), BF), pltpu.VMEM((ALL_CHUNKS - OUT_CHUNKS, CHUNK, WIDE), BF)]
     scratch += [pltpu.VMEM((width, 4 * LANE), BF)] * 3 + [DMA((2,))]
@@ -1236,105 +1254,131 @@
     scratch += [pltpu.VMEM((2, 2, width), F32)] * 2 + [pltpu.VMEM((n, 2, width), F32)]
     scratch += [DMA((n + 2,)), DMA((n + 2,))]
     both = sum_scratch(width)
-    scratch += both + both[5:] + line_scratch(n, ticks)
+    scratch += both + both[5:] + line_scratch(n, ticks, lag) + line_scratch(n, ticks_in, lag_in)
     args = [qkv, kvt, lse, d_attn, cos, sin, middle, wd, hidden, wqkv, x, rstd1, d_hidden, gain, gains_f]
     args += [part_m, part_o, acc, tot, normed]
     kernel = functools.partial(backward_kernel, q_cols, k_cols)
     ins = [VM] * (len(args) - 1) + [ANY]
     fetch = [15, 16, 6, 7, 0, 1, 3, 4, 5, 8, 9, 10, 12]
     return call(
-        kernel, 2, outs, ins, args, scratch, 5e10, vmem_limit(n), [VM] * 3 + [ANY], fetch, [0, 1], 4
+        kernel, 2, outs, ins, args, scratch, 5e10, vmem_limit(n), [VM] * 3 + [ANY] * 2, fetch, [0, 1], 4
     )
 
 
-def unpack_kernel(ticks, q_cols, k_cols, *rest):
-    tots, (down, gate, up, out, q_o, k_o, v_o), rest = rest[: len(ticks)], rest[len(ticks) : len(ticks) + 7], rest[len(ticks) + 7 :]
-    chunks, wide, parts, isem, osem = rest
+SLOTS = 4
+
+
+def unpack_kernel(q_cols, k_cols, tot1, tot2, tot3, down, gate, up, out, q_o, k_o, v_o, whole, last, wide, turned, isem, osem):
     n, s, _, _ = line_place()
-    mid = n // 2
-    off = LAG * (2 * mid - 2 - s)
-    offs = [LAG * o for o in range(mid - 1, 2 * mid - 1)]
-
-    def source(t):
-        for tot, count in zip(tots, ticks):
-            if t < count:
-                return tot.at[t]
-            t -= count
-
-    def load(c):
-        for o in offs:
-
-            @pl.when(off == o)
-            def _(o=o):
+    steps = 2 * (n // 2) - 2 - s
+    lag, lag_in = lags(n)
+    first = tot1.shape[0]
+    loads = [
+        pltpu.make_async_copy(tot1, whole.at[pl.ds(0, first)], isem.at[0]),
+        pltpu.make_async_copy(tot2, whole.at[pl.ds(first, tot2.shape[0])], isem.at[1]),
+        pltpu.make_async_copy(tot3, last, isem.at[2]),
+    ]
+    for c in loads:
+        c.start()
+    loads[0].wait()
+    late = whole.shape[0] - OUT_CHUNKS > first - DOWN_CHUNKS
+    if late:
+        loads[1].wait()
+
+    def chunk(c, lanes):
+        return whole[c + lag * steps, :, lanes].astype(F32)
+
+    def run(count, make, copies):
+        def one(b, carry):
+            slot = b % SLOTS
+
+            @pl.when(b >= SLOTS)
+            def _():
+                for c in copies(b - SLOTS, slot):
+                    c.wait()
+
+            make(b, slot)
+            for c in copies(b, slot):
+                c.start()
+            return carry
+
+        lax.fori_loop(0, count, one, 0)
+
+        def drain(b, carry):
+            for c in copies(b, b % SLOTS):
+                c.wait()
+            return carry
+
+        lax.fori_loop(max(count - SLOTS, 0), count, drain, 0)
+
+    def rows(b):
+        return pl.ds(pl.multiple_of(b * TALL, TALL), TALL)
+
+    def tall(start, to, count):
+        def make(b, slot):
+            for u in range(2):
+                wide[slot, u * CHUNK : (u + 1) * CHUNK, 0:WIDE] = chunk(start + 2 * b + u, slice(0, WIDE))
+
+        def copies(b, slot):
+            return [pltpu.make_async_copy(wide.at[slot, :, pl.ds(0, WIDE)], to.at[rows(b)], osem.at[slot, 0])]
+
+        run(count, make, copies)
+
+    def broad(start, to):
+        def make(b, slot):
+            for c in range(8):
                 for u in range(2):
-                    dst = chunks.at[c % 4, pl.ds(u * CHUNK, CHUNK)]
-                    pltpu.make_async_copy(source(2 * c + u + o), dst, isem.at[c % 4, u]).start()
-
-    def stored(c):
-        slot = c % 4
-        buf = wide.at[slot]
-        if c < 8:
-            return [pltpu.make_async_copy(buf, down.at[pl.ds(c * TALL, TALL)], osem.at[slot, 0])]
-        if c < MLP_CHUNKS // 2:
-            to, lanes = (gate, up)[c // 8 - 1], pl.ds(c % 8 * TALL, TALL)
-            return [
-                pltpu.make_async_copy(
-                    buf.at[:, pl.ds(b * TALL, TALL)], to.at[pl.ds(b * TALL, TALL), lanes], osem.at[slot, b]
-                )
-                for b in range(WIDE // TALL)
-            ]
-        if c < OUT_CHUNKS // 2:
-            return [pltpu.make_async_copy(buf, out.at[pl.ds((c - MLP_CHUNKS // 2) * TALL, TALL)], osem.at[slot, 0])]
-        rows = pl.ds((c - OUT_CHUNKS // 2) * TALL, TALL)
+                    got = chunk(start + 2 * c + u, rows(b))
+                    wide[slot, u * CHUNK : (u + 1) * CHUNK, c * TALL : (c + 1) * TALL] = got
+
+        def copies(b, slot):
+            return [pltpu.make_async_copy(wide.at[slot], to.at[rows(b)], osem.at[slot, 0])]
+
+        run(WIDE // TALL, make, copies)
+
+    tall(0, down, 8)
+    if not late:
+        loads[1].wait()
+    broad(DOWN_CHUNKS, gate)
+    broad(DOWN_CHUNKS + 16, up)
+    tall(MLP_CHUNKS, out, q_cols // TALL)
+    loads[2].wait()
+
+    def make_in(b, slot):
+        for u in range(2):
+            got = last[2 * b + u + lag_in * steps].astype(F32)
+            wide[slot, u * CHUNK : (u + 1) * CHUNK, 0:WIDE] = got
+        turned[slot, 0] = wide[slot, :, q_cols : q_cols + k_cols].T
+        turned[slot, 1] = wide[slot, :, q_cols + k_cols : WIDE].T
+
+    def copies_in(b, slot):
         return [
-            pltpu.make_async_copy(buf.at[:, pl.ds(0, q_cols)], q_o.at[rows], osem.at[slot, 0]),
-            pltpu.make_async_copy(parts.at[0, slot], k_o.at[:, rows], osem.at[slot, 1]),
-            pltpu.make_async_copy(parts.at[1, slot], v_o.at[:, rows], osem.at[slot, 2]),
+            pltpu.make_async_copy(wide.at[slot, :, pl.ds(0, q_cols)], q_o.at[rows(b)], osem.at[slot, 0]),
+            pltpu.make_async_copy(turned.at[slot, 0], k_o.at[:, rows(b)], osem.at[slot, 1]),
+            pltpu.make_async_copy(turned.at[slot, 1], v_o.at[:, rows(b)], osem.at[slot, 2]),
         ]
 
-    for c in range(3):
-        load(c)
-    for c in range(ALL_CHUNKS // 2):
-        if c + 3 < ALL_CHUNKS // 2:
-            load(c + 3)
-        if c >= 4:
-            for copy in stored(c - 4):
-                copy.wait()
-        for u in range(2):
-            dst = chunks.at[c % 4, pl.ds(u * CHUNK, CHUNK)]
-            pltpu.make_async_copy(dst, dst, isem.at[c % 4, u]).wait()
-        value = chunks[c % 4].astype(F32)
-        wide[c % 4] = value
-        if c >= OUT_CHUNKS // 2:
-            parts[0, c % 4] = value[:, q_cols : q_cols + k_cols].T
-            parts[1, c % 4] = value[:, q_cols + k_cols :].T
-        for copy in stored(c):
-            copy.start()
-    for c in range(ALL_CHUNKS // 2 - 4, ALL_CHUNKS // 2):
-        for copy in stored(c):
-            copy.wait()
+    run(WIDE // TALL, make_in, copies_in)
 
 
 def unpack(tots, q_cols, k_cols):
-    n = lax.axis_size("dp")
-    ticks = [TICKS, line_ticks(n) - TICKS]
     outs = [sds((8 * TALL, WIDE), F32), sds((WIDE, 8 * TALL), F32), sds((WIDE, 8 * TALL), F32)]
     outs += [sds((q_cols, WIDE), F32), sds((WIDE, q_cols), F32), sds((k_cols, WIDE), F32), sds((k_cols, WIDE), F32)]
-    moved = 6 * ALL_CHUNKS // 2 * TALL * WIDE
     return pl.pallas_call(
-        functools.partial(unpack_kernel, ticks, q_cols, k_cols),
+        functools.partial(unpack_kernel, q_cols, k_cols),
         out_shape=outs,
-        in_specs=[ANY] * len(tots),
+        in_specs=[ANY] * 3,
         out_specs=[ANY] * len(outs),
         scratch_shapes=[
-            pltpu.VMEM((4, TALL, WIDE), BF),
-            pltpu.VMEM((4, TALL, WIDE), F32),
-            pltpu.VMEM((2, 4, k_cols, TALL), F32),
-            DMA((4, 2)),
-            DMA((4, WIDE // TALL)),
+            pltpu.VMEM((tots[0].shape[0] + tots[1].shape[0], CHUNK, WIDE), BF),
+            pltpu.VMEM(tots[2].shape, BF),
+            pltpu.VMEM((SLOTS, TALL, 8 * TALL), F32),
+            pltpu.VMEM((SLOTS, 2, k_cols, TALL), F32),
+            DMA((3,)),
+            DMA((SLOTS, 3)),
         ],
-        compiler_params=pltpu.CompilerParams(vmem_limit_bytes=16 << 20),
-        cost_estimate=pl.CostEstimate(flops=0, bytes_accessed=moved, transcendentals=0),
+        compiler_params=pltpu.CompilerParams(vmem_limit_bytes=62 << 20),
+        cost_estimate=pl.CostEstimate(flops=0, bytes_accessed=3 * ALL_CHUNKS * TALL * WIDE, transcendentals=0),
     )(*tots)
 
 
@@ -1354,11 +1398,11 @@
     d_hidden, gains_f, part_m, part_o, d_attn, tot1, acc, tot = contract(
         d_gate, d_up, wg, wu, hidden, rstd2, gain_f, cotangent, wo, attn, part_d, all_f
     )
-    output, grad_x, gains, tot2 = backward(
+    output, grad_x, gains, tot2, tot3 = backward(
         qkv, kvt, lse, d_attn, cos, sin, middle, wd, hidden, wqkv, layer_input, rstd1, d_hidden,
         gain_a, gains_f, part_m, part_o, acc, tot, normed, q_cols, k_cols,
     )
-    down, gate, up, out, g_q, g_k, g_v = unpack([tot1, tot2], q_cols, k_cols)
+    down, gate, up, out, g_q, g_k, g_v = unpack([tot1, tot2, tot3], q_cols, k_cols)
     return output, grad_x, gains[0], gains[1], g_q, g_k.T, g_v.T, out, gate, up, down
 
 

time: 359 us -> 329 us (0.916)
  Pallas kernels: 349 us -> 324 us
    pallas_call x3, Pallas kernels: 337 us -> 313 us  [call(): pl.pallas_call(staged(kernel, len(args), fetch, spill, early), out_shape=...]
where the time goes in v5:
time: 329 us
  Pallas kernels  324 us (98%)
  local copies, waits for them, and re-layouts  4.5 us (1%)
    pallas_call x3, Pallas kernels, call(): pl.pallas_call(staged(kernel, len(args), fetch, spill, early), out_shape=...  313 us
    pallas_call x1, Pallas kernels, unpack(): pl.pallas_call(functools.partial(unpack_kernel, q_cols, k_cols), out_shap...  10.8 us

profile of v5, /device:TPU:0, one launch (start us, length us, event | category | flops | bytes accessed | tf_op | source)
XLA Modules:
  0.0 328.7 jit_solution(5470895326731502184)
XLA Ops:
  0.6 123.7 %shard_map.203 = (bf16[2,4,512,768]{3,2,1,0:T(8,128)(2,1)}, bf16[2,4,512,768]{3,2,1,0:T(8,128)(2,1)}, bf16[4,2048,128]{2,1,0:T(8,128)(2,1)}, bf16[2,128,2048]{2,...) custom-call(bf16[512,768]{1,0:T(8,128)(2,1)} %refs_10_.3, ...), custom_call_target="tpu_custom_call" | custom-call | flops 89999998976 | bytes 43014144 | tf_op jit(solution)/shard_map/pallas_call | solution.py:517
  124.4 85.8 %shard_map.204 = (f32[512,768]{1,0:T(8,128)}, f32[1,768]{1,0:T(1,128)}, bf16[32,64,768]{2,1,0:T(8,128)(2,1)}, bf16[6,64,768]{2,1,0:T(8,128)(2,1)}, bf16[4,512,25...) custom-call(bf16[4,512,512]{2,1,0:T(8,128)(2,1)} %get-tuple-element.5, ...), custom_call_target="tpu_custom_call" | custom-call | flops 49999998976 | bytes 30152704 | tf_op jit(solution)/shard_map/pallas_call | solution.py:517
  210.2 103.2 %shard_map.205 = (f32[512,768]{1,0:T(8,128)}, f32[512,768]{1,0:T(8,128)}, f32[2,768]{1,0:T(2,128)}, bf16[28,64,768]{2,1,0:T(8,128)(2,1)}, bf16[16,64,768]{2,1,0:T(8,128)(2,1)}) custom-call(bf16[4,2048,128]{2,1,0:T(8,128)(2,1)} %get-tuple-element.51.refs_0_, bf16[2,128,2048]{2,1,0:T(8,128)(2,1)} %get-tuple-element.52.refs_1_, ...), custom_call_target="tpu_custom_call" | custom-call | flops 49999998976 | bytes 32993280 | tf_op jit(solution)/shard_map/pallas_call | solution.py:517
  313.4 1.4 slice_reduce_fusion
  314.8 0.0 copy-start.1
  314.8 10.8 %shard_map.206 = (f32[1024,768]{1,0:T(8,128)}, f32[768,1024]{1,0:T(8,128)}, f32[768,1024]{1,0:T(8,128)}, f32[384,768]{1,0:T(8,128)}, f32[768,384]{1,0:T(8,128)}, /*index=5*/f32[192,768]{1,0:T(8,128)}, f32[192,768]{1,0:T(8,128)}) custom-call(bf16[34,64,768]{2,1,0:T(8,128)(2,1)} %get-tuple-element.81.tot1, bf16[28,64,768]{2,1,0:T(8,128)(2,1)} %get-tuple-element.82.tot2, ...), custom_call_target="tpu_custom_call" | custom-call | bytes 19464192 | tf_op jit(solution)/shard_map/pallas_call | solution.py:1367
  325.6 0.0 copy-done.1
  325.6 0.0 copy-start
  325.6 1.1 copy.25
  326.7 0.8 copy-done
  327.6 1.1 copy.26
Async XLA Ops:
  314.8 10.8 %copy-start.1 = (f32[512,768]{1,0:T(8,128)S(1)}, f32[512,768]{1,0:T(8,128)}, u32[]{:S(2)}) copy-start(f32[512,768]{1,0:T(8,128)} %get-tuple-element.104) | copy-start | bytes 4718596
  325.6 2.0 copy-start
